TPU v7x, 32 devices: a whole 2x2x4 slice. The times are simulated.
32 devices in a mesh: dp: 4 (over y, core), label: 8 (over z, x).
Axes of the slice: x: 2, y: 2, z: 4, core: 2. Of those that a mesh axis runs over, the one named last changes fastest.
Arguments:
- queries: bfloat16 [4096, 512], P(('dp', 'label')), may hold values from -200 to 200
- shortlist: int32 [4096, 4], P(('dp', 'label')), may hold values from 0 to 511, all different within a row; in each aligned block of 128 rows (0 to 127, 128 to 255, ...) at most 2 rows name the same one
- slab_slot: int32 [512], replicated, may hold values from 0 to 511, each once
- top_target: int32 [4096], P(('dp', 'label')), may hold values from 0 to 2047
- leaf_target: int32 [4096], P(('dp', 'label')), may hold values from 0 to 127
- top_weight: bfloat16 [2048, 512], P('label'), may hold values from -0.25 to 0.25
- mid_weight: bfloat16 [512, 512], P(('dp', 'label')), may hold values from -0.25 to 0.25
- leaf_weight: bfloat16 [512, 128, 512], P(('dp', 'label')), may hold values from -0.25 to 0.25
Outputs:
- query_grad: float32 [4096, 512], P(('dp', 'label'))
- top_grad: float32 [2048, 512], P('label')
- mid_grad: float32 [512, 512], P(('dp', 'label'))
- leaf_grad: float32 [512, 128, 512], P(('dp', 'label'))
- losses: float32 [3, 4096], P(None, ('dp', 'label'))
Inputs may be any that keep to these rules, and one draw needn't show every extreme that they name: `shortlist`: each query names 4 different mid clusters; among the 128 queries of one device no cluster is named more than 2 times. Each cluster's mid and leaf rows are row slab_slot[c] of mid_weight and leaf_weight; every row is used once.
All inputs are finite; a program needn't handle non-finite values.
Results may differ from a plain program's by a relative error of at most 0.003.
Values may be sent and summed in bfloat16 or wider, within the bound.
No kernel may reach another device: no remote copies, remote signals or barrier semaphores. Data moves between devices by JAX's collectives and lax.ppermute only.
A program may use at most 64 MiB of HBM per device.

v0:
```python
import jax
import jax.numpy as jnp
from jax import lax
from jax.sharding import PartitionSpec as P

D = 512
BLOCKS = 512
CAPB = 2


def shortened(array):

    def short(part):
        return part.astype(jnp.bfloat16) if part.dtype == jnp.float32 else part

    return jax.tree.map(short, array)


def route_narrow(payload):
    return jax.tree.map(
        lambda part, own: part.astype(own.dtype),
        lax.all_to_all(
            lax.all_to_all(shortened(payload), "label", split_axis=1, concat_axis=1, tiled=True),
            "dp",
            split_axis=0,
            concat_axis=0,
            tiled=True,
        ),
        payload,
    )


def route_wide(payload):
    return lax.all_to_all(
        lax.all_to_all(payload, "label", split_axis=1, concat_axis=1, tiled=True),
        "dp",
        split_axis=0,
        concat_axis=0,
        tiled=True,
    )


def per_device(
    queries, shortlist, slab_slot, top_target, leaf_target, top_weight, mid_weight, leaf_weight
):
    dp_size = lax.axis_size("dp")
    label_size = lax.axis_size("label")
    rows_here = queries.shape[0]
    short_len = shortlist.shape[1]
    block_dev = leaf_weight.shape[0]
    all_rows = lax.all_gather(top_weight, "label", axis=0, tiled=True)
    scores = jnp.dot(queries, all_rows.T, preferred_element_type=jnp.float32)
    totals = jax.nn.logsumexp(scores, axis=1)
    target_hit = top_target[:, None] == jnp.arange(scores.shape[1], dtype=jnp.int32)[None, :]
    top_loss = totals - jnp.sum(jnp.where(target_hit, scores, 0.0), axis=1)
    dscore = (jnp.exp(scores - totals[:, None]) - target_hit.astype(jnp.float32)).astype(
        jnp.bfloat16
    )
    top_back = jnp.dot(dscore, all_rows, preferred_element_type=jnp.float32)
    columns_held = lax.all_to_all(dscore, "label", split_axis=1, concat_axis=0, tiled=True)
    top_part = lax.dot_general(
        columns_held,
        lax.all_gather(queries, "label", axis=0, tiled=True),
        (((0,), (0,)), ((), ())),
        preferred_element_type=jnp.float32,
    )
    top_grad = lax.psum(top_part, "dp")
    position = slab_slot[shortlist].reshape(-1)
    sort_order = jnp.argsort(position, stable=True)
    ranked = position[sort_order]
    run_start = jnp.searchsorted(ranked, ranked, side="left")
    slot_rank = jnp.arange(ranked.shape[0], dtype=jnp.int32) - run_start
    slot_of = jnp.zeros_like(position).at[sort_order].set(ranked * CAPB + slot_rank)
    first_slot = (jnp.arange(short_len, dtype=jnp.int32) == 0)[None, :]
    pair_codes = jnp.where(first_slot, leaf_target[:, None], -1).reshape(-1).astype(jnp.float32)
    layout = (dp_size, label_size, block_dev, CAPB)
    send_rows = (
        jnp.zeros((BLOCKS * CAPB, D), jnp.bfloat16)
        .at[slot_of]
        .set(jnp.repeat(queries, short_len, axis=0))
    )
    send_code = (
        jnp.full((BLOCKS * CAPB,), -2.0, jnp.float32)
        .at[slot_of]
        .set(pair_codes)
        .astype(jnp.bfloat16)
    )
    got_rows, got_code = route_narrow((send_rows.reshape(layout + (D,)), send_code.reshape(layout)))
    scores_held = jnp.einsum(
        "abkcd,kld->abkcl", got_rows, leaf_weight, preferred_element_type=jnp.float32
    )
    mid_held = jnp.einsum(
        "abkcd,kd->abkc", got_rows, mid_weight, preferred_element_type=jnp.float32
    )
    block_lse = jax.nn.logsumexp(scores_held, axis=-1)
    code_float = got_code.astype(jnp.float32)
    labels = jnp.arange(scores_held.shape[-1], dtype=jnp.float32)
    target_hit = (code_float[..., None] == labels).astype(jnp.float32)
    target_held = jnp.sum(scores_held * target_hit, axis=-1)
    back_mid, back_lse, back_target = route_wide((mid_held, block_lse, target_held))
    pair_mid = back_mid.reshape(-1)[slot_of].reshape(rows_here, short_len)
    pair_lse = back_lse.reshape(-1)[slot_of].reshape(rows_here, short_len)
    pair_target = back_target.reshape(-1)[slot_of].reshape(rows_here, short_len)
    mid_totals = jax.nn.logsumexp(pair_mid, axis=1)
    mid_loss = mid_totals - pair_mid[:, 0]
    mid_delta = (jnp.exp(pair_mid - mid_totals[:, None]) - first_slot.astype(jnp.float32)).astype(
        jnp.bfloat16
    )
    leaf_lse = jax.nn.logsumexp(pair_lse, axis=1)
    leaf_loss = leaf_lse - pair_target[:, 0]
    send_delta = (
        jnp.zeros((BLOCKS * CAPB,), jnp.float32)
        .at[slot_of]
        .set(mid_delta.reshape(-1).astype(jnp.float32))
    )
    send_lse = (
        jnp.zeros((BLOCKS * CAPB,), jnp.float32).at[slot_of].set(jnp.repeat(leaf_lse, short_len))
    )
    got_delta, got_lse = route_wide((send_delta.reshape(layout), send_lse.reshape(layout)))
    live_slot = code_float > -1.5
    leaf_delta = jnp.where(
        live_slot[..., None], jnp.exp(scores_held - got_lse[..., None]) - target_hit, 0.0
    ).astype(jnp.bfloat16)
    mid_slots = got_delta.astype(jnp.bfloat16)
    leaf_grad = jnp.einsum(
        "abkcl,abkcd->kld", leaf_delta, got_rows, preferred_element_type=jnp.float32
    )
    mid_grad = jnp.einsum("abkc,abkcd->kd", mid_slots, got_rows, preferred_element_type=jnp.float32)
    pair_back = jnp.einsum(
        "abkcl,kld->abkcd", leaf_delta, leaf_weight, preferred_element_type=jnp.float32
    )
    pair_back = (
        pair_back
        + mid_slots.astype(jnp.float32)[..., None] * mid_weight.astype(jnp.float32)[:, None, :]
    ).astype(jnp.bfloat16)
    returned = route_narrow(pair_back)
    pair_sum = (
        returned.reshape(BLOCKS * CAPB, D)[slot_of]
        .astype(jnp.float32)
        .reshape(rows_here, short_len, D)
        .sum(axis=1)
    )
    query_grad = top_back + pair_sum
    losses = jnp.stack([top_loss, mid_loss, leaf_loss])
    return (query_grad, top_grad, mid_grad, leaf_grad, losses)


def solution(mesh):
    in_specs = (
        P(("dp", "label"), None),
        P(("dp", "label"), None),
        P(),
        P(("dp", "label")),
        P(("dp", "label")),
        P("label", None),
        P(("dp", "label"), None),
        P(("dp", "label"), None, None),
    )
    out_specs = (
        P(("dp", "label"), None),
        P("label", None),
        P(("dp", "label"), None),
        P(("dp", "label"), None, None),
        P(None, ("dp", "label")),
    )
    return jax.shard_map(
        per_device, mesh=mesh, in_specs=in_specs, out_specs=out_specs, check_vma=False
    )
```

profile of v0, /device:TPU:0, one launch (start us, length us, event | category | flops | bytes accessed | tf_op | source)
XLA Modules:
  0.0 342.4 jit_solution(8619157326044680296)
XLA Ops:
  8.3 3.5 %gather_fusion.1 = s32[512]{0:T(512)S(1)} fusion(s32[512]{0:T(512)S(1)} %copy-done.1, s32[1024]{0:T(1024)S(1)} %pad_clamp_fusion.3), kind=kCustom, calls=%fused_computation.1 | custom fusion | bytes 6144 | tf_op jit(solution)/shard_map/gather | solution.py:68
  11.8 3.8 %sort.17 = (s32[512]{0:T(512)}, s32[512]{0:T(512)S(1)}) sort(s32[512]{0:T(512)S(1)} %gather_fusion.1, s32[512]{0:T(512)S(1)} %iota.24), dimensions={0}, to_apply=%region_2.3 | sort | flops 4608 | bytes 8192 | tf_op jit(solution)/shard_map/jit(argsort)/sort | solution.py:69
  15.6 3.5 %gather_fusion.2 = s32[512]{0:T(512)S(1)} fusion(s32[512]{0:T(512)S(1)} %gather_fusion.1, s32[1024]{0:T(1024)S(1)} %pad_clamp_fusion.2), kind=kCustom, calls=%fused_computation.2 | custom fusion | bytes 6144 | tf_op jit(solution)/shard_map/gather | solution.py:70
  19.1 35.9 %while.25 = (s32[]{:T(128)}, u32[512]{0:T(512)S(1)}, u32[512]{0:T(512)S(1)}, s32[512]{0:T(512)S(1)}, s32[]{:T(128)}, /*index=5*/s32[]{:T(128)}, s32[]{}) while((s32[]{:T(128)}, u32[512]{0:T(512)S(1)}, u32[512]{0:T(512)S(1)}, s32[512]{0:T(512)S(1)}, s32[]{:T(128)}, /*index=5*/s32[]{:T(128)}, s32[]{}) %tuple.45), condition=%wide.region_4.5_spmd.clone, body=%wide.region_3.4_spmd.clone.sunk | while | flops 10244 | bytes 40045 | solution.py:71
  19.1 3.5 %gather_fusion = s32[512]{0:T(512)S(1)} fusion(s32[512]{0:T(512)S(1)} %get-tuple-element.156, u32[1024]{0:T(1024)S(1)} %pad_clamp_fusion.5), kind=kCustom, calls=%fused_computation.clone.clone.1 | custom fusion | bytes 6144 | tf_op jit(solution)/shard_map/jit(searchsorted)/jit(_searchsorted_scan_impl)/vmap(jit(_searchsorted_scan_impl))/while/body/eval_jaxpr/gather | solution.py:71
  22.7 3.5 %gather_fusion = s32[512]{0:T(512)S(1)} fusion(s32[512]{0:T(512)S(1)} %get-tuple-element.156, u32[1024]{0:T(1024)S(1)} %pad_clamp_fusion.5), kind=kCustom, calls=%fused_computation.clone.clone.1 | custom fusion | bytes 6144 | tf_op jit(solution)/shard_map/jit(searchsorted)/jit(_searchsorted_scan_impl)/vmap(jit(_searchsorted_scan_impl))/while/body/eval_jaxpr/gather | solution.py:71
  26.3 3.5 %gather_fusion = s32[512]{0:T(512)S(1)} fusion(s32[512]{0:T(512)S(1)} %get-tuple-element.156, u32[1024]{0:T(1024)S(1)} %pad_clamp_fusion.5), kind=kCustom, calls=%fused_computation.clone.clone.1 | custom fusion | bytes 6144 | tf_op jit(solution)/shard_map/jit(searchsorted)/jit(_searchsorted_scan_impl)/vmap(jit(_searchsorted_scan_impl))/while/body/eval_jaxpr/gather | solution.py:71
  29.9 3.5 %gather_fusion = s32[512]{0:T(512)S(1)} fusion(s32[512]{0:T(512)S(1)} %get-tuple-element.156, u32[1024]{0:T(1024)S(1)} %pad_clamp_fusion.5), kind=kCustom, calls=%fused_computation.clone.clone.1 | custom fusion | bytes 6144 | tf_op jit(solution)/shard_map/jit(searchsorted)/jit(_searchsorted_scan_impl)/vmap(jit(_searchsorted_scan_impl))/while/body/eval_jaxpr/gather | solution.py:71
  33.5 3.5 %gather_fusion = s32[512]{0:T(512)S(1)} fusion(s32[512]{0:T(512)S(1)} %get-tuple-element.156, u32[1024]{0:T(1024)S(1)} %pad_clamp_fusion.5), kind=kCustom, calls=%fused_computation.clone.clone.1 | custom fusion | bytes 6144 | tf_op jit(solution)/shard_map/jit(searchsorted)/jit(_searchsorted_scan_impl)/vmap(jit(_searchsorted_scan_impl))/while/body/eval_jaxpr/gather | solution.py:71
  37.1 3.5 %gather_fusion = s32[512]{0:T(512)S(1)} fusion(s32[512]{0:T(512)S(1)} %get-tuple-element.156, u32[1024]{0:T(1024)S(1)} %pad_clamp_fusion.5), kind=kCustom, calls=%fused_computation.clone.clone.1 | custom fusion | bytes 6144 | tf_op jit(solution)/shard_map/jit(searchsorted)/jit(_searchsorted_scan_impl)/vmap(jit(_searchsorted_scan_impl))/while/body/eval_jaxpr/gather | solution.py:71
  40.7 3.5 %gather_fusion = s32[512]{0:T(512)S(1)} fusion(s32[512]{0:T(512)S(1)} %get-tuple-element.156, u32[1024]{0:T(1024)S(1)} %pad_clamp_fusion.5), kind=kCustom, calls=%fused_computation.clone.clone.1 | custom fusion | bytes 6144 | tf_op jit(solution)/shard_map/jit(searchsorted)/jit(_searchsorted_scan_impl)/vmap(jit(_searchsorted_scan_impl))/while/body/eval_jaxpr/gather | solution.py:71
  44.3 3.5 %gather_fusion = s32[512]{0:T(512)S(1)} fusion(s32[512]{0:T(512)S(1)} %get-tuple-element.156, u32[1024]{0:T(1024)S(1)} %pad_clamp_fusion.5), kind=kCustom, calls=%fused_computation.clone.clone.1 | custom fusion | bytes 6144 | tf_op jit(solution)/shard_map/jit(searchsorted)/jit(_searchsorted_scan_impl)/vmap(jit(_searchsorted_scan_impl))/while/body/eval_jaxpr/gather | solution.py:71
  47.9 3.5 %gather_fusion = s32[512]{0:T(512)S(1)} fusion(s32[512]{0:T(512)S(1)} %get-tuple-element.156, u32[1024]{0:T(1024)S(1)} %pad_clamp_fusion.5), kind=kCustom, calls=%fused_computation.clone.clone.1 | custom fusion | bytes 6144 | tf_op jit(solution)/shard_map/jit(searchsorted)/jit(_searchsorted_scan_impl)/vmap(jit(_searchsorted_scan_impl))/while/body/eval_jaxpr/gather | solution.py:71
  51.4 3.5 %gather_fusion = s32[512]{0:T(512)S(1)} fusion(s32[512]{0:T(512)S(1)} %get-tuple-element.156, u32[1024]{0:T(1024)S(1)} %pad_clamp_fusion.5), kind=kCustom, calls=%fused_computation.clone.clone.1 | custom fusion | bytes 6144 | tf_op jit(solution)/shard_map/jit(searchsorted)/jit(_searchsorted_scan_impl)/vmap(jit(_searchsorted_scan_impl))/while/body/eval_jaxpr/gather | solution.py:71
  61.3 7.3 %all-to-all-start = ((bf16[4,8,16,2]{2,0,3,1:T(4,128)(2,1)}), bf16[4,8,16,2]{2,0,3,1:T(4,128)(2,1)S(1)}, u32[]{:S(2)}, u32[]{:S(2)}) async-start(bf16[4,8,16,2]{2,0,3,1:T(4,128)(2,1)} %copy.61), calls=%async_computation | async-start | bytes 32768 | tf_op jit(solution)/shard_map/all_to_all | solution.py:23
  77.1 6.0 %all-to-all-start.2 = ((bf16[4,8,16,2,512]{4,3,0,2,1:T(2,128)(2,1)}), bf16[4,8,16,2,512]{4,3,0,2,1:T(2,128)(2,1)S(1)}, u32[]{:S(2)}, u32[]{:S(2)}) async-start(bf16[4,8,16,2,512]{4,3,0,2,1:T(2,128)(2,1)} %copy.64), calls=%async_computation.2 | async-start | bytes 2097152 | tf_op jit(solution)/shard_map/all_to_all | solution.py:23
  83.8 24.7 %all-to-all-done.2 = bf16[4,8,16,2,512]{4,3,0,2,1:T(2,128)(2,1)S(1)} async-done(((bf16[4,8,16,2,512]{4,3,0,2,1:T(2,128)(2,1)}), bf16[4,8,16,2,512]{4,3,0,2,1:T(2,128)(2,1)S(1)}, u32[]{:S(2)}, u32[]{:S(2)}) %all-to-all-start.2) | async-done | bytes 1048608 | tf_op jit(solution)/shard_map/all_to_all | solution.py:23
  115.4 3.5 %all-to-all-start.3 = ((bf16[4,8,16,2,512]{4,1,3,2,0:T(8,128)(2,1)}), bf16[4,8,16,2,512]{4,1,3,2,0:T(8,128)(2,1)S(1)}, u32[]{:S(2)}, u32[]{:S(2)}) async-start(bf16[4,8,16,2,512]{4,1,3,2,0:T(8,128)(2,1)} %copy.65), calls=%async_computation.3 | async-start | bytes 2097152 | tf_op jit(solution)/shard_map/all_to_all | solution.py:22
  119.9 13.4 %all-to-all-done.3 = bf16[4,8,16,2,512]{4,1,3,2,0:T(8,128)(2,1)S(1)} async-done(((bf16[4,8,16,2,512]{4,1,3,2,0:T(8,128)(2,1)}), bf16[4,8,16,2,512]{4,1,3,2,0:T(8,128)(2,1)S(1)}, u32[]{:S(2)}, u32[]{:S(2)}) %all-to-all-start.3) | async-done | bytes 1048608 | tf_op jit(solution)/shard_map/all_to_all | solution.py:22
  136.6 3.5 %all-to-all-start.8 = ((f32[8,1,128]{2,1,0:T(1,128)}), f32[8,1,128]{2,1,0:T(1,128)S(1)}, u32[]{:S(2)}, u32[]{:S(2)}) async-start(f32[8,1,128]{2,1,0:T(1,128)} %reshape.371), calls=%async_computation.8 | async-start | bytes 8192 | tf_op jit(solution)/shard_map/all_to_all | solution.py:35
  146.4 4.1 %all-to-all-start.4 = ((f32[8,1,128]{2,1,0:T(1,128)}), f32[8,1,128]{2,1,0:T(1,128)S(1)}, u32[]{:S(2)}, u32[]{:S(2)}) async-start(f32[8,1,128]{2,1,0:T(1,128)} %reshape.363), calls=%async_computation.4 | async-start | bytes 8192 | tf_op jit(solution)/shard_map/all_to_all | solution.py:35
  152.4 4.7 %all-to-all-done.4 = f32[8,1,128]{2,1,0:T(1,128)S(1)} async-done(((f32[8,1,128]{2,1,0:T(1,128)}), f32[8,1,128]{2,1,0:T(1,128)S(1)}, u32[]{:S(2)}, u32[]{:S(2)}) %all-to-all-start.4) | async-done | bytes 4128 | tf_op jit(solution)/shard_map/all_to_all | solution.py:35
  182.8 5.9 %all-to-all-start.10 = ((bf16[4,8,16,2]{2,0,3,1:T(4,128)(2,1)}), bf16[4,8,16,2]{2,0,3,1:T(4,128)(2,1)S(1)}, u32[]{:S(2)}, u32[]{:S(2)}) async-start(bf16[4,8,16,2]{2,0,3,1:T(4,128)(2,1)} %copy.80), calls=%async_computation.10 | async-start | bytes 32768 | tf_op jit(solution)/shard_map/all_to_all | solution.py:35
  199.3 5.7 %all-to-all-done.6 = f32[8,1,128]{2,1,0:T(1,128)S(1)} async-done(((f32[8,1,128]{2,1,0:T(1,128)}), f32[8,1,128]{2,1,0:T(1,128)S(1)}, u32[]{:S(2)}, u32[]{:S(2)}) %all-to-all-start.6) | async-done | bytes 4128 | tf_op jit(solution)/shard_map/all_to_all | solution.py:35
  226.7 4.4 %all-to-all-start.12 = ((bf16[4,8,16,2,512]{4,3,0,2,1:T(2,128)(2,1)}), bf16[4,8,16,2,512]{4,3,0,2,1:T(2,128)(2,1)}, u32[]{:S(2)}, u32[]{:S(2)}) async-start(bf16[4,8,16,2,512]{4,3,0,2,1:T(2,128)(2,1)} %copy.83), calls=%async_computation.12 | async-start | bytes 2097152 | tf_op jit(solution)/shard_map/all_to_all | solution.py:23
  241.8 20.0 %all-to-all-done.12 = bf16[4,8,16,2,512]{4,3,0,2,1:T(2,128)(2,1)} async-done(((bf16[4,8,16,2,512]{4,3,0,2,1:T(2,128)(2,1)}), bf16[4,8,16,2,512]{4,3,0,2,1:T(2,128)(2,1)}, u32[]{:S(2)}, u32[]{:S(2)}) %all-to-all-start.12) | async-done | bytes 1048608 | tf_op jit(solution)/shard_map/all_to_all | solution.py:23
  261.9 4.4 %all-to-all-start.14 = ((bf16[128,8,256]{2,0,1:T(8,128)(2,1)}), bf16[128,8,256]{2,0,1:T(8,128)(2,1)}, u32[]{:S(2)}, u32[]{:S(2)}) async-start(bf16[128,8,256]{2,0,1:T(8,128)(2,1)} %bitcast.113), calls=%async_computation.14 | async-start | bytes 1048576 | tf_op jit(solution)/shard_map/all_to_all | solution.py:60
  271.1 17.9 %all-to-all-done.14 = bf16[128,8,256]{2,0,1:T(8,128)(2,1)} async-done(((bf16[128,8,256]{2,0,1:T(8,128)(2,1)}), bf16[128,8,256]{2,0,1:T(8,128)(2,1)}, u32[]{:S(2)}, u32[]{:S(2)}) %all-to-all-start.14) | async-done | bytes 524320 | tf_op jit(solution)/shard_map/all_to_all | solution.py:60
  289.0 4.3 %all-to-all-start.13 = ((bf16[4,8,16,2,512]{4,1,3,2,0:T(8,128)(2,1)}), bf16[4,8,16,2,512]{4,1,3,2,0:T(8,128)(2,1)}, u32[]{:S(2)}, u32[]{:S(2)}) async-start(bf16[4,8,16,2,512]{4,1,3,2,0:T(8,128)(2,1)} %copy.84), calls=%async_computation.13 | async-start | bytes 2097152 | tf_op jit(solution)/shard_map/all_to_all | solution.py:22
  293.3 4.3 %convolution_bitcast_fusion = f32[16,128,512]{2,1,0:T(8,128)} fusion(bf16[4,8,16,2,512]{4,1,3,2,0:T(8,128)(2,1)S(1)} %all-to-all-done.3, f32[4,8,16,2,128]{4,1,3,0,2:T(8,128)} %get-tuple-element.105, f32[4,8,16,2]{1,3,0,2:T(2,128)S(1)} %copy-done.9, f32[4,8,16,2]{1,3,0,2:T(2,128)S(1)} %copy-done.13, pred[4,8,16,2]{1,3,0,2:T(4,128)(4,1)S(1)} %copy-done.15), kind=kOutput, calls=%fused_computation.16 | convolution fusion | flops 135004160 | bytes 5776384 | tf_op jit(solution)/shard_map/abkcl,abkcd->kld/dot_general | solution.py:125
  300.9 6.8 %all-to-all-done.13 = bf16[4,8,16,2,512]{4,1,3,2,0:T(8,128)(2,1)} async-done(((bf16[4,8,16,2,512]{4,1,3,2,0:T(8,128)(2,1)}), bf16[4,8,16,2,512]{4,1,3,2,0:T(8,128)(2,1)}, u32[]{:S(2)}, u32[]{:S(2)}) %all-to-all-start.13) | async-done | bytes 1048608 | tf_op jit(solution)/shard_map/all_to_all | solution.py:22
  322.2 11.8 %all-reduce.2.cloned.1.call-done = f32[256,512]{1,0:T(8,128)} async-done(((f32[256,512]{1,0:T(8,128)}), f32[256,512]{1,0:T(8,128)}) %all-reduce.2.cloned.1.call-update) | async-done | bytes 524304 | tf_op jit(solution)/shard_map/psum | solution.py:67
  (271 shorter events, 128.8 us)
Async XLA Ops:
  7.2 132.9 %copy-start = (bf16[16,128,512]{2,1,0:T(8,128)(2,1)S(1)}, bf16[16,128,512]{2,1,0:T(8,128)(2,1)}, u32[]{:S(2)}) copy-start(bf16[16,128,512]{2,1,0:T(8,128)(2,1)} %param.17) | copy-start | bytes 6291460
  19.1 38.4 %copy-start.27 = (s32[128]{0:T(128)S(1)}, s32[128]{0:T(128)}, u32[]{:S(2)}) copy-start(s32[128]{0:T(128)} %param.14) | copy-start | bytes 1540
  19.1 49.5 %copy-start.4 = (bf16[128,512]{1,0:T(8,128)(2,1)S(1)}, bf16[128,512]{1,0:T(8,128)(2,1)}, u32[]{:S(2)}) copy-start(bf16[128,512]{1,0:T(8,128)(2,1)} %param.10) | copy-start | bytes 393220
  61.3 15.8 %all-to-all-start = ((bf16[4,8,16,2]{2,0,3,1:T(4,128)(2,1)}), bf16[4,8,16,2]{2,0,3,1:T(4,128)(2,1)S(1)}, u32[]{:S(2)}, u32[]{:S(2)}) async-start(bf16[4,8,16,2]{2,0,3,1:T(4,128)(2,1)} %copy.61), calls=%async_computation | async-start | bytes 32768 | tf_op jit(solution)/shard_map/all_to_all | solution.py:23
  77.1 31.4 %all-to-all-start.2 = ((bf16[4,8,16,2,512]{4,3,0,2,1:T(2,128)(2,1)}), bf16[4,8,16,2,512]{4,3,0,2,1:T(2,128)(2,1)S(1)}, u32[]{:S(2)}, u32[]{:S(2)}) async-start(bf16[4,8,16,2,512]{4,3,0,2,1:T(2,128)(2,1)} %copy.64), calls=%async_computation.2 | async-start | bytes 2097152 | tf_op jit(solution)/shard_map/all_to_all | solution.py:23
  108.5 6.9 %all-to-all-start.1 = ((bf16[4,2,128]{2,1,0:T(2,128)(2,1)}), bf16[4,2,128]{2,1,0:T(2,128)(2,1)S(1)}, u32[]{:S(2)}, u32[]{:S(2)}) async-start(bf16[4,2,128]{2,1,0:T(2,128)(2,1)} %reshape.361), calls=%async_computation.1 | async-start | bytes 4096 | tf_op jit(solution)/shard_map/all_to_all | solution.py:22
  115.4 17.9 %all-to-all-start.3 = ((bf16[4,8,16,2,512]{4,1,3,2,0:T(8,128)(2,1)}), bf16[4,8,16,2,512]{4,1,3,2,0:T(8,128)(2,1)S(1)}, u32[]{:S(2)}, u32[]{:S(2)}) async-start(bf16[4,8,16,2,512]{4,1,3,2,0:T(8,128)(2,1)} %copy.65), calls=%async_computation.3 | async-start | bytes 2097152 | tf_op jit(solution)/shard_map/all_to_all | solution.py:22
  119.0 117.8 %all-gather.3.cloned.1.call-start = ((), (), s32[]{:S(2)}) async-start(), calls=%async_computation.17 | async-start | bytes 2359296 | tf_op jit(solution)/shard_map/all_gather | solution.py:51
  119.9 103.2 %copy-start.8 = (f32[4,8,16,2]{1,3,0,2:T(2,128)}, f32[4,8,16,2]{1,3,0,2:T(2,128)S(1)}, u32[]{:S(2)}) copy-start(f32[4,8,16,2]{1,3,0,2:T(2,128)S(1)} %copy.77) | copy-start | bytes 12292
  136.6 9.8 %all-to-all-start.8 = ((f32[8,1,128]{2,1,0:T(1,128)}), f32[8,1,128]{2,1,0:T(1,128)S(1)}, u32[]{:S(2)}, u32[]{:S(2)}) async-start(f32[8,1,128]{2,1,0:T(1,128)} %reshape.371), calls=%async_computation.8 | async-start | bytes 8192 | tf_op jit(solution)/shard_map/all_to_all | solution.py:35
  146.4 10.7 %all-to-all-start.4 = ((f32[8,1,128]{2,1,0:T(1,128)}), f32[8,1,128]{2,1,0:T(1,128)S(1)}, u32[]{:S(2)}, u32[]{:S(2)}) async-start(f32[8,1,128]{2,1,0:T(1,128)} %reshape.363), calls=%async_computation.4 | async-start | bytes 8192 | tf_op jit(solution)/shard_map/all_to_all | solution.py:35
  157.0 7.0 %all-to-all-start.9 = ((f32[4,1,256]{2,1,0:T(1,128)}), f32[4,1,256]{2,1,0:T(1,128)S(1)}, u32[]{:S(2)}, u32[]{:S(2)}) async-start(f32[4,1,256]{2,1,0:T(1,128)} %reshape.373), calls=%async_computation.9 | async-start | bytes 8192 | tf_op jit(solution)/shard_map/all_to_all | solution.py:34
  164.0 7.9 %all-to-all-start.5 = ((f32[4,1,256]{2,1,0:T(1,128)}), f32[4,1,256]{2,1,0:T(1,128)S(1)}, u32[]{:S(2)}, u32[]{:S(2)}) async-start(f32[4,1,256]{2,1,0:T(1,128)} %reshape.365), calls=%async_computation.5 | async-start | bytes 8192 | tf_op jit(solution)/shard_map/all_to_all | solution.py:34
  172.0 10.8 %all-to-all-start.15 = ((f32[8,1,128]{2,1,0:T(1,128)}), f32[8,1,128]{2,1,0:T(1,128)S(1)}, u32[]{:S(2)}, u32[]{:S(2)}) async-start(f32[8,1,128]{2,1,0:T(1,128)} %reshape.377), calls=%async_computation.15 | async-start | bytes 8192 | tf_op jit(solution)/shard_map/all_to_all | solution.py:35
  182.8 12.5 %all-to-all-start.10 = ((bf16[4,8,16,2]{2,0,3,1:T(4,128)(2,1)}), bf16[4,8,16,2]{2,0,3,1:T(4,128)(2,1)S(1)}, u32[]{:S(2)}, u32[]{:S(2)}) async-start(bf16[4,8,16,2]{2,0,3,1:T(4,128)(2,1)} %copy.80), calls=%async_computation.10 | async-start | bytes 32768 | tf_op jit(solution)/shard_map/all_to_all | solution.py:35
  195.3 9.7 %all-to-all-start.6 = ((f32[8,1,128]{2,1,0:T(1,128)}), f32[8,1,128]{2,1,0:T(1,128)S(1)}, u32[]{:S(2)}, u32[]{:S(2)}) async-start(f32[8,1,128]{2,1,0:T(1,128)} %reshape.367), calls=%async_computation.6 | async-start | bytes 8192 | tf_op jit(solution)/shard_map/all_to_all | solution.py:35
  205.0 7.0 %all-to-all-start.11 = ((bf16[4,2,128]{2,1,0:T(2,128)(2,1)}), bf16[4,2,128]{2,1,0:T(2,128)(2,1)S(1)}, u32[]{:S(2)}, u32[]{:S(2)}) async-start(bf16[4,2,128]{2,1,0:T(2,128)(2,1)} %reshape.375), calls=%async_computation.11 | async-start | bytes 4096 | tf_op jit(solution)/shard_map/all_to_all | solution.py:34
  211.9 7.0 %all-to-all-start.7 = ((f32[4,1,256]{2,1,0:T(1,128)}), f32[4,1,256]{2,1,0:T(1,128)S(1)}, u32[]{:S(2)}, u32[]{:S(2)}) async-start(f32[4,1,256]{2,1,0:T(1,128)} %reshape.369), calls=%async_computation.7 | async-start | bytes 8192 | tf_op jit(solution)/shard_map/all_to_all | solution.py:34
  219.0 7.7 %all-to-all-start.16 = ((f32[4,1,256]{2,1,0:T(1,128)}), f32[4,1,256]{2,1,0:T(1,128)S(1)}, u32[]{:S(2)}, u32[]{:S(2)}) async-start(f32[4,1,256]{2,1,0:T(1,128)} %reshape.379), calls=%async_computation.16 | async-start | bytes 8192 | tf_op jit(solution)/shard_map/all_to_all | solution.py:34
  226.7 35.2 %all-to-all-start.12 = ((bf16[4,8,16,2,512]{4,3,0,2,1:T(2,128)(2,1)}), bf16[4,8,16,2,512]{4,3,0,2,1:T(2,128)(2,1)}, u32[]{:S(2)}, u32[]{:S(2)}) async-start(bf16[4,8,16,2,512]{4,3,0,2,1:T(2,128)(2,1)} %copy.83), calls=%async_computation.12 | async-start | bytes 2097152 | tf_op jit(solution)/shard_map/all_to_all | solution.py:23
  231.0 67.2 %all-gather.5.cloned.1.call-start = ((), (), s32[]{:S(2)}) async-start(), calls=%async_computation.18 | async-start | bytes 1179648 | tf_op jit(solution)/shard_map/all_gather | solution.py:63
  239.7 26.5 %copy-start.7 = (f32[128,4]{1,0:T(8,128)S(1)}, f32[128,4]{1,0:T(8,128)}, u32[]{:S(2)}) copy-start(f32[128,4]{1,0:T(8,128)} %copy-done.6) | copy-start | bytes 6148
  239.7 26.8 %copy-start.20 = (f32[128]{0:T(128)S(1)}, f32[128]{0:T(128)}, u32[]{:S(2)}) copy-start(f32[128]{0:T(128)} %copy-done.19) | copy-start | bytes 1540
  239.7 26.8 %copy-start.22 = (f32[128]{0:T(128)S(1)}, f32[128]{0:T(128)}, u32[]{:S(2)}) copy-start(f32[128]{0:T(128)} %copy-done.21) | copy-start | bytes 1540
  239.7 26.8 %copy-start.24 = (f32[128]{0:T(128)S(1)}, f32[128]{0:T(128)}, u32[]{:S(2)}) copy-start(f32[128]{0:T(128)} %copy-done.23) | copy-start | bytes 1540
  239.7 26.8 %copy-start.26 = (f32[128]{0:T(128)S(1)}, f32[128]{0:T(128)}, u32[]{:S(2)}) copy-start(f32[128]{0:T(128)} %copy-done.25) | copy-start | bytes 1540
  239.7 26.8 %copy-start.11 = (bf16[4,2,8,16]{3,2,1,0:T(8,128)(2,1)S(1)}, bf16[4,2,8,16]{3,2,1,0:T(8,128)(2,1)}, u32[]{:S(2)}) copy-start(bf16[4,2,8,16]{3,2,1,0:T(8,128)(2,1)} %copy-done.10) | copy-start | bytes 6148
  261.9 27.1 %all-to-all-start.14 = ((bf16[128,8,256]{2,0,1:T(8,128)(2,1)}), bf16[128,8,256]{2,0,1:T(8,128)(2,1)}, u32[]{:S(2)}, u32[]{:S(2)}) async-start(bf16[128,8,256]{2,0,1:T(8,128)(2,1)} %bitcast.113), calls=%async_computation.14 | async-start | bytes 1048576 | tf_op jit(solution)/shard_map/all_to_all | solution.py:60
  267.7 25.6 %copy-start.13 = (f32[4,8,16,2]{1,3,0,2:T(2,128)S(1)}, f32[4,8,16,2]{1,3,0,2:T(2,128)}, u32[]{:S(2)}) copy-start(f32[4,8,16,2]{1,3,0,2:T(2,128)} %copy-done.12) | copy-start | bytes 12292
  267.7 25.6 %copy-start.15 = (pred[4,8,16,2]{1,3,0,2:T(4,128)(4,1)S(1)}, pred[4,8,16,2]{1,3,0,2:T(4,128)(4,1)}, u32[]{:S(2)}) copy-start(pred[4,8,16,2]{1,3,0,2:T(4,128)(4,1)} %copy-done.14) | copy-start | bytes 3076
  289.0 18.8 %all-to-all-start.13 = ((bf16[4,8,16,2,512]{4,1,3,2,0:T(8,128)(2,1)}), bf16[4,8,16,2,512]{4,1,3,2,0:T(8,128)(2,1)}, u32[]{:S(2)}, u32[]{:S(2)}) async-start(bf16[4,8,16,2,512]{4,1,3,2,0:T(8,128)(2,1)} %copy.84), calls=%async_computation.13 | async-start | bytes 2097152 | tf_op jit(solution)/shard_map/all_to_all | solution.py:22
  293.2 40.7 %all-reduce.2.cloned.1.call-start = ((), (), s32[]{:S(2)}) async-start(), calls=%async_computation.19 | async-start | bytes 1048576 | tf_op jit(solution)/shard_map/psum | solution.py:67
  (16 other events, 120.0 us)
Sparse Core Ops, SparseCore 0:
  121.9 48.3 all-gather.2
  234.0 54.6 all-gather.4
  301.0 32.8 all-reduce.1
where the time goes:
time: 344 us; the launch traced here: 342 us
  waiting for transfers between devices  118 us (34%)
  local copies, waits for them, and re-layouts  105 us (31%)
  starting transfers between devices  69.4 us (20%)
  matrix products  18.5 us (5%)
  other arithmetic  16.7 us (5%)
  between operations  14.8 us (4%)
    all_to_all x3, waiting for transfers between devices, route_narrow(): lax.all_to_all(shortened(payload), 'label', split_axis=1, concat_axis=1,...  44.8 us
    gather x10, local copies, waits for them, and re-layouts, per_device(): run_start = jnp.searchsorted(ranked, ranked, side='left')  34.9 us
    all_to_all x3, waiting for transfers between devices, route_narrow(): lax.all_to_all(lax.all_to_all(shortened(payload), 'label', split_axis=1,...  21.8 us
    all_to_all x5, starting transfers between devices, route_wide(): lax.all_to_all(payload, 'label', split_axis=1, concat_axis=1, tiled=True)  20.1 us
    all_to_all x1, waiting for transfers between devices, per_device(): lax.all_to_all(dscore, 'label', split_axis=1, concat_axis=0, tiled=True)  17.9 us
    all_to_all x3, starting transfers between devices, route_narrow(): lax.all_to_all(shortened(payload), 'label', split_axis=1, concat_axis=1,...  17.6 us
    all_to_all x5, starting transfers between devices, route_wide(): lax.all_to_all(lax.all_to_all(payload, 'label', split_axis=1, concat_axis...  16.2 us
    all_to_all x5, waiting for transfers between devices, route_wide(): lax.all_to_all(payload, 'label', split_axis=1, concat_axis=1, tiled=True)  14.9 us
  transfers between devices with their start and end apart: 20, of which 14 were waited for; matrix products, arithmetic and copies ran while one was open for 25% of the time, Pallas kernels for 0%

commit v1 on v0

--- a/solution.py
+++ b/solution.py
@@ -1,6 +1,10 @@
+import functools
+
 import jax
 import jax.numpy as jnp
 from jax import lax
+from jax.experimental import pallas as pl
+from jax.experimental.pallas import tpu as pltpu
 from jax.sharding import PartitionSpec as P
 
 D = 512
@@ -40,7 +44,7 @@
     )
 
 
-def per_device(
+def per_device_any(
     queries, shortlist, slab_slot, top_target, leaf_target, top_weight, mid_weight, leaf_weight
 ):
     dp_size = lax.axis_size("dp")
@@ -145,6 +149,487 @@
     return (query_grad, top_grad, mid_grad, leaf_grad, losses)
 
 
+LANES = 128
+SUB = 8
+BF = jnp.bfloat16
+F32 = jnp.float32
+HIGH = lax.Precision.HIGHEST
+
+
+def params():
+    return pltpu.CompilerParams(vmem_limit_bytes=56 * 1024 * 1024)
+
+
+def iota(shape, dim):
+    return lax.broadcasted_iota(jnp.int32, shape, dim)
+
+
+def iota_f(shape, dim):
+    return iota(shape, dim).astype(F32)
+
+
+def dot_nn(a, b, precision=None):
+    return lax.dot_general(
+        a, b, (((1,), (0,)), ((), ())), precision=precision, preferred_element_type=F32
+    )
+
+
+def dot_nt(a, b, precision=None):
+    return lax.dot_general(
+        a, b, (((1,), (1,)), ((), ())), precision=precision, preferred_element_type=F32
+    )
+
+
+def dot_tn(a, b, precision=None):
+    return lax.dot_general(
+        a, b, (((0,), (0,)), ((), ())), precision=precision, preferred_element_type=F32
+    )
+
+
+def pack_kernel(q_ref, short_ref, slab_ref, leaf_t_ref, pay_ref, info_ref, *, devs, held):
+    rows, width = q_ref.shape
+    short_len = short_ref.shape[1]
+    clusters = slab_ref.shape[1]
+    chunks = width // LANES
+    slots = CAPB * held
+    cluster_f = iota_f((rows, clusters), 1)
+    slab = jnp.broadcast_to(slab_ref[...].astype(F32), (rows, clusters))
+    short = short_ref[...].astype(F32)
+    places, hits = [], []
+    for j in range(short_len):
+        place = jnp.sum(jnp.where(short[:, j : j + 1] == cluster_f, slab, 0.0), axis=1, keepdims=True)
+        places.append(place)
+        hits.append(jnp.where(place == cluster_f, 1.0, 0.0))
+    hit = functools.reduce(lambda a, b: a + b, hits)
+    before = jnp.where(iota((rows, rows), 1) < iota((rows, rows), 0), 1.0, 0.0).astype(BF)
+    count = dot_nn(before, hit.astype(BF))
+    lane = iota((rows, LANES), 1)
+    info = jnp.zeros((rows, LANES), F32)
+    for j in range(short_len):
+        rank = jnp.sum(hits[j] * count, axis=1, keepdims=True)
+        info = jnp.where(lane == j, places[j], info)
+        info = jnp.where(lane == short_len + j, rank, info)
+    info_ref[...] = info
+    queries = q_ref[...]
+    target = jnp.broadcast_to(leaf_t_ref[...].astype(F32) + 1.0, (SUB, rows)).astype(BF)
+    ones = jnp.ones((SUB, rows), BF)
+    table_rows = clusters // LANES
+    table = jnp.zeros((CAPB * table_rows, LANES), F32)
+    sub = iota((CAPB * table_rows, LANES), 0)
+    for r in range(CAPB):
+        pick = jnp.where(count == float(r), hit, 0.0)
+        chosen = pick.astype(BF)
+        first = (pick * hits[0]).astype(BF)
+        code = dot_nn(ones, chosen) + dot_nn(target, first)
+        for i in range(table_rows):
+            part = jnp.broadcast_to(code[0:1, i * LANES : (i + 1) * LANES], table.shape)
+            table = jnp.where(sub == r * table_rows + i, part, table)
+        got = dot_tn(chosen, queries).astype(BF)
+        for c in range(chunks):
+            start = c * slots + r * held
+            pay_ref[:, start : start + held, :] = got[:, c * LANES : (c + 1) * LANES].reshape(
+                devs, held, LANES
+            )
+    coded = table.astype(BF)
+    pay_ref[:, chunks * slots :, :] = jnp.broadcast_to(coded[None], (devs,) + coded.shape)
+
+
+def forward_kernel(
+    place_ref, got_ref, leaf_ref, mid_ref, rows_ref, score_ref, code_ref, stat_ref, wide_ref, table_ref
+):
+    devs, depth, _ = got_ref.shape
+    held, labels, width = leaf_ref.shape
+    chunks = width // LANES
+    slots = CAPB * held
+    body = chunks * slots
+    wide_ref[...] = got_ref[:, :body, :].reshape(devs * body, LANES).astype(F32)
+    tail = depth - body
+    table_ref[...] = got_ref[:, body:, :].astype(F32).reshape(devs * tail, LANES)
+    lane = iota((devs, LANES), 1)
+    codes = jnp.zeros((devs, LANES), F32)
+    for r in range(CAPB):
+        row = table_ref[pl.ds(r * (tail // CAPB) + place_ref[0], devs, stride=tail), :]
+        row = pltpu.roll(row, place_ref[1 + r], 1)
+        codes = jnp.where((lane >= r * held) & (lane < (r + 1) * held), row, codes)
+    code_ref[...] = codes
+    label_f = iota_f((CAPB * devs, labels), 1)
+    stats = jnp.zeros((devs, LANES), F32)
+    for k in range(held):
+        parts = []
+        for r in range(CAPB):
+            parts.append(
+                jnp.concatenate(
+                    [
+                        wide_ref[pl.ds(c * slots + r * held + k, devs, stride=body), :]
+                        for c in range(chunks)
+                    ],
+                    axis=1,
+                )
+            )
+        full = jnp.concatenate(parts, axis=0)
+        rows = full.astype(BF)
+        rows_ref[k] = rows
+        scores = dot_nt(rows, leaf_ref[k])
+        score_ref[k] = scores
+        mid = jnp.sum(full * mid_ref[k : k + 1, :].astype(F32), axis=1, keepdims=True)
+        peak = jnp.max(scores, axis=1, keepdims=True)
+        lse = peak + jnp.log(jnp.sum(jnp.exp(scores - peak), axis=1, keepdims=True))
+        code = jnp.concatenate(
+            [codes[:, r * held + k : r * held + k + 1] for r in range(CAPB)], axis=0
+        )
+        target = jnp.sum(jnp.where(code - 2.0 == label_f, scores, 0.0), axis=1, keepdims=True)
+        for n, value in enumerate((mid, lse, target)):
+            for r in range(CAPB):
+                stats = jnp.where(
+                    lane == n * slots + r * held + k, value[r * devs : (r + 1) * devs], stats
+                )
+    stat_ref[pl.ds(0, devs, stride=SUB), :] = stats
+
+
+def middle_kernel(info_ref, stat_ref, out_ref, loss_ref, *, devs, held, short_len):
+    rows = info_ref.shape[0]
+    slots = CAPB * held
+    info = info_ref[...]
+    stats = stat_ref[pl.ds(0, devs, stride=SUB), :]
+    lane = iota_f((rows, LANES), 1)
+    dev_f = iota_f((rows, devs), 1)
+    owners, spots, mids, lses = [], [], [], []
+    for j in range(short_len):
+        place = info[:, j : j + 1]
+        rank = info[:, short_len + j : short_len + j + 1]
+        dev = jnp.floor(place * (1.0 / held))
+        spot = place - dev * held + rank * held
+        owner = jnp.where(dev == dev_f, 1.0, 0.0)
+        values = dot_nn(owner, stats, HIGH)
+        owners.append(owner)
+        spots.append(spot)
+        mids.append(jnp.sum(jnp.where(lane == spot, values, 0.0), axis=1, keepdims=True))
+        lses.append(jnp.sum(jnp.where(lane == spot + slots, values, 0.0), axis=1, keepdims=True))
+        if j == 0:
+            target = jnp.sum(
+                jnp.where(lane == spot + 2 * slots, values, 0.0), axis=1, keepdims=True
+            )
+
+    def total(columns):
+        peak = functools.reduce(jnp.maximum, columns)
+        return peak + jnp.log(functools.reduce(lambda a, b: a + b, [jnp.exp(v - peak) for v in columns]))
+
+    mid_total = total(mids)
+    leaf_total = total(lses)
+    back = []
+    for j in range(short_len):
+        delta = jnp.exp(mids[j] - mid_total) - (1.0 if j == 0 else 0.0)
+        delta = delta.astype(BF).astype(F32)
+        back.append(
+            jnp.where(
+                lane == spots[j], leaf_total, jnp.where(lane == spots[j] + slots, delta, 0.0)
+            )
+        )
+    sent = dot_tn(jnp.concatenate(owners, axis=0), jnp.concatenate(back, axis=0), HIGH)
+    out_ref[pl.ds(0, devs, stride=SUB), :] = sent
+    losses = jnp.where(lane == 0.0, mid_total - mids[0], jnp.where(lane == 1.0, leaf_total - target, 0.0))
+    loss_ref[...] = losses.T[:SUB, :]
+
+
+def backward_kernel(
+    score_ref, code_ref, norm_ref, leaf_ref, mid_ref, delta_ref, midcol_ref, pay_ref, wide_ref
+):
+    held, pairs, labels = score_ref.shape
+    devs = pairs // CAPB
+    width = leaf_ref.shape[2]
+    chunks = width // LANES
+    slots = CAPB * held
+    body = chunks * slots
+    norms = norm_ref[pl.ds(0, devs, stride=SUB), :]
+    midcol_ref[...] = norms
+    codes = code_ref[...]
+    label_f = iota_f((pairs, labels), 1)
+
+    def column(array, base, k):
+        return jnp.concatenate(
+            [array[:, base + r * held + k : base + r * held + k + 1] for r in range(CAPB)], axis=0
+        )
+
+    for k in range(held):
+        code = column(codes, 0, k)
+        lse = column(norms, 0, k)
+        mid_delta = column(norms, slots, k)
+        onehot = jnp.where(code - 2.0 == label_f, 1.0, 0.0)
+        delta = jnp.where(code > 0.5, jnp.exp(score_ref[k] - lse) - onehot, 0.0).astype(BF)
+        delta_ref[k] = delta
+        back = dot_nn(delta, leaf_ref[k]) + mid_delta * mid_ref[k : k + 1, :].astype(F32)
+        for r in range(CAPB):
+            for c in range(chunks):
+                wide_ref[pl.ds(c * slots + r * held + k, devs, stride=body), :] = back[
+                    r * devs : (r + 1) * devs, c * LANES : (c + 1) * LANES
+                ]
+    pay_ref[...] = wide_ref[...].astype(BF).reshape(devs, body, LANES)
+
+
+def grads_kernel(delta_ref, midcol_ref, rows_ref, leaf_grad_ref, mid_grad_ref):
+    held, pairs, _ = delta_ref.shape
+    devs = pairs // CAPB
+    slots = CAPB * held
+    norms = midcol_ref[...]
+    for k in range(held):
+        rows = rows_ref[k]
+        leaf_grad_ref[k] = dot_tn(delta_ref[k], rows)
+        mid_delta = jnp.concatenate(
+            [norms[:, slots + r * held + k : slots + r * held + k + 1] for r in range(CAPB)], axis=0
+        )
+        mid_grad_ref[k : k + 1, :] = jnp.sum(mid_delta * rows.astype(F32), axis=0, keepdims=True)
+
+
+def finish_kernel(info_ref, back_ref, top_ref, out_ref, *, held, short_len):
+    rows, width = out_ref.shape
+    devs = back_ref.shape[0]
+    clusters = devs * held
+    chunks = width // LANES
+    slots = CAPB * held
+    info = info_ref[...]
+    cluster_f = iota_f((rows, clusters), 1)
+    picks = []
+    for r in range(CAPB):
+        pick = jnp.zeros((rows, clusters), F32)
+        for j in range(short_len):
+            place = jnp.where(
+                info[:, short_len + j : short_len + j + 1] == float(r), info[:, j : j + 1], -1.0
+            )
+            pick = jnp.where(place == cluster_f, 1.0, pick)
+        picks.append(pick.astype(BF))
+    for c in range(chunks):
+        total = top_ref[:, c * LANES : (c + 1) * LANES]
+        for r in range(CAPB):
+            start = c * slots + r * held
+            total = total + dot_nn(
+                picks[r], back_ref[:, start : start + held, :].reshape(clusters, LANES)
+            )
+        out_ref[:, c * LANES : (c + 1) * LANES] = total
+
+
+def top_kernel(
+    where_ref, mine_ref, other_ref, wy_ref, wc_ref, own_ref, weight_ref,
+    back_ref, part_ref, loss_ref, all_ref, *, rows, quarter,
+):
+    steps, depth, width = mine_ref.shape
+    piece = 2 * steps * quarter
+    for n in range(steps):
+        all_ref[n * quarter : (n + 1) * quarter, :] = mine_ref[n, rows : rows + quarter, :]
+        all_ref[(steps + n) * quarter : (steps + n + 1) * quarter, :] = other_ref[n, rows : rows + quarter, :]
+    all_ref[piece : 2 * piece, :] = wy_ref[...]
+    all_ref[2 * piece :, :] = wc_ref[...]
+    held = weight_ref.shape[0]
+    part_ref[...] = jnp.zeros(part_ref.shape, F32)
+    held_base = where_ref[0].astype(F32)
+    held_f = iota_f((rows, held), 1) + held_base
+    for side, ref in ((0, mine_ref), (1, other_ref)):
+        for n in range(steps):
+            block = ref[n, :rows, :]
+            scores = dot_nt(block, all_ref[...])
+            peak = jnp.max(scores, axis=1, keepdims=True)
+            total = peak + jnp.log(jnp.sum(jnp.exp(scores - peak), axis=1, keepdims=True))
+            codes = ref[n, rows + quarter : rows + quarter + 16, :LANES].astype(F32)
+            target = (codes[0:1, :] * 256.0 + codes[1:2, :])
+            target = jnp.broadcast_to(target, (LANES, LANES)).T[:, 0:1]
+            mine = dot_nt(block, weight_ref[...])
+            delta = (jnp.exp(mine - total) - jnp.where(target == held_f, 1.0, 0.0)).astype(BF)
+            part_ref[...] += dot_tn(delta, block)
+            if side == 0 and n == 0:
+                column = own_ref[...]
+                hit = jnp.broadcast_to(column, scores.shape) == target
+                full = (jnp.exp(scores - total) - jnp.where(hit, 1.0, 0.0)).astype(BF)
+                back_ref[...] = dot_nn(full, all_ref[...])
+                loss = total - jnp.sum(jnp.where(hit, scores, 0.0), axis=1, keepdims=True)
+                loss_ref[...] = jnp.broadcast_to(loss, (rows, LANES)).T[:SUB, :]
+
+
+def spec():
+    return pl.BlockSpec(memory_space=pltpu.VMEM)
+
+
+def call(kernel, outs, ins, scratch=(), scalars=0, name=None):
+    return pl.pallas_call(
+        kernel,
+        out_shape=outs,
+        in_specs=[pl.BlockSpec(memory_space=pltpu.SMEM)] * scalars + [spec()] * (len(ins) - scalars),
+        out_specs=jax.tree.map(lambda _: spec(), outs),
+        scratch_shapes=list(scratch),
+        compiler_params=params(),
+        name=name,
+    )(*ins)
+
+
+def shape(dims, dtype):
+    return jax.ShapeDtypeStruct(dims, dtype)
+
+
+def fits(queries, leaf_weight, shortlist, top_weight, devs, dp_size, label_size):
+    rows, width = queries.shape
+    held, labels = leaf_weight.shape[:2]
+    return (
+        rows == LANES
+        and labels == LANES
+        and width % LANES == 0
+        and held % 16 == 0
+        and LANES % held == 0
+        and 3 * CAPB * held <= LANES
+        and CAPB * (devs * held // LANES) % SUB == 0
+        and devs % SUB == 0
+        and dp_size == 4
+        and label_size == 8
+        and top_weight.shape[0] % (dp_size * 16) == 0
+        and top_weight.shape[0] * label_size <= 65536
+        and 2 * shortlist.shape[1] <= LANES
+    )
+
+
+def exchange(array):
+    return lax.all_to_all(array, ("dp", "label"), split_axis=0, concat_axis=0, tiled=True)
+
+
+def per_device(
+    queries, shortlist, slab_slot, top_target, leaf_target, top_weight, mid_weight, leaf_weight
+):
+    dp_size = lax.axis_size("dp")
+    label_size = lax.axis_size("label")
+    devs = dp_size * label_size
+    if not fits(queries, leaf_weight, shortlist, top_weight, devs, dp_size, label_size):
+        return per_device_any(
+            queries, shortlist, slab_slot, top_target, leaf_target, top_weight, mid_weight, leaf_weight
+        )
+    rows, width = queries.shape
+    held, labels = leaf_weight.shape[:2]
+    short_len = shortlist.shape[1]
+    clusters = devs * held
+    chunks = width // LANES
+    slots = CAPB * held
+    body = chunks * slots
+    tail = CAPB * clusters // LANES
+    dp_at = lax.axis_index("dp")
+    label_at = lax.axis_index("label")
+    me = dp_at * label_size + label_at
+
+    payload, info = call(
+        functools.partial(pack_kernel, devs=devs, held=held),
+        (shape((devs, body + tail, LANES), BF), shape((rows, LANES), F32)),
+        (queries, shortlist, slab_slot[None, :], leaf_target[None, :]),
+        name="pack",
+    )
+    got = exchange(payload)
+    first_place = me * held
+    lane_at = first_place % LANES
+    place = jnp.stack(
+        [first_place // LANES] + [(r * held - lane_at) % LANES for r in range(CAPB)]
+    ).astype(jnp.int32)
+    rows_held, scores, codes, stats = call(
+        forward_kernel,
+        (
+            shape((held, CAPB * devs, width), BF),
+            shape((held, CAPB * devs, labels), F32),
+            shape((devs, LANES), F32),
+            shape((devs * SUB, LANES), F32),
+        ),
+        (place, got, leaf_weight, mid_weight),
+        scratch=(pltpu.VMEM((devs * body, LANES), F32), pltpu.VMEM((devs * tail, LANES), F32)),
+        scalars=1,
+        name="forward",
+    )
+    stats_back = exchange(stats.reshape(devs, SUB, LANES)).reshape(devs * SUB, LANES)
+    norms, pair_losses = call(
+        functools.partial(middle_kernel, devs=devs, held=held, short_len=short_len),
+        (shape((devs * SUB, LANES), F32), shape((SUB, rows), F32)),
+        (info, stats_back),
+        name="middle",
+    )
+    norms_held = exchange(norms.reshape(devs, SUB, LANES)).reshape(devs * SUB, LANES)
+    delta, mid_cols, back = call(
+        backward_kernel,
+        (
+            shape((held, CAPB * devs, labels), BF),
+            shape((devs, LANES), F32),
+            shape((devs, body, LANES), BF),
+        ),
+        (scores, codes, norms_held, leaf_weight, mid_weight),
+        scratch=(pltpu.VMEM((devs * body, LANES), F32),),
+        name="backward",
+    )
+    returned = exchange(back)
+    leaf_grad, mid_grad = call(
+        grads_kernel,
+        (shape((held, labels, width), F32), shape((held, width), F32)),
+        (delta, mid_cols, rows_held),
+        name="grads",
+    )
+
+    steps = label_size // 2
+    quarter = top_weight.shape[0] // dp_size
+    held_top = top_weight.shape[0]
+    codes_top = jnp.zeros((16, width), BF)
+    codes_top = codes_top.at[0, :rows].set((top_target // 256).astype(BF))
+    codes_top = codes_top.at[1, :rows].set((top_target % 256).astype(BF))
+    own_quarter = lax.dynamic_slice_in_dim(top_weight, dp_at * quarter, quarter, 0)
+    sent = jnp.concatenate([queries, own_quarter, codes_top], axis=0)
+    sent, got = lax.optimization_barrier((sent, got))
+
+    def along(step):
+        return [
+            (z * 2 + x, ((z - step) % steps) * 2 + x) for z in range(steps) for x in range(2)
+        ]
+
+    mine = jnp.stack([sent] + [lax.ppermute(sent, "label", along(n)) for n in range(1, steps)])
+    other = lax.ppermute(mine, "label", [(i, i ^ 1) for i in range(label_size)])
+    w_near = jnp.concatenate([mine[:, rows : rows + quarter], other[:, rows : rows + quarter]])
+    w_near = w_near.reshape(label_size * quarter, width)
+    w_y = lax.ppermute(w_near, "dp", [(i, i ^ 2) for i in range(dp_size)])
+    w_core = lax.ppermute(
+        jnp.concatenate([w_near, w_y]), "dp", [(i, i ^ 1) for i in range(dp_size)]
+    )
+    z_at, x_at = label_at // 2, label_at % 2
+    source = jnp.concatenate(
+        [((z_at + jnp.arange(steps)) % steps) * 2 + x_at, ((z_at + jnp.arange(steps)) % steps) * 2 + 1 - x_at]
+    )
+    dp_source = jnp.stack([dp_at, dp_at ^ 2, dp_at ^ 1, dp_at ^ 3])
+    own_column = (
+        source[None, :, None] * held_top
+        + dp_source[:, None, None] * quarter
+        + jnp.arange(quarter)[None, None, :]
+    ).reshape(1, dp_size * label_size * quarter)
+    top_back, top_part, top_loss = call(
+        functools.partial(top_kernel, rows=rows, quarter=quarter),
+        (shape((rows, width), F32), shape((held_top, width), F32), shape((SUB, rows), F32)),
+        (
+            (label_at * held_top).astype(jnp.int32)[None],
+            mine,
+            other,
+            w_y,
+            w_core,
+            own_column.astype(F32),
+            top_weight,
+        ),
+        scratch=(pltpu.VMEM((label_size * held_top, width), BF),),
+        scalars=1,
+        name="top",
+    )
+    core = dp_at % 2
+    half = held_top // 2
+    both = top_part + lax.ppermute(top_part, "dp", [(i, i ^ 1) for i in range(dp_size)])
+    share = lax.dynamic_slice_in_dim(both, core * half, half, 0)
+    share = share + lax.ppermute(share, "dp", [(i, i ^ 2) for i in range(dp_size)])
+    rest = lax.ppermute(share, "dp", [(i, i ^ 1) for i in range(dp_size)])
+    low = jnp.where(core == 0, share, rest)
+    high = jnp.where(core == 0, rest, share)
+    top_grad = jnp.concatenate([low, high])
+
+    query_grad = call(
+        functools.partial(finish_kernel, held=held, short_len=short_len),
+        shape((rows, width), F32),
+        (info, returned, top_back),
+        name="finish",
+    )
+    losses = jnp.concatenate([top_loss[:1], pair_losses[:2]])
+    return (query_grad, top_grad, mid_grad, leaf_grad, losses)
+
+
 def solution(mesh):
     in_specs = (
         P(("dp", "label"), None),

time: 344 us -> 163 us (0.47)
  local copies, waits for them, and re-layouts: 105 us -> 7.12 us
  starting transfers between devices: 69.4 us -> 19.8 us
  waiting for transfers between devices: 118 us -> 77.8 us
  Pallas kernels: 0 us -> 37 us
  matrix products: 18.5 us -> 0 us
  blocking collectives: 0 us -> 14.5 us
  between operations: 14.8 us -> 0.83 us
  other arithmetic: 16.7 us -> 3.65 us
    all_to_all x17 -> x3, waiting for transfers between devices: 104 us -> 35.3 us  [exchange(): lax.all_to_all(array, ('dp', 'label'), split_axis=0, concat_axis=0, tiled...]
    all_to_all x17 -> x3, starting transfers between devices: 69.3 us -> 12.7 us  [exchange(): lax.all_to_all(array, ('dp', 'label'), split_axis=0, concat_axis=0, tiled...]
    gather x16 -> x0, local copies, waits for them, and re-layouts: 51.4 us -> none  [the longest x10 34.9 us: per_device(): run_start = jnp.searchsorted(ranked, ranked, side='left')]
    ppermute x0 -> x9, waiting for transfers between devices: none -> 42.5 us  [the longest x1 19.1 us: per_device(): other = lax.ppermute(mine, 'label', [(i, i ^ 1) for i in range(label_size)])]
    pallas_call x0 -> x7, Pallas kernels: none -> 37 us  [call(): pl.pallas_call(kernel, out_shape=outs, in_specs=[pl.BlockSpec(memory_spac...]
    dot_general x8 -> x0, matrix products: 18.5 us -> none  [the longest x1 4.33 us: per_device(): jnp.einsum('abkcl,abkcd->kld', leaf_delta, got_rows, preferred_element_ty...]
    all_to_all x0 -> x1, blocking collectives: none -> 14.5 us  [exchange(): lax.all_to_all(array, ('dp', 'label'), split_axis=0, concat_axis=0, tiled...]
    scatter x5 -> x2, local copies, waits for them, and re-layouts: 13 us -> 0.18 us  [the longest x1 0.17 us: per_device(): codes_top = codes_top.at[1, :rows].set((top_target % 256).astype(BF))]
  transfers between devices with their start and end apart: 20 -> 12, of which waited for: 14 -> 7; matrix products, arithmetic and copies ran while one was open for 25% -> 4% of each run, Pallas kernels for 0% -> 21%
where the time goes in v1:
time: 163 us; the launch traced here: 161 us
  waiting for transfers between devices  77.8 us (48%)
  Pallas kernels  37 us (23%)
  starting transfers between devices  19.8 us (12%)
  blocking collectives  14.5 us (9%)
  local copies, waits for them, and re-layouts  7.12 us (4%)
  other arithmetic  3.65 us (2%)
    pallas_call x7, Pallas kernels, call(): pl.pallas_call(kernel, out_shape=outs, in_specs=[pl.BlockSpec(memory_spac...  37 us
    all_to_all x3, waiting for transfers between devices, exchange(): lax.all_to_all(array, ('dp', 'label'), split_axis=0, concat_axis=0, tiled...  35.3 us
    ppermute x1, waiting for transfers between devices, per_device(): other = lax.ppermute(mine, 'label', [(i, i ^ 1) for i in range(label_size)])  19.1 us
    all_to_all x1, blocking collectives, exchange(): lax.all_to_all(array, ('dp', 'label'), split_axis=0, concat_axis=0, tiled...  14.5 us
    ppermute x3, waiting for transfers between devices, per_device(): lax.ppermute(sent, 'label', along(n))  14.2 us
    all_to_all x3, starting transfers between devices, exchange(): lax.all_to_all(array, ('dp', 'label'), split_axis=0, concat_axis=0, tiled...  12.7 us
    ppermute x1, waiting for transfers between devices, per_device(): lax.ppermute(share, 'dp', [(i, i ^ 2) for i in range(dp_size)])  7.15 us
    unnamed x17, local copies, waits for them, and re-layouts  4.01 us
  transfers between devices with their start and end apart: 12, of which 7 were waited for; matrix products, arithmetic and copies ran while one was open for 4% of the time, Pallas kernels for 21%

profile of v1, /device:TPU:0, one launch (start us, length us, event | category | flops | bytes accessed | tf_op | source)
XLA Modules:
  0.0 160.7 jit_solution(5933140617069355588)
XLA Ops:
  0.7 1.5 copy.13.short_ref
  2.1 3.0 %pack.1 = (bf16[32,136,128]{2,1,0:T(8,128)(2,1)}, f32[128,128]{1,0:T(8,128)}) custom-call(bf16[128,512]{1,0:T(8,128)(2,1)} %q_ref.1, s32[128,4]{1,0:T(8,128)} %copy.13.short_ref, s32[1,512]{1,0:T(1,128)} %bitcast.33, s32[1,128]{1,0:T(1,128)} %bitcast.34), custom_call_target="tpu_custom_call" | custom-call | tf_op jit(solution)/shard_map/pack/pallas_call | solution.py:451
  5.1 7.3 %all-to-all-start = ((bf16[32,136,128]{2,1,0:T(8,128)(2,1)}), bf16[32,136,128]{2,1,0:T(8,128)(2,1)S(1)}, u32[]{:S(2)}, u32[]{:S(2)}) async-start(bf16[32,136,128]{2,1,0:T(8,128)(2,1)} %get-tuple-element.47), calls=%async_computation | async-start | bytes 2228224 | tf_op jit(solution)/shard_map/all_to_all | solution.py:487
  12.7 0.9 constant_dynamic-slice_fusion
  13.5 27.8 %all-to-all-done.got_ref = bf16[32,136,128]{2,1,0:T(8,128)(2,1)S(1)} async-done(((bf16[32,136,128]{2,1,0:T(8,128)(2,1)}), bf16[32,136,128]{2,1,0:T(8,128)(2,1)S(1)}, u32[]{:S(2)}, u32[]{:S(2)}) %all-to-all-start) | async-done | bytes 1114144 | tf_op jit(solution)/shard_map/all_to_all | solution.py:487
  41.5 1.5 collective-permute-start.1
  43.0 2.1 %collective-permute-start = (bf16[208,512]{1,0:T(8,128)(2,1)S(1)}, bf16[208,512]{1,0:T(8,128)(2,1)S(1)}, u32[]{:S(2)}, u32[]{:S(2)}) collective-permute-start(bf16[208,512]{1,0:T(8,128)(2,1)S(1)} %pad_maximum_fusion.4), channel_id=1, source_target_pairs={{0,6},{1,7},{2,0},{3,1},{4,2},{5,3},{6,4},{7,5},{8,14},{9,15},{10,... | collective-permute-start | bytes 638984 | tf_op jit(solution)/shard_map/ppermute | solution.py:579
  45.1 6.2 %collective-permute-done.2 = bf16[208,512]{1,0:T(8,128)(2,1)S(1)} collective-permute-done((bf16[208,512]{1,0:T(8,128)(2,1)S(1)}, bf16[208,512]{1,0:T(8,128)(2,1)S(1)}, u32[]{:S(2)}, u32[]{:S(2)}) %collective-permute-start.2) | collective-permute-done | bytes 213024 | tf_op jit(solution)/shard_map/ppermute | solution.py:579
  51.3 8.0 %collective-permute-done.1 = bf16[208,512]{1,0:T(8,128)(2,1)S(1)} collective-permute-done((bf16[208,512]{1,0:T(8,128)(2,1)S(1)}, bf16[208,512]{1,0:T(8,128)(2,1)S(1)}, u32[]{:S(2)}, u32[]{:S(2)}) %collective-permute-start.1) | collective-permute-done | bytes 213024 | tf_op jit(solution)/shard_map/ppermute | solution.py:579
  59.4 1.0 collective-permute-start.3
  60.5 19.1 %collective-permute-done.3.other_ref = bf16[4,208,512]{2,1,0:T(8,128)(2,1)S(1)} collective-permute-done((bf16[4,208,512]{2,1,0:T(8,128)(2,1)S(1)}, bf16[4,208,512]{2,1,0:T(8,128)(2,1)S(1)}, u32[]{:S(2)}, u32[]{:S(2)}) %collective-permute-start.3) | collective-permute-done | bytes 852000 | tf_op jit(solution)/shard_map/ppermute | solution.py:580
  79.5 0.9 copy-done.4
  81.5 6.1 %forward.1 = (bf16[16,64,512]{2,1,0:T(8,128)(2,1)}, f32[16,64,128]{2,1,0:T(8,128)}, f32[32,128]{1,0:T(8,128)}, f32[256,128]{1,0:T(8,128)}) custom-call(s32[3]{0:T(128)} %pad_add_fusion.place_ref, bf16[32,136,128]{2,1,0:T(8,128)(2,1)} %copy-done.1, bf16[16,128,512]{2,1,0:T(8,128)(2,1)} %leaf_ref.3, bf16[16,512]{1,0:T(8,128)(2,1)} %mid_ref.3), custom_call_target="tpu_custom_call" | custom-call | tf_op jit(solution)/shard_map/forward/pallas_call | solution.py:451
  87.7 14.5 %all_to_all.20 = f32[32,8,128]{2,1,0:T(8,128)} all-to-all(f32[32,8,128]{2,1,0:T(8,128)} %bitcast.32), channel_id=1, replica_groups=mesh['dp'=4,'label'=8] {'dp','label'}, dimensions={0} | all-to-all | bytes 262144 | tf_op jit(solution)/shard_map/all_to_all | solution.py:487
  102.2 2.8 %middle.1 = (f32[256,128]{1,0:T(8,128)}, f32[8,128]{1,0:T(8,128)}) custom-call(f32[128,128]{1,0:T(8,128)} %get-tuple-element.46.info_ref, f32[256,128]{1,0:T(8,128)} %bitcast.27), custom_call_target="tpu_custom_call" | custom-call | tf_op jit(solution)/shard_map/middle/pallas_call | solution.py:451
  105.0 2.6 %all-to-all-start.2 = ((f32[32,8,128]{2,1,0:T(8,128)}), f32[32,8,128]{2,1,0:T(8,128)S(1)}, u32[]{:S(2)}, u32[]{:S(2)}) async-start(f32[32,8,128]{2,1,0:T(8,128)} %bitcast.31), calls=%async_computation.2 | async-start | bytes 262144 | tf_op jit(solution)/shard_map/all_to_all | solution.py:487
  107.8 7.5 %all-to-all-done.2 = f32[32,8,128]{2,1,0:T(8,128)S(1)} async-done(((f32[32,8,128]{2,1,0:T(8,128)}), f32[32,8,128]{2,1,0:T(8,128)S(1)}, u32[]{:S(2)}, u32[]{:S(2)}) %all-to-all-start.2) | async-done | bytes 131104 | tf_op jit(solution)/shard_map/all_to_all | solution.py:487
  115.4 0.7 copy-done.5
  116.0 5.5 %backward.1 = (bf16[16,64,128]{2,1,0:T(8,128)(2,1)}, f32[32,128]{1,0:T(8,128)}, bf16[32,128,128]{2,1,0:T(8,128)(2,1)}) custom-call(f32[16,64,128]{2,1,0:T(8,128)} %get-tuple-element.48.score_ref, f32[32,128]{1,0:T(8,128)} %get-tuple-element.49.code_ref, f32[256,128]{1,0:T(8,128)} %bitcast.26, bf16[16,128,512]{2,1,0:T(8,128)(2,1)} %leaf_ref.3, ...), custom_call_target="tpu_custom_call" | custom-call | tf_op jit(solution)/shard_map/backward/pallas_call | solution.py:451
  121.6 2.8 %all-to-all-start.3 = ((bf16[32,128,128]{2,1,0:T(8,128)(2,1)}), bf16[32,128,128]{2,1,0:T(8,128)(2,1)S(1)}, u32[]{:S(2)}, u32[]{:S(2)}) async-start(bf16[32,128,128]{2,1,0:T(8,128)(2,1)} %get-tuple-element.52), calls=%async_computation.3 | async-start | bytes 2097152 | tf_op jit(solution)/shard_map/all_to_all | solution.py:487
  124.7 0.7 convert_element_type.14.own_ref
  125.4 12.6 %top.1 = (f32[128,512]{1,0:T(8,128)}, f32[256,512]{1,0:T(8,128)}, f32[8,128]{1,0:T(8,128)}) custom-call(s32[1]{0:T(128)} %bitcast.9.where_ref, bf16[4,208,512]{2,1,0:T(8,128)(2,1)} %copy-done, bf16[4,208,512]{2,1,0:T(8,128)(2,1)} %copy-done.4, bf16[512,512]{1,0:T(8,128)(2,1)} %copy-done.3, bf16[1024,512]{1,0:T(8,128)(2,1)} %collective-permute-done.5.wc_ref, ...), custom_call_target="tpu_custom_call" | custom-call | tf_op jit(solution)/shard_map/top/pallas_call | solution.py:451
  138.0 2.1 %collective-permute-done.6 = f32[256,512]{1,0:T(8,128)S(1)} collective-permute-done((f32[256,512]{1,0:T(8,128)}, f32[256,512]{1,0:T(8,128)S(1)}, u32[]{:S(2)}, u32[]{:S(2)}) %collective-permute-start.6) | collective-permute-done | bytes 524320 | tf_op jit(solution)/shard_map/ppermute | solution.py:615
  140.1 1.0 dynamic-slice_add_fusion
  141.1 1.6 collective-permute-start.7
  142.7 7.1 %collective-permute-done.7 = f32[128,512]{1,0:T(8,128)S(1)} collective-permute-done((f32[128,512]{1,0:T(8,128)S(1)}, f32[128,512]{1,0:T(8,128)S(1)}, u32[]{:S(2)}, u32[]{:S(2)}) %collective-permute-start.7) | collective-permute-done | bytes 262176 | tf_op jit(solution)/shard_map/ppermute | solution.py:617
  149.9 0.7 slice.50
  150.6 4.3 %grads.1 = (f32[16,128,512]{2,1,0:T(8,128)}, f32[16,512]{1,0:T(8,128)}) custom-call(bf16[16,64,128]{2,1,0:T(8,128)(2,1)} %get-tuple-element.56.delta_ref, f32[32,128]{1,0:T(8,128)} %get-tuple-element.57.midcol_ref, bf16[16,64,512]{2,1,0:T(8,128)(2,1)} %get-tuple-element.58.rows_ref), custom_call_target="tpu_custom_call" | custom-call | tf_op jit(solution)/shard_map/grads/pallas_call | solution.py:451
  154.9 0.7 slice.49
  155.6 1.0 copy-done.2
  156.6 2.7 %finish.1 = f32[128,512]{1,0:T(8,128)} custom-call(f32[128,128]{1,0:T(8,128)} %get-tuple-element.46.info_ref, bf16[32,128,128]{2,1,0:T(8,128)(2,1)} %copy-done.2, f32[128,512]{1,0:T(8,128)} %get-tuple-element.54.top_ref), custom_call_target="tpu_custom_call" | custom-call | tf_op jit(solution)/shard_map/finish/pallas_call | solution.py:451
  159.9 0.8 pad_maximum_fusion.3
  (41 shorter events, 3.0 us)
Async XLA Ops:
  0.6 12.9 %copy-start.6 = (bf16[128,512]{1,0:T(8,128)(2,1)S(1)}, bf16[128,512]{1,0:T(8,128)(2,1)}, u32[]{:S(2)}) copy-start(bf16[128,512]{1,0:T(8,128)(2,1)} %q_ref.1) | copy-start | bytes 393220
  0.6 11.8 %copy-start.7 = (s32[128]{0:T(128)S(1)}, s32[128]{0:T(128)}, u32[]{:S(2)}) copy-start(s32[128]{0:T(128)} %param.15) | copy-start | bytes 1540
  5.1 36.2 %all-to-all-start = ((bf16[32,136,128]{2,1,0:T(8,128)(2,1)}), bf16[32,136,128]{2,1,0:T(8,128)(2,1)S(1)}, u32[]{:S(2)}, u32[]{:S(2)}) async-start(bf16[32,136,128]{2,1,0:T(8,128)(2,1)} %get-tuple-element.47), calls=%async_computation | async-start | bytes 2228224 | tf_op jit(solution)/shard_map/all_to_all | solution.py:487
  41.3 40.2 %copy-start.1 = (bf16[32,136,128]{2,1,0:T(8,128)(2,1)}, bf16[32,136,128]{2,1,0:T(8,128)(2,1)S(1)}, u32[]{:S(2)}) copy-start(bf16[32,136,128]{2,1,0:T(8,128)(2,1)S(1)} %all-to-all-done.got_ref) | copy-start | bytes 3342340
  41.3 10.0 %collective-permute-start.2 = (bf16[208,512]{1,0:T(8,128)(2,1)S(1)}, bf16[208,512]{1,0:T(8,128)(2,1)S(1)}, u32[]{:S(2)}, u32[]{:S(2)}) collective-permute-start(bf16[208,512]{1,0:T(8,128)(2,1)S(1)} %pad_maximum_fusion.4), channel_id=1, source_target_pairs={{0,2},{1,3},{2,4},{3,5},{4,6},{5,7},{6,0},{7,1},{8,10},{9,11},{10,... | collective-permute-start | bytes 638984 | tf_op jit(solution)/shard_map/ppermute | solution.py:579
  41.5 17.8 %collective-permute-start.1 = (bf16[208,512]{1,0:T(8,128)(2,1)S(1)}, bf16[208,512]{1,0:T(8,128)(2,1)S(1)}, u32[]{:S(2)}, u32[]{:S(2)}) collective-permute-start(bf16[208,512]{1,0:T(8,128)(2,1)S(1)} %pad_maximum_fusion.4), channel_id=1, source_target_pairs={{0,4},{1,5},{2,6},{3,7},{4,0},{5,1},{6,2},{7,3},{8,12},{9,13},{10,... | collective-permute-start | bytes 638984 | tf_op jit(solution)/shard_map/ppermute | solution.py:579
  43.0 16.2 %collective-permute-start = (bf16[208,512]{1,0:T(8,128)(2,1)S(1)}, bf16[208,512]{1,0:T(8,128)(2,1)S(1)}, u32[]{:S(2)}, u32[]{:S(2)}) collective-permute-start(bf16[208,512]{1,0:T(8,128)(2,1)S(1)} %pad_maximum_fusion.4), channel_id=1, source_target_pairs={{0,6},{1,7},{2,0},{3,1},{4,2},{5,3},{6,4},{7,5},{8,14},{9,15},{10,... | collective-permute-start | bytes 638984 | tf_op jit(solution)/shard_map/ppermute | solution.py:579
  59.4 28.3 %copy-start = (bf16[4,208,512]{2,1,0:T(8,128)(2,1)}, bf16[4,208,512]{2,1,0:T(8,128)(2,1)S(1)}, u32[]{:S(2)}) copy-start(bf16[4,208,512]{2,1,0:T(8,128)(2,1)S(1)} %pad_maximum_fusion.1.mine_ref) | copy-start | bytes 2555908
  59.4 20.1 %collective-permute-start.3 = (bf16[4,208,512]{2,1,0:T(8,128)(2,1)S(1)}, bf16[4,208,512]{2,1,0:T(8,128)(2,1)S(1)}, u32[]{:S(2)}, u32[]{:S(2)}) collective-permute-start(bf16[4,208,512]{2,1,0:T(8,128)(2,1)S(1)} %pad_maximum_fusion.1.mine_ref), channel_id=1, source_target_pairs={{0,1},{1,0},{2,3},{3,2},{4,5},{5,4},{6,7},{7,6},{8,9},{9,8},{10,11... | collective-permute-start | bytes 2555912 | tf_op jit(solution)/shard_map/ppermute | solution.py:580
  79.5 0.9 copy-start.4
  80.5 27.0 %collective-permute-start.4 = (bf16[512,512]{1,0:T(8,128)(2,1)S(1)}, bf16[512,512]{1,0:T(8,128)(2,1)S(1)}, u32[]{:S(2)}, u32[]{:S(2)}) collective-permute-start(bf16[512,512]{1,0:T(8,128)(2,1)S(1)} %bitcast.23), channel_id=1, source_target_pairs={{0,16},{8,24},{16,0},{24,8},{1,17},{9,25},{17,1},{25,9},{2,18},{10... | collective-permute-start | bytes 1572872 | tf_op jit(solution)/shard_map/ppermute | solution.py:583
  105.0 10.4 %all-to-all-start.2 = ((f32[32,8,128]{2,1,0:T(8,128)}), f32[32,8,128]{2,1,0:T(8,128)S(1)}, u32[]{:S(2)}, u32[]{:S(2)}) async-start(f32[32,8,128]{2,1,0:T(8,128)} %bitcast.31), calls=%async_computation.2 | async-start | bytes 262144 | tf_op jit(solution)/shard_map/all_to_all | solution.py:487
  107.6 14.0 %copy-start.3 = (bf16[512,512]{1,0:T(8,128)(2,1)}, bf16[512,512]{1,0:T(8,128)(2,1)S(1)}, u32[]{:S(2)}) copy-start(bf16[512,512]{1,0:T(8,128)(2,1)S(1)} %collective-permute-done.4.wy_ref) | copy-start | bytes 1572868
  107.7 17.8 %collective-permute-start.5 = (bf16[1024,512]{1,0:T(8,128)(2,1)S(1)}, bf16[1024,512]{1,0:T(8,128)(2,1)}, u32[]{:S(2)}, u32[]{:S(2)}) collective-permute-start(bf16[1024,512]{1,0:T(8,128)(2,1)S(1)} %pad_maximum_fusion), channel_id=1, source_target_pairs={{0,8},{8,0},{16,24},{24,16},{1,9},{9,1},{17,25},{25,17},{2,10},{10... | collective-permute-start | bytes 3145736 | tf_op jit(solution)/shard_map/ppermute | solution.py:584
  115.4 0.7 copy-start.5
  121.6 34.0 %all-to-all-start.3 = ((bf16[32,128,128]{2,1,0:T(8,128)(2,1)}), bf16[32,128,128]{2,1,0:T(8,128)(2,1)S(1)}, u32[]{:S(2)}, u32[]{:S(2)}) async-start(bf16[32,128,128]{2,1,0:T(8,128)(2,1)} %get-tuple-element.52), calls=%async_computation.3 | async-start | bytes 2097152 | tf_op jit(solution)/shard_map/all_to_all | solution.py:487
  138.0 2.1 %collective-permute-start.6 = (f32[256,512]{1,0:T(8,128)}, f32[256,512]{1,0:T(8,128)S(1)}, u32[]{:S(2)}, u32[]{:S(2)}) collective-permute-start(f32[256,512]{1,0:T(8,128)} %get-tuple-element.55), channel_id=1, source_target_pairs={{0,8},{8,0},{16,24},{24,16},{1,9},{9,1},{17,25},{25,17},{2,10},{10... | collective-permute-start | bytes 1572872 | tf_op jit(solution)/shard_map/ppermute | solution.py:615
  141.1 8.7 %collective-permute-start.7 = (f32[128,512]{1,0:T(8,128)S(1)}, f32[128,512]{1,0:T(8,128)S(1)}, u32[]{:S(2)}, u32[]{:S(2)}) collective-permute-start(f32[128,512]{1,0:T(8,128)S(1)} %dynamic-slice_add_fusion), channel_id=1, source_target_pairs={{0,16},{8,24},{16,0},{24,8},{1,17},{9,25},{17,1},{25,9},{2,18},{10... | collective-permute-start | bytes 786440 | tf_op jit(solution)/shard_map/ppermute | solution.py:617
  149.9 10.0 %collective-permute-start.8 = (f32[128,512]{1,0:T(8,128)S(1)}, f32[128,512]{1,0:T(8,128)S(1)}, u32[]{:S(2)}, u32[]{:S(2)}) collective-permute-start(f32[128,512]{1,0:T(8,128)S(1)} %add.145), channel_id=1, source_target_pairs={{0,8},{8,0},{16,24},{24,16},{1,9},{9,1},{17,25},{25,17},{2,10},{10... | collective-permute-start | bytes 786440 | tf_op jit(solution)/shard_map/ppermute | solution.py:618
  155.6 1.0 copy-start.2

commit v2 on v1

--- a/solution.py
+++ b/solution.py
@@ -156,8 +156,8 @@
 HIGH = lax.Precision.HIGHEST
 
 
-def params():
-    return pltpu.CompilerParams(vmem_limit_bytes=56 * 1024 * 1024)
+def params(mib):
+    return pltpu.CompilerParams(vmem_limit_bytes=mib * 1024 * 1024)
 
 
 def iota(shape, dim):
@@ -186,15 +186,18 @@
     )
 
 
-def pack_kernel(q_ref, short_ref, slab_ref, leaf_t_ref, pay_ref, info_ref, *, devs, held):
+def pack_kernel(
+    q_ref, short_ref, slab_ref, leaf_t_ref, top_t_ref, pay_ref, info_ref, own_ref, *, devs, held
+):
     rows, width = q_ref.shape
-    short_len = short_ref.shape[1]
+    short_len = short_ref.shape[0]
     clusters = slab_ref.shape[1]
     chunks = width // LANES
     slots = CAPB * held
     cluster_f = iota_f((rows, clusters), 1)
     slab = jnp.broadcast_to(slab_ref[...].astype(F32), (rows, clusters))
     short = short_ref[...].astype(F32)
+    short = jnp.concatenate([short, jnp.zeros((rows - short_len, rows), F32)], axis=0).T
     places, hits = [], []
     for j in range(short_len):
         place = jnp.sum(jnp.where(short[:, j : j + 1] == cluster_f, slab, 0.0), axis=1, keepdims=True)
@@ -211,6 +214,12 @@
         info = jnp.where(lane == short_len + j, rank, info)
     info_ref[...] = info
     queries = q_ref[...]
+    own_ref[:rows, :] = queries
+    top_target = jnp.broadcast_to(top_t_ref[...].astype(F32), (16, rows))
+    high = jnp.floor(top_target * (1.0 / 256.0))
+    code_at = iota((16, rows), 0)
+    coded = jnp.where(code_at == 0, high, jnp.where(code_at == 1, top_target - 256.0 * high, 0.0))
+    own_ref[rows:, :] = jnp.concatenate([coded] * chunks, axis=1).astype(BF)
     target = jnp.broadcast_to(leaf_t_ref[...].astype(F32) + 1.0, (SUB, rows)).astype(BF)
     ones = jnp.ones((SUB, rows), BF)
     table_rows = clusters // LANES
@@ -234,24 +243,46 @@
     pay_ref[:, chunks * slots :, :] = jnp.broadcast_to(coded[None], (devs,) + coded.shape)
 
 
+def halves(source, target, sems):
+    half = source.shape[0] // 2
+    return [
+        pltpu.make_async_copy(
+            source.at[pl.ds(n * half, half)], target.at[pl.ds(n * half, half)], sems.at[n]
+        )
+        for n in range(2)
+    ]
+
+
+def start(copies):
+    for copy in copies:
+        copy.start()
+    return copies
+
+
 def forward_kernel(
-    place_ref, got_ref, leaf_ref, mid_ref, rows_ref, score_ref, code_ref, stat_ref, wide_ref, table_ref
+    me_ref, got_ref, leaf_in, mid_ref, rows_out, score_out, stat_ref,
+    wide_ref, table_ref, leaf_ref, rows_ref, score_ref, leaf_sem, rows_sem, score_sem,
 ):
     devs, depth, _ = got_ref.shape
     held, labels, width = leaf_ref.shape
+    fetches = start(halves(leaf_in, leaf_ref, leaf_sem))
+    sends = list(zip(halves(rows_ref, rows_out, rows_sem), halves(score_ref, score_out, score_sem)))
     chunks = width // LANES
     slots = CAPB * held
     body = chunks * slots
     wide_ref[...] = got_ref[:, :body, :].reshape(devs * body, LANES).astype(F32)
     tail = depth - body
     table_ref[...] = got_ref[:, body:, :].astype(F32).reshape(devs * tail, LANES)
+    first = me_ref[0] * held
+    row_at = first // LANES
+    lane_at = first - row_at * LANES
     lane = iota((devs, LANES), 1)
     codes = jnp.zeros((devs, LANES), F32)
     for r in range(CAPB):
-        row = table_ref[pl.ds(r * (tail // CAPB) + place_ref[0], devs, stride=tail), :]
-        row = pltpu.roll(row, place_ref[1 + r], 1)
+        row = table_ref[pl.ds(r * (tail // CAPB) + row_at, devs, stride=tail), :]
+        row = pltpu.roll(row, lax.rem(r * held - lane_at + LANES, LANES), 1)
         codes = jnp.where((lane >= r * held) & (lane < (r + 1) * held), row, codes)
-    code_ref[...] = codes
+    stat_ref[pl.ds(1, devs, stride=SUB), :] = codes
     label_f = iota_f((CAPB * devs, labels), 1)
     stats = jnp.zeros((devs, LANES), F32)
     for k in range(held):
@@ -269,6 +300,8 @@
         full = jnp.concatenate(parts, axis=0)
         rows = full.astype(BF)
         rows_ref[k] = rows
+        if k % (held // 2) == 0:
+            fetches[k // (held // 2)].wait()
         scores = dot_nt(rows, leaf_ref[k])
         score_ref[k] = scores
         mid = jnp.sum(full * mid_ref[k : k + 1, :].astype(F32), axis=1, keepdims=True)
@@ -283,7 +316,12 @@
                 stats = jnp.where(
                     lane == n * slots + r * held + k, value[r * devs : (r + 1) * devs], stats
                 )
+        if (k + 1) % (held // 2) == 0:
+            start(sends[k // (held // 2)])
     stat_ref[pl.ds(0, devs, stride=SUB), :] = stats
+    for pair in sends:
+        for send in pair:
+            send.wait()
 
 
 def middle_kernel(info_ref, stat_ref, out_ref, loss_ref, *, devs, held, short_len):
@@ -332,17 +370,19 @@
 
 
 def backward_kernel(
-    score_ref, code_ref, norm_ref, leaf_ref, mid_ref, delta_ref, midcol_ref, pay_ref, wide_ref
+    score_in, stat_ref, norm_ref, leaf_in, mid_ref, delta_ref, pay_out,
+    wide_ref, score_ref, leaf_ref, pay_ref, score_sem, leaf_sem, pay_sem,
 ):
     held, pairs, labels = score_ref.shape
+    fetches = start(halves(score_in, score_ref, score_sem))
+    leaf_fetches = start(halves(leaf_in, leaf_ref, leaf_sem))
     devs = pairs // CAPB
     width = leaf_ref.shape[2]
     chunks = width // LANES
     slots = CAPB * held
     body = chunks * slots
     norms = norm_ref[pl.ds(0, devs, stride=SUB), :]
-    midcol_ref[...] = norms
-    codes = code_ref[...]
+    codes = stat_ref[pl.ds(1, devs, stride=SUB), :]
     label_f = iota_f((pairs, labels), 1)
 
     def column(array, base, k):
@@ -355,6 +395,9 @@
         lse = column(norms, 0, k)
         mid_delta = column(norms, slots, k)
         onehot = jnp.where(code - 2.0 == label_f, 1.0, 0.0)
+        if k % (held // 2) == 0:
+            fetches[k // (held // 2)].wait()
+            leaf_fetches[k // (held // 2)].wait()
         delta = jnp.where(code > 0.5, jnp.exp(score_ref[k] - lse) - onehot, 0.0).astype(BF)
         delta_ref[k] = delta
         back = dot_nn(delta, leaf_ref[k]) + mid_delta * mid_ref[k : k + 1, :].astype(F32)
@@ -363,14 +406,26 @@
                 wide_ref[pl.ds(c * slots + r * held + k, devs, stride=body), :] = back[
                     r * devs : (r + 1) * devs, c * LANES : (c + 1) * LANES
                 ]
-    pay_ref[...] = wide_ref[...].astype(BF).reshape(devs, body, LANES)
-
-
-def grads_kernel(delta_ref, midcol_ref, rows_ref, leaf_grad_ref, mid_grad_ref):
+    sends = []
+    for g in range(0, devs, SUB):
+        pay_ref[g : g + SUB] = (
+            wide_ref[g * body : (g + SUB) * body, :].astype(BF).reshape(SUB, body, LANES)
+        )
+        sends.append(
+            pltpu.make_async_copy(
+                pay_ref.at[pl.ds(g, SUB)], pay_out.at[pl.ds(g, SUB)], pay_sem.at[g // SUB]
+            )
+        )
+        sends[-1].start()
+    for send in sends:
+        send.wait()
+
+
+def grads_kernel(delta_ref, norm_ref, rows_ref, leaf_grad_ref, mid_grad_ref):
     held, pairs, _ = delta_ref.shape
     devs = pairs // CAPB
     slots = CAPB * held
-    norms = midcol_ref[...]
+    norms = norm_ref[pl.ds(0, devs, stride=SUB), :]
     for k in range(held):
         rows = rows_ref[k]
         leaf_grad_ref[k] = dot_tn(delta_ref[k], rows)
@@ -407,54 +462,75 @@
         out_ref[:, c * LANES : (c + 1) * LANES] = total
 
 
-def top_kernel(
-    where_ref, mine_ref, other_ref, wy_ref, wc_ref, own_ref, weight_ref,
-    back_ref, part_ref, loss_ref, all_ref, *, rows, quarter,
+def top_step(block, target, weights, weight_held, held_base):
+    scores = dot_nt(block, weights)
+    peak = jnp.max(scores, axis=1, keepdims=True)
+    total = peak + jnp.log(jnp.sum(jnp.exp(scores - peak), axis=1, keepdims=True))
+    mine = dot_nt(block, weight_held)
+    held_f = iota_f(mine.shape, 1) + held_base
+    delta = (jnp.exp(mine - total) - jnp.where(target == held_f, 1.0, 0.0)).astype(BF)
+    return scores, total, dot_tn(delta, block)
+
+
+def top_column(codes):
+    target = codes[0:1, :LANES].astype(F32) * 256.0 + codes[1:2, :LANES].astype(F32)
+    return jnp.broadcast_to(target, (LANES, LANES)).T[:, 0:1]
+
+
+def top_own_kernel(
+    where_ref, own_ref, near_ref, other_ref, wy_ref, wc_ref, column_ref, weight_ref,
+    back_ref, part_ref, loss_ref, all_ref,
 ):
-    steps, depth, width = mine_ref.shape
-    piece = 2 * steps * quarter
-    for n in range(steps):
-        all_ref[n * quarter : (n + 1) * quarter, :] = mine_ref[n, rows : rows + quarter, :]
-        all_ref[(steps + n) * quarter : (steps + n + 1) * quarter, :] = other_ref[n, rows : rows + quarter, :]
-    all_ref[piece : 2 * piece, :] = wy_ref[...]
-    all_ref[2 * piece :, :] = wc_ref[...]
-    held = weight_ref.shape[0]
-    part_ref[...] = jnp.zeros(part_ref.shape, F32)
-    held_base = where_ref[0].astype(F32)
-    held_f = iota_f((rows, held), 1) + held_base
-    for side, ref in ((0, mine_ref), (1, other_ref)):
-        for n in range(steps):
-            block = ref[n, :rows, :]
-            scores = dot_nt(block, all_ref[...])
-            peak = jnp.max(scores, axis=1, keepdims=True)
-            total = peak + jnp.log(jnp.sum(jnp.exp(scores - peak), axis=1, keepdims=True))
-            codes = ref[n, rows + quarter : rows + quarter + 16, :LANES].astype(F32)
-            target = (codes[0:1, :] * 256.0 + codes[1:2, :])
-            target = jnp.broadcast_to(target, (LANES, LANES)).T[:, 0:1]
-            mine = dot_nt(block, weight_ref[...])
-            delta = (jnp.exp(mine - total) - jnp.where(target == held_f, 1.0, 0.0)).astype(BF)
-            part_ref[...] += dot_tn(delta, block)
-            if side == 0 and n == 0:
-                column = own_ref[...]
-                hit = jnp.broadcast_to(column, scores.shape) == target
-                full = (jnp.exp(scores - total) - jnp.where(hit, 1.0, 0.0)).astype(BF)
-                back_ref[...] = dot_nn(full, all_ref[...])
-                loss = total - jnp.sum(jnp.where(hit, scores, 0.0), axis=1, keepdims=True)
-                loss_ref[...] = jnp.broadcast_to(loss, (rows, LANES)).T[:SUB, :]
+    rows = own_ref.shape[0] - 16
+    piece = near_ref.shape[0]
+    all_ref[:piece, :] = near_ref[...]
+    all_ref[piece : 2 * piece, :] = other_ref[...]
+    all_ref[2 * piece : 4 * piece, :] = wy_ref[...]
+    all_ref[4 * piece :, :] = wc_ref[...]
+    block = own_ref[:rows, :]
+    target = top_column(own_ref[rows:, :])
+    scores, total, part = top_step(
+        block, target, all_ref[...], weight_ref[...], where_ref[0].astype(F32)
+    )
+    part_ref[...] = part
+    hit = jnp.broadcast_to(column_ref[...], scores.shape) == target
+    full = (jnp.exp(scores - total) - jnp.where(hit, 1.0, 0.0)).astype(BF)
+    back_ref[...] = dot_nn(full, all_ref[...])
+    loss = total - jnp.sum(jnp.where(hit, scores, 0.0), axis=1, keepdims=True)
+    loss_ref[...] = jnp.broadcast_to(loss, (rows, LANES)).T[:SUB, :]
+
+
+def top_more_kernel(where_ref, blocks_ref, all_ref, weight_ref, part_ref, out_ref, *, first):
+    count, depth, _ = blocks_ref.shape
+    rows = depth - 16
+    numbers = range(first, count)
+    block = jnp.concatenate([blocks_ref[n, :rows, :] for n in numbers], axis=0)
+    target = jnp.concatenate([top_column(blocks_ref[n, rows:, :]) for n in numbers], axis=0)
+    base = where_ref[0].astype(F32)
+    part = top_step(block, target, all_ref[...], weight_ref[...], base)[2]
+    out_ref[...] = part_ref[...] + part
 
 
 def spec():
     return pl.BlockSpec(memory_space=pltpu.VMEM)
 
 
-def call(kernel, outs, ins, scratch=(), scalars=0, name=None):
+def call(kernel, outs, ins, scratch=(), scalars=0, far_ins=(), far_outs=(), mib=58, name=None):
+    far = pl.BlockSpec(memory_space=pltpu.HBM)
+    small = pl.BlockSpec(memory_space=pltpu.SMEM)
+    listed = isinstance(outs, tuple)
+    out_specs = tuple(
+        far if n in far_outs else spec() for n in range(len(outs) if listed else 1)
+    )
     return pl.pallas_call(
         kernel,
         out_shape=outs,
-        in_specs=[pl.BlockSpec(memory_space=pltpu.SMEM)] * scalars + [spec()] * (len(ins) - scalars),
-        out_specs=jax.tree.map(lambda _: spec(), outs),
+        in_specs=[
+            small if n < scalars else far if n in far_ins else spec() for n in range(len(ins))
+        ],
+        out_specs=out_specs if listed else out_specs[0],
         scratch_shapes=list(scratch),
-        compiler_params=params(),
+        compiler_params=params(mib),
         name=name,
     )(*ins)
 
@@ -481,6 +557,10 @@
         and top_weight.shape[0] * label_size <= 65536
         and 2 * shortlist.shape[1] <= LANES
     )
+
+
+def after(value, first):
+    return lax.optimization_barrier((value, first))[0]
 
 
 def exchange(array):
@@ -509,124 +589,161 @@
     label_at = lax.axis_index("label")
     me = dp_at * label_size + label_at
 
-    payload, info = call(
-        functools.partial(pack_kernel, devs=devs, held=held),
-        (shape((devs, body + tail, LANES), BF), shape((rows, LANES), F32)),
-        (queries, shortlist, slab_slot[None, :], leaf_target[None, :]),
-        name="pack",
-    )
-    got = exchange(payload)
-    first_place = me * held
-    lane_at = first_place % LANES
-    place = jnp.stack(
-        [first_place // LANES] + [(r * held - lane_at) % LANES for r in range(CAPB)]
-    ).astype(jnp.int32)
-    rows_held, scores, codes, stats = call(
-        forward_kernel,
-        (
-            shape((held, CAPB * devs, width), BF),
-            shape((held, CAPB * devs, labels), F32),
-            shape((devs, LANES), F32),
-            shape((devs * SUB, LANES), F32),
-        ),
-        (place, got, leaf_weight, mid_weight),
-        scratch=(pltpu.VMEM((devs * body, LANES), F32), pltpu.VMEM((devs * tail, LANES), F32)),
-        scalars=1,
-        name="forward",
-    )
-    stats_back = exchange(stats.reshape(devs, SUB, LANES)).reshape(devs * SUB, LANES)
-    norms, pair_losses = call(
-        functools.partial(middle_kernel, devs=devs, held=held, short_len=short_len),
-        (shape((devs * SUB, LANES), F32), shape((SUB, rows), F32)),
-        (info, stats_back),
-        name="middle",
-    )
-    norms_held = exchange(norms.reshape(devs, SUB, LANES)).reshape(devs * SUB, LANES)
-    delta, mid_cols, back = call(
-        backward_kernel,
-        (
-            shape((held, CAPB * devs, labels), BF),
-            shape((devs, LANES), F32),
-            shape((devs, body, LANES), BF),
-        ),
-        (scores, codes, norms_held, leaf_weight, mid_weight),
-        scratch=(pltpu.VMEM((devs * body, LANES), F32),),
-        name="backward",
-    )
-    returned = exchange(back)
-    leaf_grad, mid_grad = call(
-        grads_kernel,
-        (shape((held, labels, width), F32), shape((held, width), F32)),
-        (delta, mid_cols, rows_held),
-        name="grads",
-    )
-
     steps = label_size // 2
     quarter = top_weight.shape[0] // dp_size
     held_top = top_weight.shape[0]
-    codes_top = jnp.zeros((16, width), BF)
-    codes_top = codes_top.at[0, :rows].set((top_target // 256).astype(BF))
-    codes_top = codes_top.at[1, :rows].set((top_target % 256).astype(BF))
-    own_quarter = lax.dynamic_slice_in_dim(top_weight, dp_at * quarter, quarter, 0)
-    sent = jnp.concatenate([queries, own_quarter, codes_top], axis=0)
-    sent, got = lax.optimization_barrier((sent, got))
+    flip_x = [(i, i ^ 1) for i in range(label_size)]
+    flip_y = [(i, i ^ 2) for i in range(dp_size)]
+    flip_core = [(i, i ^ 1) for i in range(dp_size)]
 
     def along(step):
         return [
             (z * 2 + x, ((z - step) % steps) * 2 + x) for z in range(steps) for x in range(2)
         ]
 
-    mine = jnp.stack([sent] + [lax.ppermute(sent, "label", along(n)) for n in range(1, steps)])
-    other = lax.ppermute(mine, "label", [(i, i ^ 1) for i in range(label_size)])
-    w_near = jnp.concatenate([mine[:, rows : rows + quarter], other[:, rows : rows + quarter]])
-    w_near = w_near.reshape(label_size * quarter, width)
-    w_y = lax.ppermute(w_near, "dp", [(i, i ^ 2) for i in range(dp_size)])
-    w_core = lax.ppermute(
-        jnp.concatenate([w_near, w_y]), "dp", [(i, i ^ 1) for i in range(dp_size)]
-    )
+    own_quarter = lax.dynamic_slice_in_dim(top_weight, dp_at * quarter, quarter, 0)
+    w_near = jnp.concatenate(
+        [own_quarter] + [lax.ppermute(own_quarter, "label", along(n)) for n in range(1, steps)]
+    )
+    me = me.astype(jnp.int32)[None]
+    label_base = (label_at * held_top).astype(jnp.int32)[None]
+    payload, info, own = call(
+        functools.partial(pack_kernel, devs=devs, held=held),
+        (
+            shape((devs, body + tail, LANES), BF),
+            shape((rows, LANES), F32),
+            shape((rows + 16, width), BF),
+        ),
+        (
+            after(queries, (me, label_base)),
+            shortlist.T,
+            slab_slot[None, :],
+            leaf_target[None, :],
+            top_target[None, :],
+        ),
+        name="pack",
+    )
+    payload = after(payload, w_near)
+    got = exchange(payload)
+    w_other = lax.ppermute(w_near, "label", flip_x)
+    w_y = lax.ppermute(jnp.concatenate([w_near, w_other]), "dp", flip_y)
     z_at, x_at = label_at // 2, label_at % 2
-    source = jnp.concatenate(
-        [((z_at + jnp.arange(steps)) % steps) * 2 + x_at, ((z_at + jnp.arange(steps)) % steps) * 2 + 1 - x_at]
-    )
+    source = (z_at + jnp.arange(steps)) % steps * 2
+    source = jnp.concatenate([source + x_at, source + 1 - x_at])
     dp_source = jnp.stack([dp_at, dp_at ^ 2, dp_at ^ 1, dp_at ^ 3])
     own_column = (
         source[None, :, None] * held_top
         + dp_source[:, None, None] * quarter
         + jnp.arange(quarter)[None, None, :]
     ).reshape(1, dp_size * label_size * quarter)
-    top_back, top_part, top_loss = call(
-        functools.partial(top_kernel, rows=rows, quarter=quarter),
-        (shape((rows, width), F32), shape((held_top, width), F32), shape((SUB, rows), F32)),
+    sent = after(own, got)
+    peers = [lax.ppermute(sent, "label", along(n)) for n in range(1, steps)]
+    pairs = CAPB * devs
+    rows_held, scores, stats = call(
+        forward_kernel,
         (
-            (label_at * held_top).astype(jnp.int32)[None],
-            mine,
-            other,
-            w_y,
-            w_core,
-            own_column.astype(F32),
-            top_weight,
+            shape((held, pairs, width), BF),
+            shape((held, pairs, labels), F32),
+            shape((devs * SUB, LANES), F32),
         ),
-        scratch=(pltpu.VMEM((label_size * held_top, width), BF),),
+        (me, got, leaf_weight, mid_weight),
+        scratch=(
+            pltpu.VMEM((devs * body, LANES), F32),
+            pltpu.VMEM((devs * tail, LANES), F32),
+            pltpu.VMEM((held, labels, width), BF),
+            pltpu.VMEM((held, pairs, width), BF),
+            pltpu.VMEM((held, pairs, labels), F32),
+            pltpu.SemaphoreType.DMA((2,)),
+            pltpu.SemaphoreType.DMA((2,)),
+            pltpu.SemaphoreType.DMA((2,)),
+        ),
         scalars=1,
-        name="top",
-    )
+        far_ins=(2,),
+        far_outs=(0, 1),
+        name="forward",
+    )
+    w_y = after(w_y, stats)
+    w_core = lax.ppermute(jnp.concatenate([w_near, w_other, w_y]), "dp", flip_core)
+    stats_back = exchange(stats.reshape(devs, SUB, LANES)).reshape(devs * SUB, LANES)
+    norms, pair_losses = call(
+        functools.partial(middle_kernel, devs=devs, held=held, short_len=short_len),
+        (shape((devs * SUB, LANES), F32), shape((SUB, rows), F32)),
+        (info, stats_back),
+        mib=16,
+        name="middle",
+    )
+    norms_held = exchange(norms.reshape(devs, SUB, LANES)).reshape(devs * SUB, LANES)
+    top_back, top_part, top_loss, top_all = call(
+        top_own_kernel,
+        (
+            shape((rows, width), F32),
+            shape((held_top, width), F32),
+            shape((SUB, rows), F32),
+            shape((label_size * held_top, width), BF),
+        ),
+        (label_base, own, after(w_near, norms), w_other, w_y, w_core, own_column.astype(F32), top_weight),
+        scalars=1,
+        name="top_own",
+    )
+    mine = jnp.stack([sent] + after(peers, top_part))
+    other = lax.ppermute(mine, "label", flip_x)
+    norms_held = after(norms_held, top_part)
+    delta, back = call(
+        backward_kernel,
+        (shape((held, pairs, labels), BF), shape((devs, body, LANES), BF)),
+        (scores, stats, norms_held, leaf_weight, mid_weight),
+        scratch=(
+            pltpu.VMEM((devs * body, LANES), F32),
+            pltpu.VMEM((held, pairs, labels), F32),
+            pltpu.VMEM((held, labels, width), BF),
+            pltpu.VMEM((devs, body, LANES), BF),
+            pltpu.SemaphoreType.DMA((2,)),
+            pltpu.SemaphoreType.DMA((2,)),
+            pltpu.SemaphoreType.DMA((devs // SUB,)),
+        ),
+        far_ins=(0, 3),
+        far_outs=(1,),
+        name="backward",
+    )
+    returned = exchange(back)
+    top_part = call(
+        functools.partial(top_more_kernel, first=1),
+        shape((held_top, width), F32),
+        (label_base, after(mine, back), top_all, top_weight, top_part),
+        scalars=1,
+        name="top_near",
+    )
+    top_part = call(
+        functools.partial(top_more_kernel, first=0),
+        shape((held_top, width), F32),
+        (label_base, after(other, back), top_all, top_weight, top_part),
+        scalars=1,
+        name="top_far",
+    )
+    losses = jnp.concatenate([top_loss[:1], pair_losses[:2]])
     core = dp_at % 2
     half = held_top // 2
-    both = top_part + lax.ppermute(top_part, "dp", [(i, i ^ 1) for i in range(dp_size)])
+    both = top_part + lax.ppermute(top_part, "dp", flip_core)
     share = lax.dynamic_slice_in_dim(both, core * half, half, 0)
-    share = share + lax.ppermute(share, "dp", [(i, i ^ 2) for i in range(dp_size)])
-    rest = lax.ppermute(share, "dp", [(i, i ^ 1) for i in range(dp_size)])
-    low = jnp.where(core == 0, share, rest)
-    high = jnp.where(core == 0, rest, share)
-    top_grad = jnp.concatenate([low, high])
-
+    from_y = lax.ppermute(share, "dp", flip_y)
+    leaf_grad, mid_grad = call(
+        grads_kernel,
+        (shape((held, labels, width), F32), shape((held, width), F32)),
+        (delta, norms_held, after(rows_held, (share, losses))),
+        name="grads",
+    )
+    share = share + after(from_y, mid_grad)
+    rest = lax.ppermute(share, "dp", flip_core)
+    top_grad = jnp.concatenate(
+        [jnp.where(core == 0, share, rest), jnp.where(core == 0, rest, share)]
+    )
     query_grad = call(
         functools.partial(finish_kernel, held=held, short_len=short_len),
         shape((rows, width), F32),
         (info, returned, top_back),
+        mib=16,
         name="finish",
     )
-    losses = jnp.concatenate([top_loss[:1], pair_losses[:2]])
     return (query_grad, top_grad, mid_grad, leaf_grad, losses)
 
 

time: 163 us -> 122 us (0.75)
  waiting for transfers between devices: 77.8 us -> 36.5 us
  blocking collectives: 14.5 us -> 0 us
  starting transfers between devices: 19.8 us -> 33.3 us
  local copies, waits for them, and re-layouts: 7.12 us -> 9.81 us
    all_to_all x3 -> x4, waiting for transfers between devices: 35.3 us -> 14.2 us  [exchange(): lax.all_to_all(array, ('dp', 'label'), split_axis=0, concat_axis=0, tiled...]
    ppermute x9 -> x13, waiting for transfers between devices: 42.5 us -> 22.2 us  [the longest x1 15.9 us: per_device(): w_other = lax.ppermute(w_near, 'label', flip_x)]
    all_to_all x1 -> x0, blocking collectives: 14.5 us -> none  [exchange(): lax.all_to_all(array, ('dp', 'label'), split_axis=0, concat_axis=0, tiled...]
    ppermute x9 -> x13, starting transfers between devices: 7.07 us -> 19.3 us  [the longest x3 6.99 us: per_device(): lax.ppermute(own_quarter, 'label', along(n))]
    unnamed x17 -> x30, local copies, waits for them, and re-layouts: 4.01 us -> 7.62 us
    all_to_all x3 -> x4, starting transfers between devices: 12.7 us -> 14 us  [exchange(): lax.all_to_all(array, ('dp', 'label'), split_axis=0, concat_axis=0, tiled...]
    pallas_call x7 -> x9, Pallas kernels: 37 us -> 37.7 us  [call(): pl.pallas_call(kernel, out_shape=outs, in_specs=[small if n < scalars els...]
  transfers between devices with their start and end apart: 12 -> 17, of which waited for: 7 -> 10; matrix products, arithmetic and copies ran while one was open for 4% -> 6% of each run, Pallas kernels for 21% -> 30%
where the time goes in v2:
time: 122 us; the launch traced here: 121 us
  Pallas kernels  37.7 us (31%)
  waiting for transfers between devices  36.5 us (30%)
  starting transfers between devices  33.3 us (27%)
  local copies, waits for them, and re-layouts  9.81 us (8%)
  other arithmetic  2.9 us (2%)
    pallas_call x9, Pallas kernels, call(): pl.pallas_call(kernel, out_shape=outs, in_specs=[small if n < scalars els...  37.7 us
    ppermute x1, waiting for transfers between devices, per_device(): w_other = lax.ppermute(w_near, 'label', flip_x)  15.9 us
    all_to_all x4, waiting for transfers between devices, exchange(): lax.all_to_all(array, ('dp', 'label'), split_axis=0, concat_axis=0, tiled...  14.2 us
    all_to_all x4, starting transfers between devices, exchange(): lax.all_to_all(array, ('dp', 'label'), split_axis=0, concat_axis=0, tiled...  14 us
    unnamed x30, local copies, waits for them, and re-layouts  7.62 us
    ppermute x3, starting transfers between devices, per_device(): lax.ppermute(own_quarter, 'label', along(n))  6.99 us
    ppermute x3, starting transfers between devices, per_device(): peers = [lax.ppermute(sent, 'label', along(n)) for n in range(1, steps)]  5.6 us
  transfers between devices with their start and end apart: 17, of which 10 were waited for; matrix products, arithmetic and copies ran while one was open for 6% of the time, Pallas kernels for 30%

profile of v2, /device:TPU:0, one launch (start us, length us, event | category | flops | bytes accessed | tf_op | source)
XLA Modules:
  0.0 121.0 jit_solution(18371357376174511737)
XLA Ops:
  0.6 1.5 %constant_dynamic-update-slice_fusion.10 = (bf16[1024,512]{1,0:T(8,128)(2,1)}, bf16[64,512]{1,0:T(8,128)(2,1)S(1)}) fusion(bf16[256,512]{1,0:T(8,128)(2,1)} %weight_ref.5, s32[]{:T(128)S(6)} %select_n.43), kind=kLoop, calls=%fused_computation.16 | loop fusion | bytes 196612
  2.1 3.1 %collective-permute-start.2 = (bf16[64,512]{1,0:T(8,128)(2,1)S(1)}, bf16[64,512]{1,0:T(8,128)(2,1)S(1)}, u32[]{:S(2)}, u32[]{:S(2)}) collective-permute-start(bf16[64,512]{1,0:T(8,128)(2,1)S(1)} %get-tuple-element.64), channel_id=1, source_target_pairs={{0,2},{1,3},{2,4},{3,5},{4,6},{5,7},{6,0},{7,1},{8,10},{9,11},{10,... | collective-permute-start | bytes 196616 | tf_op jit(solution)/shard_map/ppermute | solution.py:606
  5.2 2.6 %collective-permute-start.1 = (bf16[64,512]{1,0:T(8,128)(2,1)S(1)}, bf16[64,512]{1,0:T(8,128)(2,1)S(1)}, u32[]{:S(2)}, u32[]{:S(2)}) collective-permute-start(bf16[64,512]{1,0:T(8,128)(2,1)S(1)} %get-tuple-element.64), channel_id=1, source_target_pairs={{0,4},{1,5},{2,6},{3,7},{4,0},{5,1},{6,2},{7,3},{8,12},{9,13},{10,... | collective-permute-start | bytes 196616 | tf_op jit(solution)/shard_map/ppermute | solution.py:606
  7.8 1.3 %collective-permute-start = (bf16[64,512]{1,0:T(8,128)(2,1)S(1)}, bf16[64,512]{1,0:T(8,128)(2,1)S(1)}, u32[]{:S(2)}, u32[]{:S(2)}) collective-permute-start(bf16[64,512]{1,0:T(8,128)(2,1)S(1)} %get-tuple-element.64), channel_id=1, source_target_pairs={{0,6},{1,7},{2,0},{3,1},{4,2},{5,3},{6,4},{7,5},{8,14},{9,15},{10,... | collective-permute-start | bytes 196616 | tf_op jit(solution)/shard_map/ppermute | solution.py:606
  9.1 3.1 %pack.1 = (bf16[32,136,128]{2,1,0:T(8,128)(2,1)}, f32[128,128]{1,0:T(8,128)}, bf16[144,512]{1,0:T(8,128)(2,1)}) custom-call(bf16[128,512]{1,0:T(8,128)(2,1)} %q_ref, s32[4,128]{1,0:T(4,128)} %bitcast.26, s32[1,512]{1,0:T(1,128)} %bitcast.27, s32[1,128]{1,0:T(1,128)} %bitcast.28, s32[1,128]{1,0:T(1,128)} %bitcast.29), custom_call_target="tpu_custom_call" | custom-call | tf_op jit(solution)/shard_map/pack/pallas_call | solution.py:525
  12.5 5.2 %all-to-all-start = ((bf16[32,136,128]{2,1,0:T(8,128)(2,1)}), bf16[32,136,128]{2,1,0:T(8,128)(2,1)S(1)}, u32[]{:S(2)}, u32[]{:S(2)}) async-start(bf16[32,136,128]{2,1,0:T(8,128)(2,1)} %get-tuple-element.37), calls=%async_computation | async-start | bytes 2228224 | tf_op jit(solution)/shard_map/all_to_all | solution.py:567
  17.7 1.8 %collective-permute-start.3 = (bf16[256,512]{1,0:T(8,128)(2,1)S(1)}, bf16[256,512]{1,0:T(8,128)(2,1)S(1)}, u32[]{:S(2)}, u32[]{:S(2)}) collective-permute-start(bf16[256,512]{1,0:T(8,128)(2,1)S(1)} %pad_maximum_fusion.2.near_ref), channel_id=1, source_target_pairs={{0,1},{1,0},{2,3},{3,2},{4,5},{5,4},{6,7},{7,6},{8,9},{9,8},{10,11... | collective-permute-start | bytes 786440 | tf_op jit(solution)/shard_map/ppermute | solution.py:628
  21.5 15.9 %collective-permute-done.3.other_ref = bf16[256,512]{1,0:T(8,128)(2,1)S(1)} collective-permute-done((bf16[256,512]{1,0:T(8,128)(2,1)S(1)}, bf16[256,512]{1,0:T(8,128)(2,1)S(1)}, u32[]{:S(2)}, u32[]{:S(2)}) %collective-permute-start.3) | collective-permute-done | bytes 262176 | tf_op jit(solution)/shard_map/ppermute | solution.py:628
  38.2 1.5 %collective-permute-start.4 = (bf16[512,512]{1,0:T(8,128)(2,1)S(1)}, bf16[512,512]{1,0:T(8,128)(2,1)S(1)}, u32[]{:S(2)}, u32[]{:S(2)}) collective-permute-start(bf16[512,512]{1,0:T(8,128)(2,1)S(1)} %get-tuple-element.68), channel_id=1, source_target_pairs={{0,16},{8,24},{16,0},{24,8},{1,17},{9,25},{17,1},{25,9},{2,18},{10... | collective-permute-start | bytes 1572872 | tf_op jit(solution)/shard_map/ppermute | solution.py:629
  39.7 7.0 %all-to-all-done.got_ref = bf16[32,136,128]{2,1,0:T(8,128)(2,1)S(1)} async-done(((bf16[32,136,128]{2,1,0:T(8,128)(2,1)}), bf16[32,136,128]{2,1,0:T(8,128)(2,1)S(1)}, u32[]{:S(2)}, u32[]{:S(2)}) %all-to-all-start) | async-done | bytes 1114144 | tf_op jit(solution)/shard_map/all_to_all | solution.py:567
  47.6 6.3 %forward.1 = (bf16[16,64,512]{2,1,0:T(8,128)(2,1)}, f32[16,64,128]{2,1,0:T(8,128)}, f32[256,128]{1,0:T(8,128)}) custom-call(s32[1]{0:T(128)} %bitcast.me_ref, bf16[32,136,128]{2,1,0:T(8,128)(2,1)} %copy-done.2, bf16[16,128,512]{2,1,0:T(8,128)(2,1)} %leaf_in.3, bf16[16,512]{1,0:T(8,128)(2,1)} %mid_ref.3), custom_call_target="tpu_custom_call" | custom-call | tf_op jit(solution)/shard_map/forward/pallas_call | solution.py:525
  54.9 3.4 %all-to-all-start.1 = ((f32[32,8,128]{2,1,0:T(8,128)}), f32[32,8,128]{2,1,0:T(8,128)S(1)}, u32[]{:S(2)}, u32[]{:S(2)}) async-start(f32[32,8,128]{2,1,0:T(8,128)} %bitcast.22), calls=%async_computation.1 | async-start | bytes 262144 | tf_op jit(solution)/shard_map/all_to_all | solution.py:567
  58.4 1.8 %collective-permute-start.8 = (bf16[144,512]{1,0:T(8,128)(2,1)S(1)}, bf16[144,512]{1,0:T(8,128)(2,1)S(1)}, u32[]{:S(2)}, u32[]{:S(2)}) collective-permute-start(bf16[144,512]{1,0:T(8,128)(2,1)S(1)} %copy-done.9), channel_id=1, source_target_pairs={{0,2},{1,3},{2,4},{3,5},{4,6},{5,7},{6,0},{7,1},{8,10},{9,11},{10,... | collective-permute-start | bytes 442376 | tf_op jit(solution)/shard_map/ppermute | solution.py:640
  60.1 2.4 %collective-permute-start.7 = (bf16[144,512]{1,0:T(8,128)(2,1)S(1)}, bf16[144,512]{1,0:T(8,128)(2,1)S(1)}, u32[]{:S(2)}, u32[]{:S(2)}) collective-permute-start(bf16[144,512]{1,0:T(8,128)(2,1)S(1)} %copy-done.9), channel_id=1, source_target_pairs={{0,4},{1,5},{2,6},{3,7},{4,0},{5,1},{6,2},{7,3},{8,12},{9,13},{10,... | collective-permute-start | bytes 442376 | tf_op jit(solution)/shard_map/ppermute | solution.py:640
  62.6 1.4 %collective-permute-start.6 = (bf16[144,512]{1,0:T(8,128)(2,1)S(1)}, bf16[144,512]{1,0:T(8,128)(2,1)S(1)}, u32[]{:S(2)}, u32[]{:S(2)}) collective-permute-start(bf16[144,512]{1,0:T(8,128)(2,1)S(1)} %copy-done.9), channel_id=1, source_target_pairs={{0,6},{1,7},{2,0},{3,1},{4,2},{5,3},{6,4},{7,5},{8,14},{9,15},{10,... | collective-permute-start | bytes 442376 | tf_op jit(solution)/shard_map/ppermute | solution.py:640
  64.0 2.1 %all-to-all-done.1 = f32[32,8,128]{2,1,0:T(8,128)S(1)} async-done(((f32[32,8,128]{2,1,0:T(8,128)}), f32[32,8,128]{2,1,0:T(8,128)S(1)}, u32[]{:S(2)}, u32[]{:S(2)}) %all-to-all-start.1) | async-done | bytes 131104 | tf_op jit(solution)/shard_map/all_to_all | solution.py:567
  66.0 1.9 %middle.1 = (f32[256,128]{1,0:T(8,128)}, f32[8,128]{1,0:T(8,128)S(1)}) custom-call(f32[128,128]{1,0:T(8,128)S(1)} %copy-done.1, f32[256,128]{1,0:T(8,128)S(1)} %bitcast.18), custom_call_target="tpu_custom_call" | custom-call | tf_op jit(solution)/shard_map/middle/pallas_call | solution.py:525
  67.9 2.6 %all-to-all-start.2 = ((f32[32,8,128]{2,1,0:T(8,128)}), f32[32,8,128]{2,1,0:T(8,128)S(1)}, u32[]{:S(2)}, u32[]{:S(2)}) async-start(f32[32,8,128]{2,1,0:T(8,128)} %bitcast.8), calls=%async_computation.2 | async-start | bytes 262144 | tf_op jit(solution)/shard_map/all_to_all | solution.py:567
  72.2 4.1 %top_own.1 = (f32[128,512]{1,0:T(8,128)}, f32[256,512]{1,0:T(8,128)}, f32[8,128]{1,0:T(8,128)}, bf16[2048,512]{1,0:T(8,128)(2,1)}) custom-call(s32[1]{0:T(128)} %bitcast.1.where_ref, bf16[144,512]{1,0:T(8,128)(2,1)} %get-tuple-element.48.own_ref, bf16[256,512]{1,0:T(8,128)(2,1)} %copy-done.8, bf16[256,512]{1,0:T(8,128)(2,1)} %copy-done.7, ...), custom_call_target="tpu_custom_call" | custom-call | tf_op jit(solution)/shard_map/top_own/pallas_call | solution.py:525
  76.4 1.8 %collective-permute-start.9 = (bf16[4,144,512]{2,1,0:T(8,128)(2,1)S(1)}, bf16[4,144,512]{2,1,0:T(8,128)(2,1)S(1)}, u32[]{:S(2)}, u32[]{:S(2)}) collective-permute-start(bf16[4,144,512]{2,1,0:T(8,128)(2,1)S(1)} %pad_maximum_fusion.blocks_ref), channel_id=1, source_target_pairs={{0,1},{1,0},{2,3},{3,2},{4,5},{5,4},{6,7},{7,6},{8,9},{9,8},{10,11... | collective-permute-start | bytes 1769480 | tf_op jit(solution)/shard_map/ppermute | solution.py:689
  78.2 3.6 %all-to-all-done.2 = f32[32,8,128]{2,1,0:T(8,128)S(1)} async-done(((f32[32,8,128]{2,1,0:T(8,128)}), f32[32,8,128]{2,1,0:T(8,128)S(1)}, u32[]{:S(2)}, u32[]{:S(2)}) %all-to-all-start.2) | async-done | bytes 131104 | tf_op jit(solution)/shard_map/all_to_all | solution.py:567
  82.5 6.9 %backward.1 = (bf16[16,64,128]{2,1,0:T(8,128)(2,1)}, bf16[32,128,128]{2,1,0:T(8,128)(2,1)}) custom-call(f32[16,64,128]{2,1,0:T(8,128)} %get-tuple-element.38.score_in, f32[256,128]{1,0:T(8,128)} %get-tuple-element.39.stat_ref, f32[256,128]{1,0:T(8,128)} %bitcast.19, bf16[16,128,512]{2,1,0:T(8,128)(2,1)} %leaf_in.3, bf16[16,512]{1,0:T(8,128)(2,1)} %mid_ref.3), custom_call_target="tpu_custom_call" | custom-call | tf_op jit(solution)/shard_map/backward/pallas_call | solution.py:525
  89.4 2.8 %all-to-all-start.3 = ((bf16[32,128,128]{2,1,0:T(8,128)(2,1)}), bf16[32,128,128]{2,1,0:T(8,128)(2,1)S(1)}, u32[]{:S(2)}, u32[]{:S(2)}) async-start(bf16[32,128,128]{2,1,0:T(8,128)(2,1)} %get-tuple-element.46), calls=%async_computation.3 | async-start | bytes 2097152 | tf_op jit(solution)/shard_map/all_to_all | solution.py:567
  92.3 4.6 %top_near.1.part_ref = f32[256,512]{1,0:T(8,128)} custom-call(s32[1]{0:T(128)} %bitcast.1.where_ref, bf16[4,144,512]{2,1,0:T(8,128)(2,1)} %copy-done.3, bf16[2048,512]{1,0:T(8,128)(2,1)} %get-tuple-element.53.all_ref, bf16[256,512]{1,0:T(8,128)(2,1)} %weight_ref.5, f32[256,512]{1,0:T(8,128)} %get-tuple-element.44.part_ref), custom_call_target="tpu_custom_call" | custom-call | tf_op jit(solution)/shard_map/top_near/pallas_call | solution.py:525
  97.7 5.0 %top_far.1 = f32[256,512]{1,0:T(8,128)} custom-call(s32[1]{0:T(128)} %bitcast.1.where_ref, bf16[4,144,512]{2,1,0:T(8,128)(2,1)} %copy-done.11, bf16[2048,512]{1,0:T(8,128)(2,1)} %get-tuple-element.53.all_ref, bf16[256,512]{1,0:T(8,128)(2,1)} %weight_ref.5, f32[256,512]{1,0:T(8,128)} %top_near.1.part_ref), custom_call_target="tpu_custom_call" | custom-call | tf_op jit(solution)/shard_map/top_far/pallas_call | solution.py:525
  102.8 2.1 %collective-permute-done.10 = f32[256,512]{1,0:T(8,128)S(1)} collective-permute-done((f32[256,512]{1,0:T(8,128)}, f32[256,512]{1,0:T(8,128)S(1)}, u32[]{:S(2)}, u32[]{:S(2)}) %collective-permute-start.10) | collective-permute-done | bytes 524320 | tf_op jit(solution)/shard_map/ppermute | solution.py:726
  105.9 1.5 %collective-permute-start.11 = (f32[128,512]{1,0:T(8,128)S(1)}, f32[128,512]{1,0:T(8,128)S(1)}, u32[]{:S(2)}, u32[]{:S(2)}) collective-permute-start(f32[128,512]{1,0:T(8,128)S(1)} %dynamic-slice_add_fusion), channel_id=1, source_target_pairs={{0,16},{8,24},{16,0},{24,8},{1,17},{9,25},{17,1},{25,9},{2,18},{10... | collective-permute-start | bytes 786440 | tf_op jit(solution)/shard_map/ppermute | solution.py:728
  108.7 4.4 %grads.1 = (f32[16,128,512]{2,1,0:T(8,128)}, f32[16,512]{1,0:T(8,128)}) custom-call(bf16[16,64,128]{2,1,0:T(8,128)(2,1)} %get-tuple-element.55.delta_ref, f32[256,128]{1,0:T(8,128)} %bitcast.20, bf16[16,64,512]{2,1,0:T(8,128)(2,1)} %get-tuple-element.59.rows_ref), custom_call_target="tpu_custom_call" | custom-call | tf_op jit(solution)/shard_map/grads/pallas_call | solution.py:525
  113.0 2.4 %collective-permute-done.11 = f32[128,512]{1,0:T(8,128)S(1)} collective-permute-done((f32[128,512]{1,0:T(8,128)S(1)}, f32[128,512]{1,0:T(8,128)S(1)}, u32[]{:S(2)}, u32[]{:S(2)}) %collective-permute-start.11) | collective-permute-done | bytes 262176 | tf_op jit(solution)/shard_map/ppermute | solution.py:728
  115.5 1.5 %collective-permute-done.12 = f32[128,512]{1,0:T(8,128)S(1)} collective-permute-done((f32[128,512]{1,0:T(8,128)S(1)}, f32[128,512]{1,0:T(8,128)S(1)}, u32[]{:S(2)}, u32[]{:S(2)}) %collective-permute-start.12) | collective-permute-done | bytes 262176 | tf_op jit(solution)/shard_map/ppermute | solution.py:736
  117.9 1.6 %all-to-all-done.3.back_ref = bf16[32,128,128]{2,1,0:T(8,128)(2,1)S(1)} async-done(((bf16[32,128,128]{2,1,0:T(8,128)(2,1)}), bf16[32,128,128]{2,1,0:T(8,128)(2,1)S(1)}, u32[]{:S(2)}, u32[]{:S(2)}) %all-to-all-start.3) | async-done | bytes 1048608 | tf_op jit(solution)/shard_map/all_to_all | solution.py:567
  119.6 1.4 %finish.1 = f32[128,512]{1,0:T(8,128)} custom-call(f32[128,128]{1,0:T(8,128)S(1)} %copy-done.1, bf16[32,128,128]{2,1,0:T(8,128)(2,1)S(1)} %all-to-all-done.3.back_ref, f32[128,512]{1,0:T(8,128)S(1)} %copy-done), custom_call_target="tpu_custom_call" | custom-call | tf_op jit(solution)/shard_map/finish/pallas_call | solution.py:525
  (57 shorter events, 11.6 us)
Async XLA Ops:
  2.1 10.1 %collective-permute-start.2 = (bf16[64,512]{1,0:T(8,128)(2,1)S(1)}, bf16[64,512]{1,0:T(8,128)(2,1)S(1)}, u32[]{:S(2)}, u32[]{:S(2)}) collective-permute-start(bf16[64,512]{1,0:T(8,128)(2,1)S(1)} %get-tuple-element.64), channel_id=1, source_target_pairs={{0,2},{1,3},{2,4},{3,5},{4,6},{5,7},{6,0},{7,1},{8,10},{9,11},{10,... | collective-permute-start | bytes 196616 | tf_op jit(solution)/shard_map/ppermute | solution.py:606
  5.2 7.1 %collective-permute-start.1 = (bf16[64,512]{1,0:T(8,128)(2,1)S(1)}, bf16[64,512]{1,0:T(8,128)(2,1)S(1)}, u32[]{:S(2)}, u32[]{:S(2)}) collective-permute-start(bf16[64,512]{1,0:T(8,128)(2,1)S(1)} %get-tuple-element.64), channel_id=1, source_target_pairs={{0,4},{1,5},{2,6},{3,7},{4,0},{5,1},{6,2},{7,3},{8,12},{9,13},{10,... | collective-permute-start | bytes 196616 | tf_op jit(solution)/shard_map/ppermute | solution.py:606
  7.8 4.7 %collective-permute-start = (bf16[64,512]{1,0:T(8,128)(2,1)S(1)}, bf16[64,512]{1,0:T(8,128)(2,1)S(1)}, u32[]{:S(2)}, u32[]{:S(2)}) collective-permute-start(bf16[64,512]{1,0:T(8,128)(2,1)S(1)} %get-tuple-element.64), channel_id=1, source_target_pairs={{0,6},{1,7},{2,0},{3,1},{4,2},{5,3},{6,4},{7,5},{8,14},{9,15},{10,... | collective-permute-start | bytes 196616 | tf_op jit(solution)/shard_map/ppermute | solution.py:606
  12.5 41.4 %copy-start.8 = (bf16[256,512]{1,0:T(8,128)(2,1)}, bf16[256,512]{1,0:T(8,128)(2,1)S(1)}, u32[]{:S(2)}) copy-start(bf16[256,512]{1,0:T(8,128)(2,1)S(1)} %pad_maximum_fusion.2.near_ref) | copy-start | bytes 786436
  12.5 34.1 %all-to-all-start = ((bf16[32,136,128]{2,1,0:T(8,128)(2,1)}), bf16[32,136,128]{2,1,0:T(8,128)(2,1)S(1)}, u32[]{:S(2)}, u32[]{:S(2)}) async-start(bf16[32,136,128]{2,1,0:T(8,128)(2,1)} %get-tuple-element.37), calls=%async_computation | async-start | bytes 2228224 | tf_op jit(solution)/shard_map/all_to_all | solution.py:567
  17.7 19.6 %collective-permute-start.3 = (bf16[256,512]{1,0:T(8,128)(2,1)S(1)}, bf16[256,512]{1,0:T(8,128)(2,1)S(1)}, u32[]{:S(2)}, u32[]{:S(2)}) collective-permute-start(bf16[256,512]{1,0:T(8,128)(2,1)S(1)} %pad_maximum_fusion.2.near_ref), channel_id=1, source_target_pairs={{0,1},{1,0},{2,3},{3,2},{4,5},{5,4},{6,7},{7,6},{8,9},{9,8},{10,11... | collective-permute-start | bytes 786440 | tf_op jit(solution)/shard_map/ppermute | solution.py:628
  37.4 17.4 %copy-start.7 = (bf16[256,512]{1,0:T(8,128)(2,1)}, bf16[256,512]{1,0:T(8,128)(2,1)S(1)}, u32[]{:S(2)}) copy-start(bf16[256,512]{1,0:T(8,128)(2,1)S(1)} %collective-permute-done.3.other_ref) | copy-start | bytes 786436
  38.2 20.2 %copy-start.9 = (bf16[144,512]{1,0:T(8,128)(2,1)S(1)}, bf16[144,512]{1,0:T(8,128)(2,1)}, u32[]{:S(2)}) copy-start(bf16[144,512]{1,0:T(8,128)(2,1)} %get-tuple-element.48.own_ref) | copy-start | bytes 442372
  38.2 27.8 %copy-start.1 = (f32[128,128]{1,0:T(8,128)S(1)}, f32[128,128]{1,0:T(8,128)}, u32[]{:S(2)}) copy-start(f32[128,128]{1,0:T(8,128)} %get-tuple-element.35.info_ref) | copy-start | bytes 196612
  38.2 15.7 %collective-permute-start.4 = (bf16[512,512]{1,0:T(8,128)(2,1)S(1)}, bf16[512,512]{1,0:T(8,128)(2,1)S(1)}, u32[]{:S(2)}, u32[]{:S(2)}) collective-permute-start(bf16[512,512]{1,0:T(8,128)(2,1)S(1)} %get-tuple-element.68), channel_id=1, source_target_pairs={{0,16},{8,24},{16,0},{24,8},{1,17},{9,25},{17,1},{25,9},{2,18},{10... | collective-permute-start | bytes 1572872 | tf_op jit(solution)/shard_map/ppermute | solution.py:629
  46.6 1.0 copy-start.2
  53.9 17.3 %copy-start.4 = (bf16[512,512]{1,0:T(8,128)(2,1)}, bf16[512,512]{1,0:T(8,128)(2,1)S(1)}, u32[]{:S(2)}) copy-start(bf16[512,512]{1,0:T(8,128)(2,1)S(1)} %collective-permute-done.4.wy_ref) | copy-start | bytes 1572868
  53.9 22.4 %copy-start.10 = (bf16[144,512]{1,0:T(8,128)(2,1)S(1)}, bf16[144,512]{1,0:T(8,128)(2,1)}, u32[]{:S(2)}) copy-start(bf16[144,512]{1,0:T(8,128)(2,1)} %get-tuple-element.48.own_ref) | copy-start | bytes 442372
  54.8 16.5 %collective-permute-start.5 = (bf16[1024,512]{1,0:T(8,128)(2,1)}, bf16[1024,512]{1,0:T(8,128)(2,1)S(1)}, u32[]{:S(2)}, u32[]{:S(2)}) collective-permute-start(bf16[1024,512]{1,0:T(8,128)(2,1)} %constant_dynamic-update-slice_fusion.5), channel_id=1, source_target_pairs={{0,8},{8,0},{16,24},{24,16},{1,9},{9,1},{17,25},{25,17},{2,10},{10... | collective-permute-start | bytes 3145736 | tf_op jit(solution)/shard_map/ppermute | solution.py:666
  54.9 11.2 %all-to-all-start.1 = ((f32[32,8,128]{2,1,0:T(8,128)}), f32[32,8,128]{2,1,0:T(8,128)S(1)}, u32[]{:S(2)}, u32[]{:S(2)}) async-start(f32[32,8,128]{2,1,0:T(8,128)} %bitcast.22), calls=%async_computation.1 | async-start | bytes 262144 | tf_op jit(solution)/shard_map/all_to_all | solution.py:567
  58.4 17.9 %collective-permute-start.8 = (bf16[144,512]{1,0:T(8,128)(2,1)S(1)}, bf16[144,512]{1,0:T(8,128)(2,1)S(1)}, u32[]{:S(2)}, u32[]{:S(2)}) collective-permute-start(bf16[144,512]{1,0:T(8,128)(2,1)S(1)} %copy-done.9), channel_id=1, source_target_pairs={{0,2},{1,3},{2,4},{3,5},{4,6},{5,7},{6,0},{7,1},{8,10},{9,11},{10,... | collective-permute-start | bytes 442376 | tf_op jit(solution)/shard_map/ppermute | solution.py:640
  60.1 16.2 %collective-permute-start.7 = (bf16[144,512]{1,0:T(8,128)(2,1)S(1)}, bf16[144,512]{1,0:T(8,128)(2,1)S(1)}, u32[]{:S(2)}, u32[]{:S(2)}) collective-permute-start(bf16[144,512]{1,0:T(8,128)(2,1)S(1)} %copy-done.9), channel_id=1, source_target_pairs={{0,4},{1,5},{2,6},{3,7},{4,0},{5,1},{6,2},{7,3},{8,12},{9,13},{10,... | collective-permute-start | bytes 442376 | tf_op jit(solution)/shard_map/ppermute | solution.py:640
  62.6 13.8 %collective-permute-start.6 = (bf16[144,512]{1,0:T(8,128)(2,1)S(1)}, bf16[144,512]{1,0:T(8,128)(2,1)S(1)}, u32[]{:S(2)}, u32[]{:S(2)}) collective-permute-start(bf16[144,512]{1,0:T(8,128)(2,1)S(1)} %copy-done.9), channel_id=1, source_target_pairs={{0,6},{1,7},{2,0},{3,1},{4,2},{5,3},{6,4},{7,5},{8,14},{9,15},{10,... | collective-permute-start | bytes 442376 | tf_op jit(solution)/shard_map/ppermute | solution.py:640
  67.9 13.9 %all-to-all-start.2 = ((f32[32,8,128]{2,1,0:T(8,128)}), f32[32,8,128]{2,1,0:T(8,128)S(1)}, u32[]{:S(2)}, u32[]{:S(2)}) async-start(f32[32,8,128]{2,1,0:T(8,128)} %bitcast.8), calls=%async_computation.2 | async-start | bytes 262144 | tf_op jit(solution)/shard_map/all_to_all | solution.py:567
  71.2 1.0 copy-start.6
  76.4 13.0 %copy-start.3 = (bf16[4,144,512]{2,1,0:T(8,128)(2,1)}, bf16[4,144,512]{2,1,0:T(8,128)(2,1)S(1)}, u32[]{:S(2)}) copy-start(bf16[4,144,512]{2,1,0:T(8,128)(2,1)S(1)} %pad_maximum_fusion.blocks_ref) | copy-start | bytes 1769476
  76.4 20.5 %collective-permute-start.9 = (bf16[4,144,512]{2,1,0:T(8,128)(2,1)S(1)}, bf16[4,144,512]{2,1,0:T(8,128)(2,1)S(1)}, u32[]{:S(2)}, u32[]{:S(2)}) collective-permute-start(bf16[4,144,512]{2,1,0:T(8,128)(2,1)S(1)} %pad_maximum_fusion.blocks_ref), channel_id=1, source_target_pairs={{0,1},{1,0},{2,3},{3,2},{4,5},{5,4},{6,7},{7,6},{8,9},{9,8},{10,11... | collective-permute-start | bytes 1769480 | tf_op jit(solution)/shard_map/ppermute | solution.py:689
  81.8 0.6 copy-start.5
  89.4 30.1 %all-to-all-start.3 = ((bf16[32,128,128]{2,1,0:T(8,128)(2,1)}), bf16[32,128,128]{2,1,0:T(8,128)(2,1)S(1)}, u32[]{:S(2)}, u32[]{:S(2)}) async-start(bf16[32,128,128]{2,1,0:T(8,128)(2,1)} %get-tuple-element.46), calls=%async_computation.3 | async-start | bytes 2097152 | tf_op jit(solution)/shard_map/all_to_all | solution.py:567
  96.9 0.8 copy-start.11
  102.8 2.1 %collective-permute-start.10 = (f32[256,512]{1,0:T(8,128)}, f32[256,512]{1,0:T(8,128)S(1)}, u32[]{:S(2)}, u32[]{:S(2)}) collective-permute-start(f32[256,512]{1,0:T(8,128)} %top_far.1), channel_id=1, source_target_pairs={{0,8},{8,0},{16,24},{24,16},{1,9},{9,1},{17,25},{25,17},{2,10},{10... | collective-permute-start | bytes 1572872 | tf_op jit(solution)/shard_map/ppermute | solution.py:726
  105.9 9.5 %collective-permute-start.11 = (f32[128,512]{1,0:T(8,128)S(1)}, f32[128,512]{1,0:T(8,128)S(1)}, u32[]{:S(2)}, u32[]{:S(2)}) collective-permute-start(f32[128,512]{1,0:T(8,128)S(1)} %dynamic-slice_add_fusion), channel_id=1, source_target_pairs={{0,16},{8,24},{16,0},{24,8},{1,17},{9,25},{17,1},{25,9},{2,18},{10... | collective-permute-start | bytes 786440 | tf_op jit(solution)/shard_map/ppermute | solution.py:728
  108.7 10.9 %copy-start = (f32[128,512]{1,0:T(8,128)S(1)}, f32[128,512]{1,0:T(8,128)}, u32[]{:S(2)}) copy-start(f32[128,512]{1,0:T(8,128)} %get-tuple-element.47.top_ref) | copy-start | bytes 786436
  115.5 1.6 %collective-permute-start.12 = (f32[128,512]{1,0:T(8,128)S(1)}, f32[128,512]{1,0:T(8,128)S(1)}, u32[]{:S(2)}, u32[]{:S(2)}) collective-permute-start(f32[128,512]{1,0:T(8,128)S(1)} %add.114), channel_id=1, source_target_pairs={{0,8},{8,0},{16,24},{24,16},{1,9},{9,1},{17,25},{25,17},{2,10},{10... | collective-permute-start | bytes 786440 | tf_op jit(solution)/shard_map/ppermute | solution.py:736

commit v3 on v2

--- a/solution.py
+++ b/solution.py
@@ -6,6 +6,7 @@
 from jax.experimental import pallas as pl
 from jax.experimental.pallas import tpu as pltpu
 from jax.sharding import PartitionSpec as P
+
 
 D = 512
 BLOCKS = 512
@@ -215,9 +216,9 @@
     info_ref[...] = info
     queries = q_ref[...]
     own_ref[:rows, :] = queries
-    top_target = jnp.broadcast_to(top_t_ref[...].astype(F32), (16, rows))
+    top_target = jnp.broadcast_to(top_t_ref[...].astype(F32), (SUB, rows))
     high = jnp.floor(top_target * (1.0 / 256.0))
-    code_at = iota((16, rows), 0)
+    code_at = iota((SUB, rows), 0)
     coded = jnp.where(code_at == 0, high, jnp.where(code_at == 1, top_target - 256.0 * high, 0.0))
     own_ref[rows:, :] = jnp.concatenate([coded] * chunks, axis=1).astype(BF)
     target = jnp.broadcast_to(leaf_t_ref[...].astype(F32) + 1.0, (SUB, rows)).astype(BF)
@@ -260,7 +261,7 @@
 
 
 def forward_kernel(
-    me_ref, got_ref, leaf_in, mid_ref, rows_out, score_out, stat_ref,
+    me_ref, got_ref, leaf_in, mid_ref, rows_out, score_out, stat_ref, code_ref,
     wide_ref, table_ref, leaf_ref, rows_ref, score_ref, leaf_sem, rows_sem, score_sem,
 ):
     devs, depth, _ = got_ref.shape
@@ -282,7 +283,7 @@
         row = table_ref[pl.ds(r * (tail // CAPB) + row_at, devs, stride=tail), :]
         row = pltpu.roll(row, lax.rem(r * held - lane_at + LANES, LANES), 1)
         codes = jnp.where((lane >= r * held) & (lane < (r + 1) * held), row, codes)
-    stat_ref[pl.ds(1, devs, stride=SUB), :] = codes
+    code_ref[...] = codes
     label_f = iota_f((CAPB * devs, labels), 1)
     stats = jnp.zeros((devs, LANES), F32)
     for k in range(held):
@@ -318,7 +319,7 @@
                 )
         if (k + 1) % (held // 2) == 0:
             start(sends[k // (held // 2)])
-    stat_ref[pl.ds(0, devs, stride=SUB), :] = stats
+    stat_ref[...] = stats.reshape(stat_ref.shape)
     for pair in sends:
         for send in pair:
             send.wait()
@@ -328,7 +329,7 @@
     rows = info_ref.shape[0]
     slots = CAPB * held
     info = info_ref[...]
-    stats = stat_ref[pl.ds(0, devs, stride=SUB), :]
+    stats = stat_ref[...].reshape(devs, LANES)
     lane = iota_f((rows, LANES), 1)
     dev_f = iota_f((rows, devs), 1)
     owners, spots, mids, lses = [], [], [], []
@@ -364,25 +365,22 @@
             )
         )
     sent = dot_tn(jnp.concatenate(owners, axis=0), jnp.concatenate(back, axis=0), HIGH)
-    out_ref[pl.ds(0, devs, stride=SUB), :] = sent
+    out_ref[...] = sent.reshape(out_ref.shape)
     losses = jnp.where(lane == 0.0, mid_total - mids[0], jnp.where(lane == 1.0, leaf_total - target, 0.0))
     loss_ref[...] = losses.T[:SUB, :]
 
 
 def backward_kernel(
-    score_in, stat_ref, norm_ref, leaf_in, mid_ref, delta_ref, pay_out,
-    wide_ref, score_ref, leaf_ref, pay_ref, score_sem, leaf_sem, pay_sem,
+    score_ref, code_ref, norm_ref, leaf_ref, mid_ref, delta_ref, pay_ref, wide_ref
 ):
     held, pairs, labels = score_ref.shape
-    fetches = start(halves(score_in, score_ref, score_sem))
-    leaf_fetches = start(halves(leaf_in, leaf_ref, leaf_sem))
     devs = pairs // CAPB
     width = leaf_ref.shape[2]
     chunks = width // LANES
     slots = CAPB * held
     body = chunks * slots
-    norms = norm_ref[pl.ds(0, devs, stride=SUB), :]
-    codes = stat_ref[pl.ds(1, devs, stride=SUB), :]
+    norms = norm_ref[...].reshape(devs, LANES)
+    codes = code_ref[...]
     label_f = iota_f((pairs, labels), 1)
 
     def column(array, base, k):
@@ -395,9 +393,6 @@
         lse = column(norms, 0, k)
         mid_delta = column(norms, slots, k)
         onehot = jnp.where(code - 2.0 == label_f, 1.0, 0.0)
-        if k % (held // 2) == 0:
-            fetches[k // (held // 2)].wait()
-            leaf_fetches[k // (held // 2)].wait()
         delta = jnp.where(code > 0.5, jnp.exp(score_ref[k] - lse) - onehot, 0.0).astype(BF)
         delta_ref[k] = delta
         back = dot_nn(delta, leaf_ref[k]) + mid_delta * mid_ref[k : k + 1, :].astype(F32)
@@ -406,26 +401,14 @@
                 wide_ref[pl.ds(c * slots + r * held + k, devs, stride=body), :] = back[
                     r * devs : (r + 1) * devs, c * LANES : (c + 1) * LANES
                 ]
-    sends = []
-    for g in range(0, devs, SUB):
-        pay_ref[g : g + SUB] = (
-            wide_ref[g * body : (g + SUB) * body, :].astype(BF).reshape(SUB, body, LANES)
-        )
-        sends.append(
-            pltpu.make_async_copy(
-                pay_ref.at[pl.ds(g, SUB)], pay_out.at[pl.ds(g, SUB)], pay_sem.at[g // SUB]
-            )
-        )
-        sends[-1].start()
-    for send in sends:
-        send.wait()
+    pay_ref[...] = wide_ref[...].astype(BF).reshape(devs, body, LANES)
 
 
 def grads_kernel(delta_ref, norm_ref, rows_ref, leaf_grad_ref, mid_grad_ref):
     held, pairs, _ = delta_ref.shape
     devs = pairs // CAPB
     slots = CAPB * held
-    norms = norm_ref[pl.ds(0, devs, stride=SUB), :]
+    norms = norm_ref[...].reshape(devs, LANES)
     for k in range(held):
         rows = rows_ref[k]
         leaf_grad_ref[k] = dot_tn(delta_ref[k], rows)
@@ -462,8 +445,8 @@
         out_ref[:, c * LANES : (c + 1) * LANES] = total
 
 
-def top_step(block, target, weights, weight_held, held_base):
-    scores = dot_nt(block, weights)
+def top_step(block, target, pieces, weight_held, held_base):
+    scores = jnp.concatenate([dot_nt(block, ref[...]) for ref in pieces], axis=1)
     peak = jnp.max(scores, axis=1, keepdims=True)
     total = peak + jnp.log(jnp.sum(jnp.exp(scores - peak), axis=1, keepdims=True))
     mine = dot_nt(block, weight_held)
@@ -478,36 +461,40 @@
 
 
 def top_own_kernel(
-    where_ref, own_ref, near_ref, other_ref, wy_ref, wc_ref, column_ref, weight_ref,
-    back_ref, part_ref, loss_ref, all_ref,
+    where_ref, own_ref, near_ref, y_ref, core_ref, far_ref, column_ref, weight_ref,
+    back_ref, part_ref, loss_ref,
 ):
-    rows = own_ref.shape[0] - 16
+    rows = own_ref.shape[0] - SUB
     piece = near_ref.shape[0]
-    all_ref[:piece, :] = near_ref[...]
-    all_ref[piece : 2 * piece, :] = other_ref[...]
-    all_ref[2 * piece : 4 * piece, :] = wy_ref[...]
-    all_ref[4 * piece :, :] = wc_ref[...]
+    pieces = (near_ref, y_ref, core_ref, far_ref)
     block = own_ref[:rows, :]
     target = top_column(own_ref[rows:, :])
     scores, total, part = top_step(
-        block, target, all_ref[...], weight_ref[...], where_ref[0].astype(F32)
+        block, target, pieces, weight_ref[...], where_ref[0].astype(F32)
     )
     part_ref[...] = part
     hit = jnp.broadcast_to(column_ref[...], scores.shape) == target
     full = (jnp.exp(scores - total) - jnp.where(hit, 1.0, 0.0)).astype(BF)
-    back_ref[...] = dot_nn(full, all_ref[...])
+    back = dot_nn(full[:, :piece], pieces[0][...])
+    for n in range(1, len(pieces)):
+        back = back + dot_nn(full[:, n * piece : (n + 1) * piece], pieces[n][...])
+    back_ref[...] = back
     loss = total - jnp.sum(jnp.where(hit, scores, 0.0), axis=1, keepdims=True)
     loss_ref[...] = jnp.broadcast_to(loss, (rows, LANES)).T[:SUB, :]
 
 
-def top_more_kernel(where_ref, blocks_ref, all_ref, weight_ref, part_ref, out_ref, *, first):
+def top_more_kernel(
+    where_ref, blocks_ref, near_ref, y_ref, core_ref, far_ref, weight_ref, part_ref, out_ref,
+    *, first,
+):
     count, depth, _ = blocks_ref.shape
-    rows = depth - 16
+    rows = depth - SUB
     numbers = range(first, count)
     block = jnp.concatenate([blocks_ref[n, :rows, :] for n in numbers], axis=0)
     target = jnp.concatenate([top_column(blocks_ref[n, rows:, :]) for n in numbers], axis=0)
     base = where_ref[0].astype(F32)
-    part = top_step(block, target, all_ref[...], weight_ref[...], base)[2]
+    pieces = (near_ref, y_ref, core_ref, far_ref)
+    part = top_step(block, target, pieces, weight_ref[...], base)[2]
     out_ref[...] = part_ref[...] + part
 
 
@@ -515,7 +502,7 @@
     return pl.BlockSpec(memory_space=pltpu.VMEM)
 
 
-def call(kernel, outs, ins, scratch=(), scalars=0, far_ins=(), far_outs=(), mib=58, name=None):
+def call(kernel, outs, ins, scratch=(), scalars=0, far_ins=(), far_outs=(), mib=58):
     far = pl.BlockSpec(memory_space=pltpu.HBM)
     small = pl.BlockSpec(memory_space=pltpu.SMEM)
     listed = isinstance(outs, tuple)
@@ -531,7 +518,6 @@
         out_specs=out_specs if listed else out_specs[0],
         scratch_shapes=list(scratch),
         compiler_params=params(mib),
-        name=name,
     )(*ins)
 
 
@@ -552,8 +538,8 @@
         and CAPB * (devs * held // LANES) % SUB == 0
         and devs % SUB == 0
         and dp_size == 4
-        and label_size == 8
-        and top_weight.shape[0] % (dp_size * 16) == 0
+        and label_size == 2 * dp_size
+        and top_weight.shape[0] % 32 == 0
         and top_weight.shape[0] * label_size <= 65536
         and 2 * shortlist.shape[1] <= LANES
     )
@@ -590,7 +576,6 @@
     me = dp_at * label_size + label_at
 
     steps = label_size // 2
-    quarter = top_weight.shape[0] // dp_size
     held_top = top_weight.shape[0]
     flip_x = [(i, i ^ 1) for i in range(label_size)]
     flip_y = [(i, i ^ 2) for i in range(dp_size)]
@@ -601,10 +586,13 @@
             (z * 2 + x, ((z - step) % steps) * 2 + x) for z in range(steps) for x in range(2)
         ]
 
-    own_quarter = lax.dynamic_slice_in_dim(top_weight, dp_at * quarter, quarter, 0)
-    w_near = jnp.concatenate(
-        [own_quarter] + [lax.ppermute(own_quarter, "label", along(n)) for n in range(1, steps)]
-    )
+    shift_z = [
+        (d * label_size + z * 2 + x, d * label_size + (z + d + 1) % steps * 2 + x)
+        for d in range(dp_size)
+        for z in range(steps)
+        for x in range(2)
+    ]
+    w_near = lax.ppermute(top_weight, ("dp", "label"), shift_z)
     me = me.astype(jnp.int32)[None]
     label_base = (label_at * held_top).astype(jnp.int32)[None]
     payload, info, own = call(
@@ -612,7 +600,7 @@
         (
             shape((devs, body + tail, LANES), BF),
             shape((rows, LANES), F32),
-            shape((rows + 16, width), BF),
+            shape((rows + SUB, width), BF),
         ),
         (
             after(queries, (me, label_base)),
@@ -621,30 +609,29 @@
             leaf_target[None, :],
             top_target[None, :],
         ),
-        name="pack",
-    )
-    payload = after(payload, w_near)
+    )
     got = exchange(payload)
     w_other = lax.ppermute(w_near, "label", flip_x)
-    w_y = lax.ppermute(jnp.concatenate([w_near, w_other]), "dp", flip_y)
+    w_own = jnp.concatenate([w_near, w_other])
+    w_y = lax.ppermute(w_own, "dp", flip_y)
+    w_core = lax.ppermute(w_own, "dp", flip_core)
     z_at, x_at = label_at // 2, label_at % 2
-    source = (z_at + jnp.arange(steps)) % steps * 2
-    source = jnp.concatenate([source + x_at, source + 1 - x_at])
     dp_source = jnp.stack([dp_at, dp_at ^ 2, dp_at ^ 1, dp_at ^ 3])
-    own_column = (
-        source[None, :, None] * held_top
-        + dp_source[:, None, None] * quarter
-        + jnp.arange(quarter)[None, None, :]
-    ).reshape(1, dp_size * label_size * quarter)
-    sent = after(own, got)
+    source = (z_at - dp_source - 1) % steps * 2
+    source = jnp.stack([source + x_at, source + 1 - x_at], axis=1)
+    own_column = (source[:, :, None] * held_top + jnp.arange(held_top)).reshape(
+        1, label_size * held_top
+    )
+    sent = after(own, w_near)
     peers = [lax.ppermute(sent, "label", along(n)) for n in range(1, steps)]
     pairs = CAPB * devs
-    rows_held, scores, stats = call(
+    rows_held, scores, stats, codes = call(
         forward_kernel,
         (
             shape((held, pairs, width), BF),
             shape((held, pairs, labels), F32),
-            shape((devs * SUB, LANES), F32),
+            shape((devs, 1, LANES), F32),
+            shape((devs, LANES), F32),
         ),
         (me, got, leaf_weight, mid_weight),
         scratch=(
@@ -660,30 +647,26 @@
         scalars=1,
         far_ins=(2,),
         far_outs=(0, 1),
-        name="forward",
     )
     w_y = after(w_y, stats)
-    w_core = lax.ppermute(jnp.concatenate([w_near, w_other, w_y]), "dp", flip_core)
-    stats_back = exchange(stats.reshape(devs, SUB, LANES)).reshape(devs * SUB, LANES)
+    w_far = lax.ppermute(w_y, "dp", flip_core)
+    stats_back = exchange(stats)
     norms, pair_losses = call(
         functools.partial(middle_kernel, devs=devs, held=held, short_len=short_len),
-        (shape((devs * SUB, LANES), F32), shape((SUB, rows), F32)),
+        (shape((devs, 1, LANES), F32), shape((SUB, rows), F32)),
         (info, stats_back),
         mib=16,
-        name="middle",
-    )
-    norms_held = exchange(norms.reshape(devs, SUB, LANES)).reshape(devs * SUB, LANES)
-    top_back, top_part, top_loss, top_all = call(
+    )
+    norms_held = exchange(norms)
+    top_back, top_part, top_loss = call(
         top_own_kernel,
         (
             shape((rows, width), F32),
             shape((held_top, width), F32),
             shape((SUB, rows), F32),
-            shape((label_size * held_top, width), BF),
         ),
-        (label_base, own, after(w_near, norms), w_other, w_y, w_core, own_column.astype(F32), top_weight),
+        (label_base, own, after(w_own, norms), w_y, w_core, w_far, own_column.astype(F32), top_weight),
         scalars=1,
-        name="top_own",
     )
     mine = jnp.stack([sent] + after(peers, top_part))
     other = lax.ppermute(mine, "label", flip_x)
@@ -691,34 +674,22 @@
     delta, back = call(
         backward_kernel,
         (shape((held, pairs, labels), BF), shape((devs, body, LANES), BF)),
-        (scores, stats, norms_held, leaf_weight, mid_weight),
-        scratch=(
-            pltpu.VMEM((devs * body, LANES), F32),
-            pltpu.VMEM((held, pairs, labels), F32),
-            pltpu.VMEM((held, labels, width), BF),
-            pltpu.VMEM((devs, body, LANES), BF),
-            pltpu.SemaphoreType.DMA((2,)),
-            pltpu.SemaphoreType.DMA((2,)),
-            pltpu.SemaphoreType.DMA((devs // SUB,)),
-        ),
-        far_ins=(0, 3),
-        far_outs=(1,),
-        name="backward",
+        (scores, codes, norms_held, leaf_weight, mid_weight),
+        scratch=(pltpu.VMEM((devs * body, LANES), F32),),
+        mib=24,
     )
     returned = exchange(back)
     top_part = call(
         functools.partial(top_more_kernel, first=1),
         shape((held_top, width), F32),
-        (label_base, after(mine, back), top_all, top_weight, top_part),
+        (label_base, after(mine, back), w_own, w_y, w_core, w_far, top_weight, top_part),
         scalars=1,
-        name="top_near",
     )
     top_part = call(
         functools.partial(top_more_kernel, first=0),
         shape((held_top, width), F32),
-        (label_base, after(other, back), top_all, top_weight, top_part),
+        (label_base, after(other, back), w_own, w_y, w_core, w_far, top_weight, top_part),
         scalars=1,
-        name="top_far",
     )
     losses = jnp.concatenate([top_loss[:1], pair_losses[:2]])
     core = dp_at % 2
@@ -730,7 +701,6 @@
         grads_kernel,
         (shape((held, labels, width), F32), shape((held, width), F32)),
         (delta, norms_held, after(rows_held, (share, losses))),
-        name="grads",
     )
     share = share + after(from_y, mid_grad)
     rest = lax.ppermute(share, "dp", flip_core)
@@ -742,7 +712,6 @@
         shape((rows, width), F32),
         (info, returned, top_back),
         mib=16,
-        name="finish",
     )
     return (query_grad, top_grad, mid_grad, leaf_grad, losses)
 

time: 122 us -> 142 us (1.16)
  blocking collectives: 0 us -> 14.8 us
  waiting for transfers between devices: 36.5 us -> 46 us
  local copies, waits for them, and re-layouts: 9.81 us -> 3.18 us
  starting transfers between devices: 33.3 us -> 38.3 us
  Pallas kernels: 37.7 us -> 33.9 us
    ppermute x5 -> x4, waiting for transfers between devices: 0.3 us -> 24.4 us  [the longest x1 24.4 us: per_device(): w_near = lax.ppermute(top_weight, ('dp', 'label'), shift_z)]
    all_to_all x0 -> x1, blocking collectives: none -> 14.8 us  [exchange(): lax.all_to_all(array, ('dp', 'label'), split_axis=0, concat_axis=0, tiled...]
    ppermute x1, waiting for transfers between devices: 15.9 us -> 5.61 us  [per_device(): w_other = lax.ppermute(w_near, 'label', flip_x)]
    unnamed x30 -> x27, local copies, waits for them, and re-layouts: 7.62 us -> 1.76 us
    all_to_all x4 -> x3, waiting for transfers between devices: 14.2 us -> 9.74 us  [exchange(): lax.all_to_all(array, ('dp', 'label'), split_axis=0, concat_axis=0, tiled...]
    pallas_call x9, Pallas kernels: 37.7 us -> 33.9 us  [call(): pl.pallas_call(kernel, out_shape=outs, in_specs=[small if n < scalars els...]
    ppermute x3, starting transfers between devices: 5.6 us -> 9.13 us  [per_device(): peers = [lax.ppermute(sent, 'label', along(n)) for n in range(1, steps)]]
    ppermute x5 -> x4, starting transfers between devices: 8.46 us -> 11.1 us  [the longest x1 6.2 us: per_device(): w_core = lax.ppermute(w_own, 'dp', flip_core)]
  transfers between devices with their start and end apart: 17 -> 15, of which waited for: 10 -> 7; matrix products, arithmetic and copies ran while one was open for 6% -> 3% of each run, Pallas kernels for 30% -> 21%
where the time goes in v3:
time: 142 us; the launch traced here: 141 us
  waiting for transfers between devices  46 us (32%)
  starting transfers between devices  38.3 us (27%)
  Pallas kernels  33.9 us (24%)
  blocking collectives  14.8 us (10%)
  other arithmetic  3.78 us (3%)
  local copies, waits for them, and re-layouts  3.18 us (2%)
    pallas_call x9, Pallas kernels, call(): pl.pallas_call(kernel, out_shape=outs, in_specs=[small if n < scalars els...  33.9 us
    ppermute x1, waiting for transfers between devices, per_device(): w_near = lax.ppermute(top_weight, ('dp', 'label'), shift_z)  24.4 us
    all_to_all x1, blocking collectives, exchange(): lax.all_to_all(array, ('dp', 'label'), split_axis=0, concat_axis=0, tiled...  14.8 us
    all_to_all x3, starting transfers between devices, exchange(): lax.all_to_all(array, ('dp', 'label'), split_axis=0, concat_axis=0, tiled...  14.1 us
    all_to_all x3, waiting for transfers between devices, exchange(): lax.all_to_all(array, ('dp', 'label'), split_axis=0, concat_axis=0, tiled...  9.74 us
    ppermute x3, starting transfers between devices, per_device(): peers = [lax.ppermute(sent, 'label', along(n)) for n in range(1, steps)]  9.13 us
    ppermute x1, starting transfers between devices, per_device(): w_core = lax.ppermute(w_own, 'dp', flip_core)  6.2 us
    ppermute x1, waiting for transfers between devices, per_device(): w_other = lax.ppermute(w_near, 'label', flip_x)  5.61 us
  transfers between devices with their start and end apart: 15, of which 7 were waited for; matrix products, arithmetic and copies ran while one was open for 3% of the time, Pallas kernels for 21%

profile of v3, /device:TPU:0, one launch (start us, length us, event | category | flops | bytes accessed | tf_op | source)
XLA Modules:
  0.0 140.9 jit_solution(13691686311720205589)
XLA Ops:
  0.7 3.1 %shard_map.119 = (bf16[32,136,128]{2,1,0:T(8,128)(2,1)}, f32[128,128]{1,0:T(8,128)}, bf16[136,512]{1,0:T(8,128)(2,1)}) custom-call(bf16[128,512]{1,0:T(8,128)(2,1)} %q_ref, s32[4,128]{1,0:T(4,128)} %bitcast.15, s32[1,512]{1,0:T(1,128)} %bitcast.16, s32[1,128]{1,0:T(1,128)} %bitcast.17, s32[1,128]{1,0:T(1,128)} %bitcast.18), custom_call_target="tpu_custom_call" | custom-call | tf_op jit(solution)/shard_map/pallas_call | solution.py:512
  3.8 7.3 %all-to-all-start = ((bf16[32,136,128]{2,1,0:T(8,128)(2,1)}), bf16[32,136,128]{2,1,0:T(8,128)(2,1)S(1)}, u32[]{:S(2)}, u32[]{:S(2)}) async-start(bf16[32,136,128]{2,1,0:T(8,128)(2,1)} %get-tuple-element.35), calls=%async_computation | async-start | bytes 2228224 | tf_op jit(solution)/shard_map/all_to_all | solution.py:553
  11.1 3.8 %collective-permute-start = (bf16[256,512]{1,0:T(8,128)(2,1)S(1)}, bf16[256,512]{1,0:T(8,128)(2,1)S(1)}, u32[]{:S(2)}, u32[]{:S(2)}) collective-permute-start(bf16[256,512]{1,0:T(8,128)(2,1)S(1)} %copy-done.10), channel_id=1, source_target_pairs={{0,2},{1,3},{2,4},{3,5},{4,6},{5,7},{6,0},{7,1},{8,12},{9,13},{10,... | collective-permute-start | bytes 786440 | tf_op jit(solution)/shard_map/ppermute | solution.py:595
  14.9 24.4 %collective-permute-done = bf16[256,512]{1,0:T(8,128)(2,1)S(1)} collective-permute-done((bf16[256,512]{1,0:T(8,128)(2,1)S(1)}, bf16[256,512]{1,0:T(8,128)(2,1)S(1)}, u32[]{:S(2)}, u32[]{:S(2)}) %collective-permute-start) | collective-permute-done | bytes 262176 | tf_op jit(solution)/shard_map/ppermute | solution.py:595
  39.3 1.5 %collective-permute-start.1 = (bf16[256,512]{1,0:T(8,128)(2,1)S(1)}, bf16[256,512]{1,0:T(8,128)(2,1)S(1)}, u32[]{:S(2)}, u32[]{:S(2)}) collective-permute-start(bf16[256,512]{1,0:T(8,128)(2,1)S(1)} %collective-permute-done), channel_id=1, source_target_pairs={{0,1},{1,0},{2,3},{3,2},{4,5},{5,4},{6,7},{7,6},{8,9},{9,8},{10,11... | collective-permute-start | bytes 786440 | tf_op jit(solution)/shard_map/ppermute | solution.py:614
  40.8 5.6 %collective-permute-done.1 = bf16[256,512]{1,0:T(8,128)(2,1)S(1)} collective-permute-done((bf16[256,512]{1,0:T(8,128)(2,1)S(1)}, bf16[256,512]{1,0:T(8,128)(2,1)S(1)}, u32[]{:S(2)}, u32[]{:S(2)}) %collective-permute-start.1) | collective-permute-done | bytes 262176 | tf_op jit(solution)/shard_map/ppermute | solution.py:614
  46.6 6.2 %collective-permute-start.3 = (bf16[512,512]{1,0:T(8,128)(2,1)S(1)}, bf16[512,512]{1,0:T(8,128)(2,1)}, u32[]{:S(2)}, u32[]{:S(2)}) collective-permute-start(bf16[512,512]{1,0:T(8,128)(2,1)S(1)} %constant_dynamic-update-slice_fusion.near_ref), channel_id=1, source_target_pairs={{0,8},{8,0},{16,24},{24,16},{1,9},{9,1},{17,25},{25,17},{2,10},{10... | collective-permute-start | bytes 1572872 | tf_op jit(solution)/shard_map/ppermute | solution.py:617
  52.9 1.0 copy-done.9
  53.8 6.3 %shard_map.120 = (bf16[16,64,512]{2,1,0:T(8,128)(2,1)}, f32[16,64,128]{2,1,0:T(8,128)}, f32[32,1,128]{2,1,0:T(1,128)}, f32[32,128]{1,0:T(8,128)}) custom-call(s32[1]{0:T(128)} %bitcast.me_ref, bf16[32,136,128]{2,1,0:T(8,128)(2,1)} %copy-done.9, bf16[16,128,512]{2,1,0:T(8,128)(2,1)} %leaf_ref.1, bf16[16,512]{1,0:T(8,128)(2,1)} %mid_ref.3), custom_call_target="tpu_custom_call" | custom-call | tf_op jit(solution)/shard_map/pallas_call | solution.py:512
  60.2 1.0 collective-permute-start.4
  61.4 5.7 %collective-permute-start.7 = (bf16[136,512]{1,0:T(8,128)(2,1)}, bf16[136,512]{1,0:T(8,128)(2,1)}, u32[]{:S(2)}, u32[]{:S(2)}) collective-permute-start(bf16[136,512]{1,0:T(8,128)(2,1)} %get-tuple-element.47.own_ref), channel_id=1, source_target_pairs={{0,2},{1,3},{2,4},{3,5},{4,6},{5,7},{6,0},{7,1},{8,10},{9,11},{10,... | collective-permute-start | bytes 417800 | tf_op jit(solution)/shard_map/ppermute | solution.py:626
  67.6 2.9 %collective-permute-start.5 = (bf16[136,512]{1,0:T(8,128)(2,1)}, bf16[136,512]{1,0:T(8,128)(2,1)}, u32[]{:S(2)}, u32[]{:S(2)}) collective-permute-start(bf16[136,512]{1,0:T(8,128)(2,1)} %get-tuple-element.47.own_ref), channel_id=1, source_target_pairs={{0,6},{1,7},{2,0},{3,1},{4,2},{5,3},{6,4},{7,5},{8,14},{9,15},{10,... | collective-permute-start | bytes 417800 | tf_op jit(solution)/shard_map/ppermute | solution.py:626
  70.5 2.5 %all-to-all-start.1 = ((f32[32,1,128]{2,1,0:T(1,128)}), f32[32,1,128]{2,1,0:T(1,128)S(1)}, u32[]{:S(2)}, u32[]{:S(2)}) async-start(f32[32,1,128]{2,1,0:T(1,128)} %get-tuple-element.38), calls=%async_computation.1 | async-start | bytes 32768 | tf_op jit(solution)/shard_map/all_to_all | solution.py:553
  73.7 7.7 %all-to-all-done.1.stat_ref = f32[32,1,128]{2,1,0:T(1,128)S(1)} async-done(((f32[32,1,128]{2,1,0:T(1,128)}), f32[32,1,128]{2,1,0:T(1,128)S(1)}, u32[]{:S(2)}, u32[]{:S(2)}) %all-to-all-start.1) | async-done | bytes 16416 | tf_op jit(solution)/shard_map/all_to_all | solution.py:553
  81.4 1.2 shard_map.121
  82.7 4.1 %shard_map.122 = (f32[128,512]{1,0:T(8,128)}, f32[256,512]{1,0:T(8,128)}, f32[8,128]{1,0:T(8,128)}) custom-call(s32[1]{0:T(128)} %bitcast.1.where_ref, bf16[136,512]{1,0:T(8,128)(2,1)} %get-tuple-element.47.own_ref, bf16[512,512]{1,0:T(8,128)(2,1)} %copy-done.8, bf16[512,512]{1,0:T(8,128)(2,1)} %collective-permute-done.2.y_ref, ...), custom_call_target="tpu_custom_call" | custom-call | tf_op jit(solution)/shard_map/pallas_call | solution.py:512
  86.8 1.1 pad_maximum_fusion.blocks_ref
  88.6 14.8 %all_to_all.20.norm_ref = f32[32,1,128]{2,1,0:T(1,128)S(1)} all-to-all(f32[32,1,128]{2,1,0:T(1,128)S(1)} %get-tuple-element.39), channel_id=1, replica_groups=mesh['dp'=4,'label'=8] {'dp','label'}, dimensions={0} | all-to-all | bytes 32768 | tf_op jit(solution)/shard_map/all_to_all | solution.py:553
  103.4 3.8 %shard_map.123 = (bf16[16,64,128]{2,1,0:T(8,128)(2,1)S(1)}, bf16[32,128,128]{2,1,0:T(8,128)(2,1)}) custom-call(f32[16,64,128]{2,1,0:T(8,128)S(1)} %copy-done.1, f32[32,128]{1,0:T(8,128)S(1)} %copy-done.7, f32[32,1,128]{2,1,0:T(1,128)S(1)} %all_to_all.20.norm_ref, bf16[16,128,512]{2,1,0:T(8,128)(2,1)S(1)} %copy-done, bf16[16,512]{1,0:T(8,128)(2,1)S(1)} %copy-done.6), custom_call_target="tpu_custom_call" | custom-call | tf_op jit(solution)/shard_map/pallas_call | solution.py:512
  107.3 0.7 copy-done.4
  108.0 4.2 %all-to-all-start.3 = ((bf16[32,128,128]{2,1,0:T(8,128)(2,1)}), bf16[32,128,128]{2,1,0:T(8,128)(2,1)S(1)}, u32[]{:S(2)}, u32[]{:S(2)}) async-start(bf16[32,128,128]{2,1,0:T(8,128)(2,1)} %get-tuple-element.45), calls=%async_computation.3 | async-start | bytes 2097152 | tf_op jit(solution)/shard_map/all_to_all | solution.py:553
  112.2 4.6 %shard_map.125.part_ref = f32[256,512]{1,0:T(8,128)} custom-call(s32[1]{0:T(128)} %bitcast.1.where_ref, bf16[4,136,512]{2,1,0:T(8,128)(2,1)} %copy-done.11, bf16[512,512]{1,0:T(8,128)(2,1)} %copy-done.8, bf16[512,512]{1,0:T(8,128)(2,1)} %collective-permute-done.2.y_ref, bf16[512,512]{1,0:T(8,128)(2,1)} %collective-permute-done.3.core_ref, ...), custom_call_target="tpu_custom_call" | custom-call | tf_op jit(solution)/shard_map/pallas_call | solution.py:512
  116.8 5.0 %shard_map.126 = f32[256,512]{1,0:T(8,128)} custom-call(s32[1]{0:T(128)} %bitcast.1.where_ref, bf16[4,136,512]{2,1,0:T(8,128)(2,1)} %collective-permute-done.8.blocks_ref, bf16[512,512]{1,0:T(8,128)(2,1)} %copy-done.8, bf16[512,512]{1,0:T(8,128)(2,1)} %collective-permute-done.2.y_ref, bf16[512,512]{1,0:T(8,128)(2,1)} %collective-permute-done.3.core_ref, ...), custom_call_target="tpu_custom_call" | custom-call | tf_op jit(solution)/shard_map/pallas_call | solution.py:512
  121.9 2.0 %collective-permute-done.9 = f32[256,512]{1,0:T(8,128)S(1)} collective-permute-done((f32[256,512]{1,0:T(8,128)}, f32[256,512]{1,0:T(8,128)S(1)}, u32[]{:S(2)}, u32[]{:S(2)}) %collective-permute-start.9) | collective-permute-done | bytes 524320 | tf_op jit(solution)/shard_map/ppermute | solution.py:697
  124.0 1.0 dynamic-slice_add_fusion
  125.0 1.7 %collective-permute-start.10 = (f32[128,512]{1,0:T(8,128)S(1)}, f32[128,512]{1,0:T(8,128)S(1)}, u32[]{:S(2)}, u32[]{:S(2)}) collective-permute-start(f32[128,512]{1,0:T(8,128)S(1)} %dynamic-slice_add_fusion), channel_id=1, source_target_pairs={{0,16},{8,24},{16,0},{24,8},{1,17},{9,25},{17,1},{25,9},{2,18},{10... | collective-permute-start | bytes 786440 | tf_op jit(solution)/shard_map/ppermute | solution.py:699
  127.9 4.3 %shard_map.127 = (f32[16,128,512]{2,1,0:T(8,128)}, f32[16,512]{1,0:T(8,128)}) custom-call(bf16[16,64,128]{2,1,0:T(8,128)(2,1)} %copy-done.4, f32[32,1,128]{2,1,0:T(1,128)} %copy-done.5, bf16[16,64,512]{2,1,0:T(8,128)(2,1)} %get-tuple-element.57.rows_ref), custom_call_target="tpu_custom_call" | custom-call | tf_op jit(solution)/shard_map/pallas_call | solution.py:512
  132.2 2.7 %collective-permute-done.10 = f32[128,512]{1,0:T(8,128)S(1)} collective-permute-done((f32[128,512]{1,0:T(8,128)S(1)}, f32[128,512]{1,0:T(8,128)S(1)}, u32[]{:S(2)}, u32[]{:S(2)}) %collective-permute-start.10) | collective-permute-done | bytes 262176 | tf_op jit(solution)/shard_map/ppermute | solution.py:699
  135.1 1.5 %collective-permute-done.11 = f32[128,512]{1,0:T(8,128)S(1)} collective-permute-done((f32[128,512]{1,0:T(8,128)S(1)}, f32[128,512]{1,0:T(8,128)S(1)}, u32[]{:S(2)}, u32[]{:S(2)}) %collective-permute-start.11) | collective-permute-done | bytes 262176 | tf_op jit(solution)/shard_map/ppermute | solution.py:706
  136.6 0.8 pad_maximum_fusion.1
  137.5 2.0 %all-to-all-done.3.back_ref = bf16[32,128,128]{2,1,0:T(8,128)(2,1)S(1)} async-done(((bf16[32,128,128]{2,1,0:T(8,128)(2,1)}), bf16[32,128,128]{2,1,0:T(8,128)(2,1)S(1)}, u32[]{:S(2)}, u32[]{:S(2)}) %all-to-all-start.3) | async-done | bytes 1048608 | tf_op jit(solution)/shard_map/all_to_all | solution.py:553
  139.5 1.4 shard_map.124
  (50 shorter events, 3.8 us)
Async XLA Ops:
  0.6 10.5 %copy-start.10 = (bf16[256,512]{1,0:T(8,128)(2,1)S(1)}, bf16[256,512]{1,0:T(8,128)(2,1)}, u32[]{:S(2)}) copy-start(bf16[256,512]{1,0:T(8,128)(2,1)} %weight_ref.5) | copy-start | bytes 786436
  3.8 49.1 %all-to-all-start = ((bf16[32,136,128]{2,1,0:T(8,128)(2,1)}), bf16[32,136,128]{2,1,0:T(8,128)(2,1)S(1)}, u32[]{:S(2)}, u32[]{:S(2)}) async-start(bf16[32,136,128]{2,1,0:T(8,128)(2,1)} %get-tuple-element.35), calls=%async_computation | async-start | bytes 2228224 | tf_op jit(solution)/shard_map/all_to_all | solution.py:553
  11.1 70.3 %copy-start.3 = (f32[128,128]{1,0:T(8,128)S(1)}, f32[128,128]{1,0:T(8,128)}, u32[]{:S(2)}) copy-start(f32[128,128]{1,0:T(8,128)} %get-tuple-element.34.info_ref) | copy-start | bytes 196612
  11.1 28.2 %collective-permute-start = (bf16[256,512]{1,0:T(8,128)(2,1)S(1)}, bf16[256,512]{1,0:T(8,128)(2,1)S(1)}, u32[]{:S(2)}, u32[]{:S(2)}) collective-permute-start(bf16[256,512]{1,0:T(8,128)(2,1)S(1)} %copy-done.10), channel_id=1, source_target_pairs={{0,2},{1,3},{2,4},{3,5},{4,6},{5,7},{6,0},{7,1},{8,12},{9,13},{10,... | collective-permute-start | bytes 786440 | tf_op jit(solution)/shard_map/ppermute | solution.py:595
  39.3 7.1 %collective-permute-start.1 = (bf16[256,512]{1,0:T(8,128)(2,1)S(1)}, bf16[256,512]{1,0:T(8,128)(2,1)S(1)}, u32[]{:S(2)}, u32[]{:S(2)}) collective-permute-start(bf16[256,512]{1,0:T(8,128)(2,1)S(1)} %collective-permute-done), channel_id=1, source_target_pairs={{0,1},{1,0},{2,3},{3,2},{4,5},{5,4},{6,7},{7,6},{8,9},{9,8},{10,11... | collective-permute-start | bytes 786440 | tf_op jit(solution)/shard_map/ppermute | solution.py:614
  46.4 36.2 %copy-start.8 = (bf16[512,512]{1,0:T(8,128)(2,1)}, bf16[512,512]{1,0:T(8,128)(2,1)S(1)}, u32[]{:S(2)}) copy-start(bf16[512,512]{1,0:T(8,128)(2,1)S(1)} %constant_dynamic-update-slice_fusion.near_ref) | copy-start | bytes 1572868
  46.5 13.7 %collective-permute-start.2 = (bf16[512,512]{1,0:T(8,128)(2,1)S(1)}, bf16[512,512]{1,0:T(8,128)(2,1)}, u32[]{:S(2)}, u32[]{:S(2)}) collective-permute-start(bf16[512,512]{1,0:T(8,128)(2,1)S(1)} %constant_dynamic-update-slice_fusion.near_ref), channel_id=1, source_target_pairs={{0,16},{8,24},{16,0},{24,8},{1,17},{9,25},{17,1},{25,9},{2,18},{10... | collective-permute-start | bytes 1572872 | tf_op jit(solution)/shard_map/ppermute | solution.py:616
  46.6 36.0 %collective-permute-start.3 = (bf16[512,512]{1,0:T(8,128)(2,1)S(1)}, bf16[512,512]{1,0:T(8,128)(2,1)}, u32[]{:S(2)}, u32[]{:S(2)}) collective-permute-start(bf16[512,512]{1,0:T(8,128)(2,1)S(1)} %constant_dynamic-update-slice_fusion.near_ref), channel_id=1, source_target_pairs={{0,8},{8,0},{16,24},{24,16},{1,9},{9,1},{17,25},{25,17},{2,10},{10... | collective-permute-start | bytes 1572872 | tf_op jit(solution)/shard_map/ppermute | solution.py:617
  52.9 1.0 copy-start.9
  53.8 33.0 %copy-start.12 = (bf16[136,512]{1,0:T(8,128)(2,1)S(1)}, bf16[136,512]{1,0:T(8,128)(2,1)}, u32[]{:S(2)}) copy-start(bf16[136,512]{1,0:T(8,128)(2,1)} %get-tuple-element.47.own_ref) | copy-start | bytes 417796
  60.1 43.3 %copy-start = (bf16[16,128,512]{2,1,0:T(8,128)(2,1)S(1)}, bf16[16,128,512]{2,1,0:T(8,128)(2,1)}, u32[]{:S(2)}) copy-start(bf16[16,128,512]{2,1,0:T(8,128)(2,1)} %leaf_ref.1) | copy-start | bytes 6291460
  60.2 43.3 %copy-start.1 = (f32[16,64,128]{2,1,0:T(8,128)S(1)}, f32[16,64,128]{2,1,0:T(8,128)}, u32[]{:S(2)}) copy-start(f32[16,64,128]{2,1,0:T(8,128)} %get-tuple-element.36.score_ref) | copy-start | bytes 1572868
  60.2 43.2 %copy-start.6 = (bf16[16,512]{1,0:T(8,128)(2,1)S(1)}, bf16[16,512]{1,0:T(8,128)(2,1)}, u32[]{:S(2)}) copy-start(bf16[16,512]{1,0:T(8,128)(2,1)} %mid_ref.3) | copy-start | bytes 49156
  60.2 43.2 %copy-start.7 = (f32[32,128]{1,0:T(8,128)S(1)}, f32[32,128]{1,0:T(8,128)}, u32[]{:S(2)}) copy-start(f32[32,128]{1,0:T(8,128)} %get-tuple-element.37.code_ref) | copy-start | bytes 49156
  60.2 22.5 %collective-permute-start.4 = (bf16[512,512]{1,0:T(8,128)(2,1)}, bf16[512,512]{1,0:T(8,128)(2,1)}, u32[]{:S(2)}, u32[]{:S(2)}) collective-permute-start(bf16[512,512]{1,0:T(8,128)(2,1)} %collective-permute-done.2.y_ref), channel_id=1, source_target_pairs={{0,8},{8,0},{16,24},{24,16},{1,9},{9,1},{17,25},{25,17},{2,10},{10... | collective-permute-start | bytes 1572872 | tf_op jit(solution)/shard_map/ppermute | solution.py:652
  61.4 25.4 %collective-permute-start.7 = (bf16[136,512]{1,0:T(8,128)(2,1)}, bf16[136,512]{1,0:T(8,128)(2,1)}, u32[]{:S(2)}, u32[]{:S(2)}) collective-permute-start(bf16[136,512]{1,0:T(8,128)(2,1)} %get-tuple-element.47.own_ref), channel_id=1, source_target_pairs={{0,2},{1,3},{2,4},{3,5},{4,6},{5,7},{6,0},{7,1},{8,10},{9,11},{10,... | collective-permute-start | bytes 417800 | tf_op jit(solution)/shard_map/ppermute | solution.py:626
  67.0 19.8 %collective-permute-start.6 = (bf16[136,512]{1,0:T(8,128)(2,1)}, bf16[136,512]{1,0:T(8,128)(2,1)}, u32[]{:S(2)}, u32[]{:S(2)}) collective-permute-start(bf16[136,512]{1,0:T(8,128)(2,1)} %get-tuple-element.47.own_ref), channel_id=1, source_target_pairs={{0,4},{1,5},{2,6},{3,7},{4,0},{5,1},{6,2},{7,3},{8,12},{9,13},{10,... | collective-permute-start | bytes 417800 | tf_op jit(solution)/shard_map/ppermute | solution.py:626
  67.6 19.2 %collective-permute-start.5 = (bf16[136,512]{1,0:T(8,128)(2,1)}, bf16[136,512]{1,0:T(8,128)(2,1)}, u32[]{:S(2)}, u32[]{:S(2)}) collective-permute-start(bf16[136,512]{1,0:T(8,128)(2,1)} %get-tuple-element.47.own_ref), channel_id=1, source_target_pairs={{0,6},{1,7},{2,0},{3,1},{4,2},{5,3},{6,4},{7,5},{8,14},{9,15},{10,... | collective-permute-start | bytes 417800 | tf_op jit(solution)/shard_map/ppermute | solution.py:626
  70.5 10.9 %all-to-all-start.1 = ((f32[32,1,128]{2,1,0:T(1,128)}), f32[32,1,128]{2,1,0:T(1,128)S(1)}, u32[]{:S(2)}, u32[]{:S(2)}) async-start(f32[32,1,128]{2,1,0:T(1,128)} %get-tuple-element.38), calls=%async_computation.1 | async-start | bytes 32768 | tf_op jit(solution)/shard_map/all_to_all | solution.py:553
  87.9 20.0 %copy-start.11 = (bf16[4,136,512]{2,1,0:T(8,128)(2,1)}, bf16[4,136,512]{2,1,0:T(8,128)(2,1)S(1)}, u32[]{:S(2)}) copy-start(bf16[4,136,512]{2,1,0:T(8,128)(2,1)S(1)} %pad_maximum_fusion.blocks_ref) | copy-start | bytes 1671172
  87.9 28.9 %collective-permute-start.8 = (bf16[4,136,512]{2,1,0:T(8,128)(2,1)S(1)}, bf16[4,136,512]{2,1,0:T(8,128)(2,1)}, u32[]{:S(2)}, u32[]{:S(2)}) collective-permute-start(bf16[4,136,512]{2,1,0:T(8,128)(2,1)S(1)} %pad_maximum_fusion.blocks_ref), channel_id=1, source_target_pairs={{0,1},{1,0},{2,3},{3,2},{4,5},{5,4},{6,7},{7,6},{8,9},{9,8},{10,11... | collective-permute-start | bytes 1671176 | tf_op jit(solution)/shard_map/ppermute | solution.py:672
  103.4 4.5 %copy-start.5 = (f32[32,1,128]{2,1,0:T(1,128)}, f32[32,1,128]{2,1,0:T(1,128)S(1)}, u32[]{:S(2)}) copy-start(f32[32,1,128]{2,1,0:T(1,128)S(1)} %all_to_all.20.norm_ref) | copy-start | bytes 49156
  107.3 0.7 copy-start.4
  108.0 31.5 %all-to-all-start.3 = ((bf16[32,128,128]{2,1,0:T(8,128)(2,1)}), bf16[32,128,128]{2,1,0:T(8,128)(2,1)S(1)}, u32[]{:S(2)}, u32[]{:S(2)}) async-start(bf16[32,128,128]{2,1,0:T(8,128)(2,1)} %get-tuple-element.45), calls=%async_computation.3 | async-start | bytes 2097152 | tf_op jit(solution)/shard_map/all_to_all | solution.py:553
  121.9 2.1 %collective-permute-start.9 = (f32[256,512]{1,0:T(8,128)}, f32[256,512]{1,0:T(8,128)S(1)}, u32[]{:S(2)}, u32[]{:S(2)}) collective-permute-start(f32[256,512]{1,0:T(8,128)} %shard_map.126), channel_id=1, source_target_pairs={{0,8},{8,0},{16,24},{24,16},{1,9},{9,1},{17,25},{25,17},{2,10},{10... | collective-permute-start | bytes 1572872 | tf_op jit(solution)/shard_map/ppermute | solution.py:697
  125.0 10.0 %collective-permute-start.10 = (f32[128,512]{1,0:T(8,128)S(1)}, f32[128,512]{1,0:T(8,128)S(1)}, u32[]{:S(2)}, u32[]{:S(2)}) collective-permute-start(f32[128,512]{1,0:T(8,128)S(1)} %dynamic-slice_add_fusion), channel_id=1, source_target_pairs={{0,16},{8,24},{16,0},{24,8},{1,17},{9,25},{17,1},{25,9},{2,18},{10... | collective-permute-start | bytes 786440 | tf_op jit(solution)/shard_map/ppermute | solution.py:699
  127.9 11.6 %copy-start.2 = (f32[128,512]{1,0:T(8,128)S(1)}, f32[128,512]{1,0:T(8,128)}, u32[]{:S(2)}) copy-start(f32[128,512]{1,0:T(8,128)} %get-tuple-element.46.top_ref) | copy-start | bytes 786436
  135.0 1.6 %collective-permute-start.11 = (f32[128,512]{1,0:T(8,128)S(1)}, f32[128,512]{1,0:T(8,128)S(1)}, u32[]{:S(2)}, u32[]{:S(2)}) collective-permute-start(f32[128,512]{1,0:T(8,128)S(1)} %add.118), channel_id=1, source_target_pairs={{0,8},{8,0},{16,24},{24,16},{1,9},{9,1},{17,25},{25,17},{2,10},{10... | collective-permute-start | bytes 786440 | tf_op jit(solution)/shard_map/ppermute | solution.py:706

commit v4 on v3

--- a/solution.py
+++ b/solution.py
@@ -260,14 +260,30 @@
     return copies
 
 
+def cluster_rows(wide_ref, k, devs, held, chunks):
+    slots = CAPB * held
+    return jnp.concatenate(
+        [
+            jnp.concatenate(
+                [
+                    wide_ref[pl.ds(c * slots + r * held + k, devs, stride=chunks * slots), :]
+                    for c in range(chunks)
+                ],
+                axis=1,
+            )
+            for r in range(CAPB)
+        ],
+        axis=0,
+    )
+
+
 def forward_kernel(
-    me_ref, got_ref, leaf_in, mid_ref, rows_out, score_out, stat_ref, code_ref,
-    wide_ref, table_ref, leaf_ref, rows_ref, score_ref, leaf_sem, rows_sem, score_sem,
+    me_ref, got_ref, leaf_in, mid_ref, score_ref, stat_ref, code_ref,
+    wide_ref, table_ref, leaf_ref, leaf_sem,
 ):
     devs, depth, _ = got_ref.shape
     held, labels, width = leaf_ref.shape
     fetches = start(halves(leaf_in, leaf_ref, leaf_sem))
-    sends = list(zip(halves(rows_ref, rows_out, rows_sem), halves(score_ref, score_out, score_sem)))
     chunks = width // LANES
     slots = CAPB * held
     body = chunks * slots
@@ -287,20 +303,8 @@
     label_f = iota_f((CAPB * devs, labels), 1)
     stats = jnp.zeros((devs, LANES), F32)
     for k in range(held):
-        parts = []
-        for r in range(CAPB):
-            parts.append(
-                jnp.concatenate(
-                    [
-                        wide_ref[pl.ds(c * slots + r * held + k, devs, stride=body), :]
-                        for c in range(chunks)
-                    ],
-                    axis=1,
-                )
-            )
-        full = jnp.concatenate(parts, axis=0)
+        full = cluster_rows(wide_ref, k, devs, held, chunks)
         rows = full.astype(BF)
-        rows_ref[k] = rows
         if k % (held // 2) == 0:
             fetches[k // (held // 2)].wait()
         scores = dot_nt(rows, leaf_ref[k])
@@ -317,12 +321,7 @@
                 stats = jnp.where(
                     lane == n * slots + r * held + k, value[r * devs : (r + 1) * devs], stats
                 )
-        if (k + 1) % (held // 2) == 0:
-            start(sends[k // (held // 2)])
     stat_ref[...] = stats.reshape(stat_ref.shape)
-    for pair in sends:
-        for send in pair:
-            send.wait()
 
 
 def middle_kernel(info_ref, stat_ref, out_ref, loss_ref, *, devs, held, short_len):
@@ -404,21 +403,28 @@
     pay_ref[...] = wide_ref[...].astype(BF).reshape(devs, body, LANES)
 
 
-def grads_kernel(delta_ref, norm_ref, rows_ref, leaf_grad_ref, mid_grad_ref):
+def grads_kernel(delta_ref, norm_ref, got_ref, leaf_grad_ref, mid_grad_ref, wide_ref):
     held, pairs, _ = delta_ref.shape
     devs = pairs // CAPB
     slots = CAPB * held
+    chunks = leaf_grad_ref.shape[2] // LANES
+    body = chunks * slots
+    wide_ref[...] = got_ref[:, :body, :].reshape(devs * body, LANES).astype(F32)
     norms = norm_ref[...].reshape(devs, LANES)
     for k in range(held):
-        rows = rows_ref[k]
-        leaf_grad_ref[k] = dot_tn(delta_ref[k], rows)
+        full = cluster_rows(wide_ref, k, devs, held, chunks)
+        leaf_grad_ref[k] = dot_tn(delta_ref[k], full.astype(BF))
         mid_delta = jnp.concatenate(
             [norms[:, slots + r * held + k : slots + r * held + k + 1] for r in range(CAPB)], axis=0
         )
-        mid_grad_ref[k : k + 1, :] = jnp.sum(mid_delta * rows.astype(F32), axis=0, keepdims=True)
-
-
-def finish_kernel(info_ref, back_ref, top_ref, out_ref, *, held, short_len):
+        mid_grad_ref[k : k + 1, :] = jnp.sum(mid_delta * full, axis=0, keepdims=True)
+
+
+def finish_kernel(
+    info_ref, back_ref, top_ref, top_loss_ref, pair_loss_ref, out_ref, loss_ref, *, held, short_len
+):
+    loss_ref[0:1, :] = top_loss_ref[0:1, :]
+    loss_ref[1:3, :] = pair_loss_ref[0:2, :]
     rows, width = out_ref.shape
     devs = back_ref.shape[0]
     clusters = devs * held
@@ -460,9 +466,31 @@
     return jnp.broadcast_to(target, (LANES, LANES)).T[:, 0:1]
 
 
+def own_columns(me, dims, label_size, held_top):
+    steps = label_size // 2
+
+    def split(value, size):
+        high = jnp.floor((value + 0.5) * (1.0 / size))
+        return high, value - high * size
+
+    def flip(bit, other):
+        return bit + other - 2.0 * bit * other
+
+    dp_at, label_at = split(jnp.full(dims, me, jnp.int32).astype(F32), label_size)
+    y_at, core_at = split(dp_at, 2)
+    z_at, x_at = split(label_at, 2)
+    part, rest = split(iota_f(dims, 1), 2 * held_top)
+    side, row = split(rest, held_top)
+    core_bit, y_bit = split(part, 2)
+    dp_from = flip(y_at, y_bit) * 2.0 + flip(core_at, core_bit)
+    z_from = z_at - dp_from - 1.0
+    z_from = jnp.where(z_from < 0.0, z_from + steps, z_from)
+    return (z_from * 2.0 + flip(x_at, side)) * held_top + row
+
+
 def top_own_kernel(
-    where_ref, own_ref, near_ref, y_ref, core_ref, far_ref, column_ref, weight_ref,
-    back_ref, part_ref, loss_ref,
+    where_ref, me_ref, own_ref, near_ref, y_ref, core_ref, far_ref, weight_ref,
+    back_ref, part_ref, loss_ref, *, label_size,
 ):
     rows = own_ref.shape[0] - SUB
     piece = near_ref.shape[0]
@@ -473,7 +501,8 @@
         block, target, pieces, weight_ref[...], where_ref[0].astype(F32)
     )
     part_ref[...] = part
-    hit = jnp.broadcast_to(column_ref[...], scores.shape) == target
+    column = own_columns(me_ref[0], (SUB, scores.shape[1]), label_size, weight_ref.shape[0])
+    hit = jnp.broadcast_to(column[0:1, :], scores.shape) == target
     full = (jnp.exp(scores - total) - jnp.where(hit, 1.0, 0.0)).astype(BF)
     back = dot_nn(full[:, :piece], pieces[0][...])
     for n in range(1, len(pieces)):
@@ -483,19 +512,32 @@
     loss_ref[...] = jnp.broadcast_to(loss, (rows, LANES)).T[:SUB, :]
 
 
-def top_more_kernel(
-    where_ref, blocks_ref, near_ref, y_ref, core_ref, far_ref, weight_ref, part_ref, out_ref,
-    *, first,
-):
+def top_blocks(where_ref, blocks_ref, pieces, weight_ref, first):
     count, depth, _ = blocks_ref.shape
     rows = depth - SUB
     numbers = range(first, count)
     block = jnp.concatenate([blocks_ref[n, :rows, :] for n in numbers], axis=0)
     target = jnp.concatenate([top_column(blocks_ref[n, rows:, :]) for n in numbers], axis=0)
-    base = where_ref[0].astype(F32)
+    return top_step(block, target, pieces, weight_ref[...], where_ref[0].astype(F32))[2]
+
+
+def top_near_kernel(
+    where_ref, blocks_ref, near_ref, y_ref, core_ref, far_ref, weight_ref, part_ref, out_ref
+):
     pieces = (near_ref, y_ref, core_ref, far_ref)
-    part = top_step(block, target, pieces, weight_ref[...], base)[2]
-    out_ref[...] = part_ref[...] + part
+    out_ref[...] = part_ref[...] + top_blocks(where_ref, blocks_ref, pieces, weight_ref, 1)
+
+
+def top_far_kernel(
+    where_ref, me_ref, blocks_ref, near_ref, y_ref, core_ref, far_ref, weight_ref, part_ref,
+    kept_ref, given_ref, sum_ref, *, label_size,
+):
+    pieces = (near_ref, y_ref, core_ref, far_ref)
+    sum_ref[...] = part_ref[...] + top_blocks(where_ref, blocks_ref, pieces, weight_ref, 0)
+    half = kept_ref.shape[0]
+    core = lax.rem(lax.div(me_ref[0], label_size), 2)
+    kept_ref[...] = sum_ref[pl.ds(pl.multiple_of(core * half, SUB), half), :]
+    given_ref[...] = sum_ref[pl.ds(pl.multiple_of((1 - core) * half, SUB), half), :]
 
 
 def spec():
@@ -615,20 +657,12 @@
     w_own = jnp.concatenate([w_near, w_other])
     w_y = lax.ppermute(w_own, "dp", flip_y)
     w_core = lax.ppermute(w_own, "dp", flip_core)
-    z_at, x_at = label_at // 2, label_at % 2
-    dp_source = jnp.stack([dp_at, dp_at ^ 2, dp_at ^ 1, dp_at ^ 3])
-    source = (z_at - dp_source - 1) % steps * 2
-    source = jnp.stack([source + x_at, source + 1 - x_at], axis=1)
-    own_column = (source[:, :, None] * held_top + jnp.arange(held_top)).reshape(
-        1, label_size * held_top
-    )
     sent = after(own, w_near)
     peers = [lax.ppermute(sent, "label", along(n)) for n in range(1, steps)]
     pairs = CAPB * devs
-    rows_held, scores, stats, codes = call(
+    scores, stats, codes = call(
         forward_kernel,
         (
-            shape((held, pairs, width), BF),
             shape((held, pairs, labels), F32),
             shape((devs, 1, LANES), F32),
             shape((devs, LANES), F32),
@@ -638,15 +672,11 @@
             pltpu.VMEM((devs * body, LANES), F32),
             pltpu.VMEM((devs * tail, LANES), F32),
             pltpu.VMEM((held, labels, width), BF),
-            pltpu.VMEM((held, pairs, width), BF),
-            pltpu.VMEM((held, pairs, labels), F32),
-            pltpu.SemaphoreType.DMA((2,)),
-            pltpu.SemaphoreType.DMA((2,)),
             pltpu.SemaphoreType.DMA((2,)),
         ),
         scalars=1,
         far_ins=(2,),
-        far_outs=(0, 1),
+        mib=50,
     )
     w_y = after(w_y, stats)
     w_far = lax.ppermute(w_y, "dp", flip_core)
@@ -659,14 +689,14 @@
     )
     norms_held = exchange(norms)
     top_back, top_part, top_loss = call(
-        top_own_kernel,
+        functools.partial(top_own_kernel, label_size=label_size),
         (
             shape((rows, width), F32),
             shape((held_top, width), F32),
             shape((SUB, rows), F32),
         ),
-        (label_base, own, after(w_own, norms), w_y, w_core, w_far, own_column.astype(F32), top_weight),
-        scalars=1,
+        (label_base, me, own, after(w_own, norms), w_y, w_core, w_far, top_weight),
+        scalars=2,
     )
     mine = jnp.stack([sent] + after(peers, top_part))
     other = lax.ppermute(mine, "label", flip_x)
@@ -680,37 +710,36 @@
     )
     returned = exchange(back)
     top_part = call(
-        functools.partial(top_more_kernel, first=1),
+        top_near_kernel,
         shape((held_top, width), F32),
         (label_base, after(mine, back), w_own, w_y, w_core, w_far, top_weight, top_part),
         scalars=1,
     )
-    top_part = call(
-        functools.partial(top_more_kernel, first=0),
-        shape((held_top, width), F32),
-        (label_base, after(other, back), w_own, w_y, w_core, w_far, top_weight, top_part),
-        scalars=1,
-    )
-    losses = jnp.concatenate([top_loss[:1], pair_losses[:2]])
+    kept, given = call(
+        functools.partial(top_far_kernel, label_size=label_size),
+        (shape((held_top // 2, width), F32), shape((held_top // 2, width), F32)),
+        (label_base, me, after(other, back), w_own, w_y, w_core, w_far, top_weight, top_part),
+        scalars=2,
+        scratch=(pltpu.VMEM((held_top, width), F32),),
+    )
     core = dp_at % 2
-    half = held_top // 2
-    both = top_part + lax.ppermute(top_part, "dp", flip_core)
-    share = lax.dynamic_slice_in_dim(both, core * half, half, 0)
+    share = kept + lax.ppermute(given, "dp", flip_core)
     from_y = lax.ppermute(share, "dp", flip_y)
     leaf_grad, mid_grad = call(
         grads_kernel,
         (shape((held, labels, width), F32), shape((held, width), F32)),
-        (delta, norms_held, after(rows_held, (share, losses))),
+        (delta, norms_held, after(got, share)),
+        scratch=(pltpu.VMEM((devs * body, LANES), F32),),
     )
     share = share + after(from_y, mid_grad)
     rest = lax.ppermute(share, "dp", flip_core)
     top_grad = jnp.concatenate(
         [jnp.where(core == 0, share, rest), jnp.where(core == 0, rest, share)]
     )
-    query_grad = call(
+    query_grad, losses = call(
         functools.partial(finish_kernel, held=held, short_len=short_len),
-        shape((rows, width), F32),
-        (info, returned, top_back),
+        (shape((rows, width), F32), shape((3, rows), F32)),
+        (info, returned, top_back, top_loss, pair_losses),
         mib=16,
     )
     return (query_grad, top_grad, mid_grad, leaf_grad, losses)

time: 142 us -> 168 us (1.18)
  waiting for transfers between devices: 46 us -> 73.9 us
  other arithmetic: 3.78 us -> 1.96 us
    ppermute x3, waiting for transfers between devices: 0.01 us -> 30.1 us  [per_device(): peers = [lax.ppermute(sent, 'label', along(n)) for n in range(1, steps)]]
    ppermute x1, waiting for transfers between devices: 0.01 us -> 7.4 us  [per_device(): other = lax.ppermute(mine, 'label', flip_x)]
    all_to_all x3, waiting for transfers between devices: 9.74 us -> 2.94 us  [exchange(): lax.all_to_all(array, ('dp', 'label'), split_axis=0, concat_axis=0, tiled...]
    ppermute x1, starting transfers between devices: 1.04 us -> 4.89 us  [per_device(): w_far = lax.ppermute(w_y, 'dp', flip_core)]
    ppermute x3, starting transfers between devices: 9.13 us -> 5.65 us  [per_device(): peers = [lax.ppermute(sent, 'label', along(n)) for n in range(1, steps)]]
    unnamed x27, local copies, waits for them, and re-layouts: 1.76 us -> 4.11 us
    ppermute x1, waiting for transfers between devices: 2.71 us -> 0.96 us  [per_device(): from_y = lax.ppermute(share, 'dp', flip_y)]
  transfers between devices with their start and end apart: 15 -> 15, of which waited for: 7 -> 9; matrix products, arithmetic and copies ran while one was open for 3% -> 2% of each run, Pallas kernels for 21% -> 15%
where the time goes in v4:
time: 168 us; the launch traced here: 167 us
  waiting for transfers between devices  73.9 us (44%)
  starting transfers between devices  37.9 us (23%)
  Pallas kernels  33 us (20%)
  blocking collectives  14.6 us (9%)
  local copies, waits for them, and re-layouts  4.83 us (3%)
  other arithmetic  1.96 us (1%)
    pallas_call x9, Pallas kernels, call(): pl.pallas_call(kernel, out_shape=outs, in_specs=[small if n < scalars els...  33 us
    ppermute x3, waiting for transfers between devices, per_device(): peers = [lax.ppermute(sent, 'label', along(n)) for n in range(1, steps)]  30.1 us
    ppermute x1, waiting for transfers between devices, per_device(): w_near = lax.ppermute(top_weight, ('dp', 'label'), shift_z)  24.4 us
    all_to_all x1, blocking collectives, exchange(): lax.all_to_all(array, ('dp', 'label'), split_axis=0, concat_axis=0, tiled...  14.6 us
    all_to_all x3, starting transfers between devices, exchange(): lax.all_to_all(array, ('dp', 'label'), split_axis=0, concat_axis=0, tiled...  12.8 us
    ppermute x1, waiting for transfers between devices, per_device(): other = lax.ppermute(mine, 'label', flip_x)  7.4 us
    ppermute x1, starting transfers between devices, per_device(): w_core = lax.ppermute(w_own, 'dp', flip_core)  6.15 us
    ppermute x3, starting transfers between devices, per_device(): peers = [lax.ppermute(sent, 'label', along(n)) for n in range(1, steps)]  5.65 us
  transfers between devices with their start and end apart: 15, of which 9 were waited for; matrix products, arithmetic and copies ran while one was open for 2% of the time, Pallas kernels for 15%

profile of v4, /device:TPU:0, one launch (start us, length us, event | category | flops | bytes accessed | tf_op | source)
XLA Modules:
  0.0 167.1 jit_solution(10620478432754116388)
XLA Ops:
  0.7 3.2 %shard_map.119 = (bf16[32,136,128]{2,1,0:T(8,128)(2,1)}, f32[128,128]{1,0:T(8,128)}, bf16[136,512]{1,0:T(8,128)(2,1)}) custom-call(bf16[128,512]{1,0:T(8,128)(2,1)} %q_ref, s32[4,128]{1,0:T(4,128)} %bitcast.14, s32[1,512]{1,0:T(1,128)} %bitcast.15, s32[1,128]{1,0:T(1,128)} %bitcast.16, s32[1,128]{1,0:T(1,128)} %bitcast.17), custom_call_target="tpu_custom_call" | custom-call | tf_op jit(solution)/shard_map/pallas_call | solution.py:554
  3.9 7.3 %all-to-all-start = ((bf16[32,136,128]{2,1,0:T(8,128)(2,1)}), bf16[32,136,128]{2,1,0:T(8,128)(2,1)S(1)}, u32[]{:S(2)}, u32[]{:S(2)}) async-start(bf16[32,136,128]{2,1,0:T(8,128)(2,1)} %get-tuple-element.38), calls=%async_computation | async-start | bytes 2228224 | tf_op jit(solution)/shard_map/all_to_all | solution.py:595
  11.2 3.8 %collective-permute-start = (bf16[256,512]{1,0:T(8,128)(2,1)}, bf16[256,512]{1,0:T(8,128)(2,1)S(1)}, u32[]{:S(2)}, u32[]{:S(2)}) collective-permute-start(bf16[256,512]{1,0:T(8,128)(2,1)} %weight_ref.5), channel_id=1, source_target_pairs={{0,2},{1,3},{2,4},{3,5},{4,6},{5,7},{6,0},{7,1},{8,12},{9,13},{10,... | collective-permute-start | bytes 786440 | tf_op jit(solution)/shard_map/ppermute | solution.py:637
  15.0 24.4 %collective-permute-done = bf16[256,512]{1,0:T(8,128)(2,1)S(1)} collective-permute-done((bf16[256,512]{1,0:T(8,128)(2,1)}, bf16[256,512]{1,0:T(8,128)(2,1)S(1)}, u32[]{:S(2)}, u32[]{:S(2)}) %collective-permute-start) | collective-permute-done | bytes 262176 | tf_op jit(solution)/shard_map/ppermute | solution.py:637
  39.4 1.5 collective-permute-start.1
  41.6 4.9 %collective-permute-done.1 = bf16[256,512]{1,0:T(8,128)(2,1)S(1)} collective-permute-done((bf16[256,512]{1,0:T(8,128)(2,1)S(1)}, bf16[256,512]{1,0:T(8,128)(2,1)S(1)}, u32[]{:S(2)}, u32[]{:S(2)}) %collective-permute-start.1) | collective-permute-done | bytes 262176 | tf_op jit(solution)/shard_map/ppermute | solution.py:656
  47.3 6.1 %collective-permute-start.3 = (bf16[512,512]{1,0:T(8,128)(2,1)}, bf16[512,512]{1,0:T(8,128)(2,1)}, u32[]{:S(2)}, u32[]{:S(2)}) collective-permute-start(bf16[512,512]{1,0:T(8,128)(2,1)} %constant_dynamic-update-slice_fusion.near_ref), channel_id=1, source_target_pairs={{0,8},{8,0},{16,24},{24,16},{1,9},{9,1},{17,25},{25,17},{2,10},{10... | collective-permute-start | bytes 1572872 | tf_op jit(solution)/shard_map/ppermute | solution.py:659
  53.4 3.1 %shard_map.120 = (f32[16,64,128]{2,1,0:T(8,128)S(1)}, f32[32,1,128]{2,1,0:T(1,128)S(1)}, f32[32,128]{1,0:T(8,128)S(1)}) custom-call(s32[1]{0:T(128)} %bitcast.me_ref, bf16[32,136,128]{2,1,0:T(8,128)(2,1)S(1)} %all-to-all-done.got_ref, bf16[16,128,512]{2,1,0:T(8,128)(2,1)S(1)} %copy-done.1, bf16[16,512]{1,0:T(8,128)(2,1)S(1)} %copy-done.8), custom_call_target="tpu_custom_call" | custom-call | tf_op jit(solution)/shard_map/pallas_call | solution.py:554
  57.3 4.9 %collective-permute-start.4 = (bf16[512,512]{1,0:T(8,128)(2,1)}, bf16[512,512]{1,0:T(8,128)(2,1)}, u32[]{:S(2)}, u32[]{:S(2)}) collective-permute-start(bf16[512,512]{1,0:T(8,128)(2,1)} %collective-permute-done.2.y_ref), channel_id=1, source_target_pairs={{0,8},{8,0},{16,24},{24,16},{1,9},{9,1},{17,25},{25,17},{2,10},{10... | collective-permute-start | bytes 1572872 | tf_op jit(solution)/shard_map/ppermute | solution.py:682
  62.2 14.6 %all_to_all.20.stat_ref = f32[32,1,128]{2,1,0:T(1,128)S(1)} all-to-all(f32[32,1,128]{2,1,0:T(1,128)S(1)} %get-tuple-element.41), channel_id=1, replica_groups=mesh['dp'=4,'label'=8] {'dp','label'}, dimensions={0} | all-to-all | bytes 32768 | tf_op jit(solution)/shard_map/all_to_all | solution.py:595
  76.8 1.8 %shard_map.121 = (f32[32,1,128]{2,1,0:T(1,128)}, f32[8,128]{1,0:T(8,128)S(1)}) custom-call(f32[128,128]{1,0:T(8,128)S(1)} %copy-done.6, f32[32,1,128]{2,1,0:T(1,128)S(1)} %all_to_all.20.stat_ref), custom_call_target="tpu_custom_call" | custom-call | tf_op jit(solution)/shard_map/pallas_call | solution.py:554
  78.6 2.5 %all-to-all-start.2 = ((f32[32,1,128]{2,1,0:T(1,128)}), f32[32,1,128]{2,1,0:T(1,128)S(1)}, u32[]{:S(2)}, u32[]{:S(2)}) async-start(f32[32,1,128]{2,1,0:T(1,128)} %get-tuple-element.42), calls=%async_computation.2 | async-start | bytes 32768 | tf_op jit(solution)/shard_map/all_to_all | solution.py:595
  81.2 4.1 %shard_map.122 = (f32[128,512]{1,0:T(8,128)}, f32[256,512]{1,0:T(8,128)}, f32[8,128]{1,0:T(8,128)}) custom-call(s32[1]{0:T(128)} %bitcast.1.where_ref, s32[1]{0:T(128)} %bitcast.me_ref, bf16[136,512]{1,0:T(8,128)(2,1)} %get-tuple-element.53.own_ref, bf16[512,512]{1,0:T(8,128)(2,1)} %constant_dynamic-update-slice_fusion.near_ref, ...), custom_call_target="tpu_custom_call" | custom-call | tf_op jit(solution)/shard_map/pallas_call | solution.py:554
  85.3 2.9 %all-to-all-done.2.norm_ref = f32[32,1,128]{2,1,0:T(1,128)S(1)} async-done(((f32[32,1,128]{2,1,0:T(1,128)}), f32[32,1,128]{2,1,0:T(1,128)S(1)}, u32[]{:S(2)}, u32[]{:S(2)}) %all-to-all-start.2) | async-done | bytes 16416 | tf_op jit(solution)/shard_map/all_to_all | solution.py:595
  88.2 1.0 copy-done.3
  89.3 3.8 %shard_map.123 = (bf16[16,64,128]{2,1,0:T(8,128)(2,1)S(1)}, bf16[32,128,128]{2,1,0:T(8,128)(2,1)}) custom-call(f32[16,64,128]{2,1,0:T(8,128)S(1)} %copy-done.3, f32[32,128]{1,0:T(8,128)S(1)} %get-tuple-element.40.code_ref, f32[32,1,128]{2,1,0:T(1,128)S(1)} %all-to-all-done.2.norm_ref, bf16[16,128,512]{2,1,0:T(8,128)(2,1)S(1)} %copy-done.1, ...), custom_call_target="tpu_custom_call" | custom-call | tf_op jit(solution)/shard_map/pallas_call | solution.py:554
  93.8 2.9 %all-to-all-start.3 = ((bf16[32,128,128]{2,1,0:T(8,128)(2,1)}), bf16[32,128,128]{2,1,0:T(8,128)(2,1)S(1)}, u32[]{:S(2)}, u32[]{:S(2)}) async-start(bf16[32,128,128]{2,1,0:T(8,128)(2,1)} %get-tuple-element.48), calls=%async_computation.3 | async-start | bytes 2097152 | tf_op jit(solution)/shard_map/all_to_all | solution.py:595
  96.7 1.8 %collective-permute-start.7 = (bf16[136,512]{1,0:T(8,128)(2,1)S(1)}, bf16[136,512]{1,0:T(8,128)(2,1)S(1)}, u32[]{:S(2)}, u32[]{:S(2)}) collective-permute-start(bf16[136,512]{1,0:T(8,128)(2,1)S(1)} %copy-done.12), channel_id=1, source_target_pairs={{0,2},{1,3},{2,4},{3,5},{4,6},{5,7},{6,0},{7,1},{8,10},{9,11},{10,... | collective-permute-start | bytes 417800 | tf_op jit(solution)/shard_map/ppermute | solution.py:661
  98.6 2.4 %collective-permute-start.6 = (bf16[136,512]{1,0:T(8,128)(2,1)S(1)}, bf16[136,512]{1,0:T(8,128)(2,1)S(1)}, u32[]{:S(2)}, u32[]{:S(2)}) collective-permute-start(bf16[136,512]{1,0:T(8,128)(2,1)S(1)} %copy-done.12), channel_id=1, source_target_pairs={{0,4},{1,5},{2,6},{3,7},{4,0},{5,1},{6,2},{7,3},{8,12},{9,13},{10,... | collective-permute-start | bytes 417800 | tf_op jit(solution)/shard_map/ppermute | solution.py:661
  101.0 1.4 collective-permute-start.5
  102.4 19.4 %collective-permute-done.7 = bf16[136,512]{1,0:T(8,128)(2,1)S(1)} collective-permute-done((bf16[136,512]{1,0:T(8,128)(2,1)S(1)}, bf16[136,512]{1,0:T(8,128)(2,1)S(1)}, u32[]{:S(2)}, u32[]{:S(2)}) %collective-permute-start.7) | collective-permute-done | bytes 139296 | tf_op jit(solution)/shard_map/ppermute | solution.py:661
  121.8 10.6 %collective-permute-done.6 = bf16[136,512]{1,0:T(8,128)(2,1)S(1)} collective-permute-done((bf16[136,512]{1,0:T(8,128)(2,1)S(1)}, bf16[136,512]{1,0:T(8,128)(2,1)S(1)}, u32[]{:S(2)}, u32[]{:S(2)}) %collective-permute-start.6) | collective-permute-done | bytes 139296 | tf_op jit(solution)/shard_map/ppermute | solution.py:661
  132.5 1.5 collective-permute-start.8
  134.1 4.6 %shard_map.125.part_ref = f32[256,512]{1,0:T(8,128)} custom-call(s32[1]{0:T(128)} %bitcast.1.where_ref, bf16[4,136,512]{2,1,0:T(8,128)(2,1)} %copy-done.10, bf16[512,512]{1,0:T(8,128)(2,1)} %constant_dynamic-update-slice_fusion.near_ref, bf16[512,512]{1,0:T(8,128)(2,1)} %collective-permute-done.2.y_ref, bf16[512,512]{1,0:T(8,128)(2,1)} %collective-permute-done.3.core_ref, ...), custom_call_target="tpu_custom_call" | custom-call | tf_op jit(solution)/shard_map/pallas_call | solution.py:554
  138.7 7.4 %collective-permute-done.8.blocks_ref = bf16[4,136,512]{2,1,0:T(8,128)(2,1)S(1)} collective-permute-done((bf16[4,136,512]{2,1,0:T(8,128)(2,1)S(1)}, bf16[4,136,512]{2,1,0:T(8,128)(2,1)S(1)}, u32[]{:S(2)}, u32[]{:S(2)}) %collective-permute-start.8) | collective-permute-done | bytes 557088 | tf_op jit(solution)/shard_map/ppermute | solution.py:702
  146.9 5.1 %shard_map.126 = (f32[128,512]{1,0:T(8,128)}, f32[128,512]{1,0:T(8,128)}) custom-call(s32[1]{0:T(128)} %bitcast.1.where_ref, s32[1]{0:T(128)} %bitcast.me_ref, bf16[4,136,512]{2,1,0:T(8,128)(2,1)} %copy-done.11, bf16[512,512]{1,0:T(8,128)(2,1)} %constant_dynamic-update-slice_fusion.near_ref, bf16[512,512]{1,0:T(8,128)(2,1)} %collective-permute-done.2.y_ref, ...), custom_call_target="tpu_custom_call" | custom-call | tf_op jit(solution)/shard_map/pallas_call | solution.py:554
  152.0 1.7 %collective-permute-done.9 = f32[128,512]{1,0:T(8,128)S(1)} collective-permute-done((f32[128,512]{1,0:T(8,128)}, f32[128,512]{1,0:T(8,128)S(1)}, u32[]{:S(2)}, u32[]{:S(2)}) %collective-permute-start.9) | collective-permute-done | bytes 262176 | tf_op jit(solution)/shard_map/ppermute | solution.py:726
  153.7 1.0 add.15
  154.7 1.6 collective-permute-start.10
  156.3 5.9 %shard_map.127 = (f32[16,128,512]{2,1,0:T(8,128)}, f32[16,512]{1,0:T(8,128)}) custom-call(bf16[16,64,128]{2,1,0:T(8,128)(2,1)} %copy-done.5, f32[32,1,128]{2,1,0:T(1,128)} %copy-done.7, bf16[32,136,128]{2,1,0:T(8,128)(2,1)} %copy-done), custom_call_target="tpu_custom_call" | custom-call | tf_op jit(solution)/shard_map/pallas_call | solution.py:554
  163.3 1.5 collective-permute-done.11
  165.7 1.4 shard_map.124
  (41 shorter events, 5.8 us)
Async XLA Ops:
  0.6 52.8 %copy-start.1 = (bf16[16,128,512]{2,1,0:T(8,128)(2,1)S(1)}, bf16[16,128,512]{2,1,0:T(8,128)(2,1)}, u32[]{:S(2)}) copy-start(bf16[16,128,512]{2,1,0:T(8,128)(2,1)} %leaf_ref.1) | copy-start | bytes 6291460
  0.6 52.8 %copy-start.8 = (bf16[16,512]{1,0:T(8,128)(2,1)S(1)}, bf16[16,512]{1,0:T(8,128)(2,1)}, u32[]{:S(2)}) copy-start(bf16[16,512]{1,0:T(8,128)(2,1)} %mid_ref.3) | copy-start | bytes 49156
  3.9 49.5 %all-to-all-start = ((bf16[32,136,128]{2,1,0:T(8,128)(2,1)}), bf16[32,136,128]{2,1,0:T(8,128)(2,1)S(1)}, u32[]{:S(2)}, u32[]{:S(2)}) async-start(bf16[32,136,128]{2,1,0:T(8,128)(2,1)} %get-tuple-element.38), calls=%async_computation | async-start | bytes 2228224 | tf_op jit(solution)/shard_map/all_to_all | solution.py:595
  11.2 65.6 %copy-start.6 = (f32[128,128]{1,0:T(8,128)S(1)}, f32[128,128]{1,0:T(8,128)}, u32[]{:S(2)}) copy-start(f32[128,128]{1,0:T(8,128)} %get-tuple-element.37.info_ref) | copy-start | bytes 196612
  11.2 28.2 %collective-permute-start = (bf16[256,512]{1,0:T(8,128)(2,1)}, bf16[256,512]{1,0:T(8,128)(2,1)S(1)}, u32[]{:S(2)}, u32[]{:S(2)}) collective-permute-start(bf16[256,512]{1,0:T(8,128)(2,1)} %weight_ref.5), channel_id=1, source_target_pairs={{0,2},{1,3},{2,4},{3,5},{4,6},{5,7},{6,0},{7,1},{8,12},{9,13},{10,... | collective-permute-start | bytes 786440 | tf_op jit(solution)/shard_map/ppermute | solution.py:637
  39.4 7.1 %collective-permute-start.1 = (bf16[256,512]{1,0:T(8,128)(2,1)S(1)}, bf16[256,512]{1,0:T(8,128)(2,1)S(1)}, u32[]{:S(2)}, u32[]{:S(2)}) collective-permute-start(bf16[256,512]{1,0:T(8,128)(2,1)S(1)} %collective-permute-done), channel_id=1, source_target_pairs={{0,1},{1,0},{2,3},{3,2},{4,5},{5,4},{6,7},{7,6},{8,9},{9,8},{10,11... | collective-permute-start | bytes 786440 | tf_op jit(solution)/shard_map/ppermute | solution.py:656
  47.3 10.0 %collective-permute-start.2 = (bf16[512,512]{1,0:T(8,128)(2,1)}, bf16[512,512]{1,0:T(8,128)(2,1)}, u32[]{:S(2)}, u32[]{:S(2)}) collective-permute-start(bf16[512,512]{1,0:T(8,128)(2,1)} %constant_dynamic-update-slice_fusion.near_ref), channel_id=1, source_target_pairs={{0,16},{8,24},{16,0},{24,8},{1,17},{9,25},{17,1},{25,9},{2,18},{10... | collective-permute-start | bytes 1572872 | tf_op jit(solution)/shard_map/ppermute | solution.py:658
  47.3 33.9 %collective-permute-start.3 = (bf16[512,512]{1,0:T(8,128)(2,1)}, bf16[512,512]{1,0:T(8,128)(2,1)}, u32[]{:S(2)}, u32[]{:S(2)}) collective-permute-start(bf16[512,512]{1,0:T(8,128)(2,1)} %constant_dynamic-update-slice_fusion.near_ref), channel_id=1, source_target_pairs={{0,8},{8,0},{16,24},{24,16},{1,9},{9,1},{17,25},{25,17},{2,10},{10... | collective-permute-start | bytes 1572872 | tf_op jit(solution)/shard_map/ppermute | solution.py:659
  53.4 31.9 %copy-start = (bf16[32,136,128]{2,1,0:T(8,128)(2,1)}, bf16[32,136,128]{2,1,0:T(8,128)(2,1)S(1)}, u32[]{:S(2)}) copy-start(bf16[32,136,128]{2,1,0:T(8,128)(2,1)S(1)} %all-to-all-done.got_ref) | copy-start | bytes 3342340
  56.5 0.8 copy-start.2
  57.3 23.8 %collective-permute-start.4 = (bf16[512,512]{1,0:T(8,128)(2,1)}, bf16[512,512]{1,0:T(8,128)(2,1)}, u32[]{:S(2)}, u32[]{:S(2)}) collective-permute-start(bf16[512,512]{1,0:T(8,128)(2,1)} %collective-permute-done.2.y_ref), channel_id=1, source_target_pairs={{0,8},{8,0},{16,24},{24,16},{1,9},{9,1},{17,25},{25,17},{2,10},{10... | collective-permute-start | bytes 1572872 | tf_op jit(solution)/shard_map/ppermute | solution.py:682
  78.6 9.6 %all-to-all-start.2 = ((f32[32,1,128]{2,1,0:T(1,128)}), f32[32,1,128]{2,1,0:T(1,128)S(1)}, u32[]{:S(2)}, u32[]{:S(2)}) async-start(f32[32,1,128]{2,1,0:T(1,128)} %get-tuple-element.42), calls=%async_computation.2 | async-start | bytes 32768 | tf_op jit(solution)/shard_map/all_to_all | solution.py:595
  88.2 5.6 %copy-start.7 = (f32[32,1,128]{2,1,0:T(1,128)}, f32[32,1,128]{2,1,0:T(1,128)S(1)}, u32[]{:S(2)}) copy-start(f32[32,1,128]{2,1,0:T(1,128)S(1)} %all-to-all-done.2.norm_ref) | copy-start | bytes 49156
  88.2 1.0 copy-start.3
  89.3 7.5 %copy-start.12 = (bf16[136,512]{1,0:T(8,128)(2,1)S(1)}, bf16[136,512]{1,0:T(8,128)(2,1)}, u32[]{:S(2)}) copy-start(bf16[136,512]{1,0:T(8,128)(2,1)} %get-tuple-element.53.own_ref) | copy-start | bytes 417796
  93.1 0.7 copy-start.5
  93.8 71.9 %all-to-all-start.3 = ((bf16[32,128,128]{2,1,0:T(8,128)(2,1)}), bf16[32,128,128]{2,1,0:T(8,128)(2,1)S(1)}, u32[]{:S(2)}, u32[]{:S(2)}) async-start(bf16[32,128,128]{2,1,0:T(8,128)(2,1)} %get-tuple-element.48), calls=%async_computation.3 | async-start | bytes 2097152 | tf_op jit(solution)/shard_map/all_to_all | solution.py:595
  96.7 25.1 %collective-permute-start.7 = (bf16[136,512]{1,0:T(8,128)(2,1)S(1)}, bf16[136,512]{1,0:T(8,128)(2,1)S(1)}, u32[]{:S(2)}, u32[]{:S(2)}) collective-permute-start(bf16[136,512]{1,0:T(8,128)(2,1)S(1)} %copy-done.12), channel_id=1, source_target_pairs={{0,2},{1,3},{2,4},{3,5},{4,6},{5,7},{6,0},{7,1},{8,10},{9,11},{10,... | collective-permute-start | bytes 417800 | tf_op jit(solution)/shard_map/ppermute | solution.py:661
  98.6 33.9 %collective-permute-start.6 = (bf16[136,512]{1,0:T(8,128)(2,1)S(1)}, bf16[136,512]{1,0:T(8,128)(2,1)S(1)}, u32[]{:S(2)}, u32[]{:S(2)}) collective-permute-start(bf16[136,512]{1,0:T(8,128)(2,1)S(1)} %copy-done.12), channel_id=1, source_target_pairs={{0,4},{1,5},{2,6},{3,7},{4,0},{5,1},{6,2},{7,3},{8,12},{9,13},{10,... | collective-permute-start | bytes 417800 | tf_op jit(solution)/shard_map/ppermute | solution.py:661
  101.0 31.5 %collective-permute-start.5 = (bf16[136,512]{1,0:T(8,128)(2,1)S(1)}, bf16[136,512]{1,0:T(8,128)(2,1)S(1)}, u32[]{:S(2)}, u32[]{:S(2)}) collective-permute-start(bf16[136,512]{1,0:T(8,128)(2,1)S(1)} %copy-done.12), channel_id=1, source_target_pairs={{0,6},{1,7},{2,0},{3,1},{4,2},{5,3},{6,4},{7,5},{8,14},{9,15},{10,... | collective-permute-start | bytes 417800 | tf_op jit(solution)/shard_map/ppermute | solution.py:661
  132.5 1.5 copy-start.10
  132.5 13.6 %collective-permute-start.8 = (bf16[4,136,512]{2,1,0:T(8,128)(2,1)S(1)}, bf16[4,136,512]{2,1,0:T(8,128)(2,1)S(1)}, u32[]{:S(2)}, u32[]{:S(2)}) collective-permute-start(bf16[4,136,512]{2,1,0:T(8,128)(2,1)S(1)} %pad_maximum_fusion.blocks_ref), channel_id=1, source_target_pairs={{0,1},{1,0},{2,3},{3,2},{4,5},{5,4},{6,7},{7,6},{8,9},{9,8},{10,11... | collective-permute-start | bytes 1671176 | tf_op jit(solution)/shard_map/ppermute | solution.py:702
  146.1 0.8 copy-start.11
  152.0 1.7 %collective-permute-start.9 = (f32[128,512]{1,0:T(8,128)}, f32[128,512]{1,0:T(8,128)S(1)}, u32[]{:S(2)}, u32[]{:S(2)}) collective-permute-start(f32[128,512]{1,0:T(8,128)} %get-tuple-element.60), channel_id=1, source_target_pairs={{0,8},{8,0},{16,24},{24,16},{1,9},{9,1},{17,25},{25,17},{2,10},{10... | collective-permute-start | bytes 786440 | tf_op jit(solution)/shard_map/ppermute | solution.py:726
  154.7 8.4 %collective-permute-start.10 = (f32[128,512]{1,0:T(8,128)S(1)}, f32[128,512]{1,0:T(8,128)S(1)}, u32[]{:S(2)}, u32[]{:S(2)}) collective-permute-start(f32[128,512]{1,0:T(8,128)S(1)} %add.15), channel_id=1, source_target_pairs={{0,16},{8,24},{16,0},{24,8},{1,17},{9,25},{17,1},{25,9},{2,18},{10... | collective-permute-start | bytes 786440 | tf_op jit(solution)/shard_map/ppermute | solution.py:727
  156.3 9.4 %copy-start.4 = (f32[128,512]{1,0:T(8,128)S(1)}, f32[128,512]{1,0:T(8,128)}, u32[]{:S(2)}) copy-start(f32[128,512]{1,0:T(8,128)} %get-tuple-element.49.top_ref) | copy-start | bytes 786436
  156.3 9.4 %copy-start.9 = (f32[8,128]{1,0:T(8,128)S(1)}, f32[8,128]{1,0:T(8,128)}, u32[]{:S(2)}) copy-start(f32[8,128]{1,0:T(8,128)} %get-tuple-element.50.top_loss_ref) | copy-start | bytes 12292
  163.2 1.6 collective-permute-start.11

commit v5 on v4

--- a/solution.py
+++ b/solution.py
@@ -369,10 +369,21 @@
     loss_ref[...] = losses.T[:SUB, :]
 
 
-def backward_kernel(
-    score_ref, code_ref, norm_ref, leaf_ref, mid_ref, delta_ref, pay_ref, wide_ref
-):
-    held, pairs, labels = score_ref.shape
+def slot_column(array, base, k, held):
+    return jnp.concatenate(
+        [array[:, base + r * held + k : base + r * held + k + 1] for r in range(CAPB)], axis=0
+    )
+
+
+def leaf_delta(scores, codes, norms, k, held):
+    code = slot_column(codes, 0, k, held)
+    onehot = jnp.where(code - 2.0 == iota_f(scores.shape, 1), 1.0, 0.0)
+    chance = jnp.exp(scores - slot_column(norms, 0, k, held))
+    return jnp.where(code > 0.5, chance - onehot, 0.0).astype(BF)
+
+
+def backward_kernel(score_ref, code_ref, norm_ref, leaf_ref, mid_ref, pay_ref, wide_ref):
+    held, pairs, _ = score_ref.shape
     devs = pairs // CAPB
     width = leaf_ref.shape[2]
     chunks = width // LANES
@@ -380,20 +391,9 @@
     body = chunks * slots
     norms = norm_ref[...].reshape(devs, LANES)
     codes = code_ref[...]
-    label_f = iota_f((pairs, labels), 1)
-
-    def column(array, base, k):
-        return jnp.concatenate(
-            [array[:, base + r * held + k : base + r * held + k + 1] for r in range(CAPB)], axis=0
-        )
-
     for k in range(held):
-        code = column(codes, 0, k)
-        lse = column(norms, 0, k)
-        mid_delta = column(norms, slots, k)
-        onehot = jnp.where(code - 2.0 == label_f, 1.0, 0.0)
-        delta = jnp.where(code > 0.5, jnp.exp(score_ref[k] - lse) - onehot, 0.0).astype(BF)
-        delta_ref[k] = delta
+        delta = leaf_delta(score_ref[k], codes, norms, k, held)
+        mid_delta = slot_column(norms, slots, k, held)
         back = dot_nn(delta, leaf_ref[k]) + mid_delta * mid_ref[k : k + 1, :].astype(F32)
         for r in range(CAPB):
             for c in range(chunks):
@@ -403,20 +403,22 @@
     pay_ref[...] = wide_ref[...].astype(BF).reshape(devs, body, LANES)
 
 
-def grads_kernel(delta_ref, norm_ref, got_ref, leaf_grad_ref, mid_grad_ref, wide_ref):
-    held, pairs, _ = delta_ref.shape
+def grads_kernel(
+    score_ref, code_ref, norm_ref, got_ref, leaf_grad_ref, mid_grad_ref, wide_ref
+):
+    held, pairs, _ = score_ref.shape
     devs = pairs // CAPB
     slots = CAPB * held
     chunks = leaf_grad_ref.shape[2] // LANES
     body = chunks * slots
     wide_ref[...] = got_ref[:, :body, :].reshape(devs * body, LANES).astype(F32)
     norms = norm_ref[...].reshape(devs, LANES)
+    codes = code_ref[...]
     for k in range(held):
         full = cluster_rows(wide_ref, k, devs, held, chunks)
-        leaf_grad_ref[k] = dot_tn(delta_ref[k], full.astype(BF))
-        mid_delta = jnp.concatenate(
-            [norms[:, slots + r * held + k : slots + r * held + k + 1] for r in range(CAPB)], axis=0
-        )
+        delta = leaf_delta(score_ref[k], codes, norms, k, held)
+        leaf_grad_ref[k] = dot_tn(delta, full.astype(BF))
+        mid_delta = slot_column(norms, slots, k, held)
         mid_grad_ref[k : k + 1, :] = jnp.sum(mid_delta * full, axis=0, keepdims=True)
 
 
@@ -466,6 +468,12 @@
     return jnp.broadcast_to(target, (LANES, LANES)).T[:, 0:1]
 
 
+def top_rows(blocks):
+    rows = blocks[0].shape[0] - SUB
+    block = jnp.concatenate([ref[:rows, :] for ref in blocks], axis=0)
+    return block, jnp.concatenate([top_column(ref[rows:, :]) for ref in blocks], axis=0)
+
+
 def own_columns(me, dims, label_size, held_top):
     steps = label_size // 2
 
@@ -489,17 +497,18 @@
 
 
 def top_own_kernel(
-    where_ref, me_ref, own_ref, near_ref, y_ref, core_ref, far_ref, weight_ref,
+    where_ref, me_ref, own_ref, blocks_ref, near_ref, y_ref, core_ref, far_ref, weight_ref,
     back_ref, part_ref, loss_ref, *, label_size,
 ):
     rows = own_ref.shape[0] - SUB
     piece = near_ref.shape[0]
     pieces = (near_ref, y_ref, core_ref, far_ref)
-    block = own_ref[:rows, :]
-    target = top_column(own_ref[rows:, :])
+    blocks = [own_ref] + [blocks_ref.at[n] for n in range(blocks_ref.shape[0])]
+    block, target = top_rows(blocks)
     scores, total, part = top_step(
         block, target, pieces, weight_ref[...], where_ref[0].astype(F32)
     )
+    scores, total, target = scores[:rows], total[:rows], target[:rows]
     part_ref[...] = part
     column = own_columns(me_ref[0], (SUB, scores.shape[1]), label_size, weight_ref.shape[0])
     hit = jnp.broadcast_to(column[0:1, :], scores.shape) == target
@@ -512,28 +521,15 @@
     loss_ref[...] = jnp.broadcast_to(loss, (rows, LANES)).T[:SUB, :]
 
 
-def top_blocks(where_ref, blocks_ref, pieces, weight_ref, first):
-    count, depth, _ = blocks_ref.shape
-    rows = depth - SUB
-    numbers = range(first, count)
-    block = jnp.concatenate([blocks_ref[n, :rows, :] for n in numbers], axis=0)
-    target = jnp.concatenate([top_column(blocks_ref[n, rows:, :]) for n in numbers], axis=0)
-    return top_step(block, target, pieces, weight_ref[...], where_ref[0].astype(F32))[2]
-
-
-def top_near_kernel(
-    where_ref, blocks_ref, near_ref, y_ref, core_ref, far_ref, weight_ref, part_ref, out_ref
-):
-    pieces = (near_ref, y_ref, core_ref, far_ref)
-    out_ref[...] = part_ref[...] + top_blocks(where_ref, blocks_ref, pieces, weight_ref, 1)
-
-
 def top_far_kernel(
-    where_ref, me_ref, blocks_ref, near_ref, y_ref, core_ref, far_ref, weight_ref, part_ref,
+    where_ref, me_ref, first_ref, blocks_ref, near_ref, y_ref, core_ref, far_ref, weight_ref, part_ref,
     kept_ref, given_ref, sum_ref, *, label_size,
 ):
     pieces = (near_ref, y_ref, core_ref, far_ref)
-    sum_ref[...] = part_ref[...] + top_blocks(where_ref, blocks_ref, pieces, weight_ref, 0)
+    blocks = [first_ref] + [blocks_ref.at[n] for n in range(blocks_ref.shape[0])]
+    block, target = top_rows(blocks)
+    base = where_ref[0].astype(F32)
+    sum_ref[...] = part_ref[...] + top_step(block, target, pieces, weight_ref[...], base)[2]
     half = kept_ref.shape[0]
     core = lax.rem(lax.div(me_ref[0], label_size), 2)
     kept_ref[...] = sum_ref[pl.ds(pl.multiple_of(core * half, SUB), half), :]
@@ -658,6 +654,7 @@
     w_y = lax.ppermute(w_own, "dp", flip_y)
     w_core = lax.ppermute(w_own, "dp", flip_core)
     sent = after(own, w_near)
+    own_other = lax.ppermute(own, "label", flip_x)
     peers = [lax.ppermute(sent, "label", along(n)) for n in range(1, steps)]
     pairs = CAPB * devs
     scores, stats, codes = call(
@@ -688,6 +685,16 @@
         mib=16,
     )
     norms_held = exchange(norms)
+    mine = jnp.stack(after(peers, norms))
+    other = lax.ppermute(mine, "label", flip_x)
+    back = call(
+        backward_kernel,
+        shape((devs, body, LANES), BF),
+        (scores, codes, norms_held, leaf_weight, mid_weight),
+        scratch=(pltpu.VMEM((devs * body, LANES), F32),),
+        mib=24,
+    )
+    returned = exchange(back)
     top_back, top_part, top_loss = call(
         functools.partial(top_own_kernel, label_size=label_size),
         (
@@ -695,30 +702,13 @@
             shape((held_top, width), F32),
             shape((SUB, rows), F32),
         ),
-        (label_base, me, own, after(w_own, norms), w_y, w_core, w_far, top_weight),
+        (label_base, me, own, after(mine, back), w_own, w_y, w_core, w_far, top_weight),
         scalars=2,
-    )
-    mine = jnp.stack([sent] + after(peers, top_part))
-    other = lax.ppermute(mine, "label", flip_x)
-    norms_held = after(norms_held, top_part)
-    delta, back = call(
-        backward_kernel,
-        (shape((held, pairs, labels), BF), shape((devs, body, LANES), BF)),
-        (scores, codes, norms_held, leaf_weight, mid_weight),
-        scratch=(pltpu.VMEM((devs * body, LANES), F32),),
-        mib=24,
-    )
-    returned = exchange(back)
-    top_part = call(
-        top_near_kernel,
-        shape((held_top, width), F32),
-        (label_base, after(mine, back), w_own, w_y, w_core, w_far, top_weight, top_part),
-        scalars=1,
     )
     kept, given = call(
         functools.partial(top_far_kernel, label_size=label_size),
         (shape((held_top // 2, width), F32), shape((held_top // 2, width), F32)),
-        (label_base, me, after(other, back), w_own, w_y, w_core, w_far, top_weight, top_part),
+        (label_base, me, own_other, after(other, back), w_own, w_y, w_core, w_far, top_weight, top_part),
         scalars=2,
         scratch=(pltpu.VMEM((held_top, width), F32),),
     )
@@ -728,7 +718,7 @@
     leaf_grad, mid_grad = call(
         grads_kernel,
         (shape((held, labels, width), F32), shape((held, width), F32)),
-        (delta, norms_held, after(got, share)),
+        (scores, codes, norms_held, after(got, share)),
         scratch=(pltpu.VMEM((devs * body, LANES), F32),),
     )
     share = share + after(from_y, mid_grad)

time: 168 us -> 163 us (0.970)
  starting transfers between devices: 37.9 us -> 25.1 us
  blocking collectives: 14.6 us -> 27.2 us
  Pallas kernels: 33 us -> 28 us
    all_to_all x1 -> x2, blocking collectives: 14.6 us -> 27.2 us  [exchange(): lax.all_to_all(array, ('dp', 'label'), split_axis=0, concat_axis=0, tiled...]
    ppermute x1, starting transfers between devices: 6.15 us -> 0.01 us  [per_device(): w_core = lax.ppermute(w_own, 'dp', flip_core)]
    pallas_call x9 -> x8, Pallas kernels: 33 us -> 28 us  [call(): pl.pallas_call(kernel, out_shape=outs, in_specs=[small if n < scalars els...]
    ppermute x1, starting transfers between devices: 4.89 us -> 0.51 us  [per_device(): w_far = lax.ppermute(w_y, 'dp', flip_core)]
    all_to_all x3 -> x2, waiting for transfers between devices: 2.94 us -> 0.01 us  [exchange(): lax.all_to_all(array, ('dp', 'label'), split_axis=0, concat_axis=0, tiled...]
    all_to_all x3 -> x2, starting transfers between devices: 12.8 us -> 9.97 us  [exchange(): lax.all_to_all(array, ('dp', 'label'), split_axis=0, concat_axis=0, tiled...]
    ppermute x1, waiting for transfers between devices: 7.4 us -> 9.99 us  [per_device(): other = lax.ppermute(mine, 'label', flip_x)]
    unnamed x27 -> x33, local copies, waits for them, and re-layouts: 4.11 us -> 4.82 us
  transfers between devices with their start and end apart: 15 -> 15, of which waited for: 9 -> 8; matrix products, arithmetic and copies ran while one was open for 2% -> 2% of each run, Pallas kernels for 15% -> 14%
where the time goes in v5:
time: 163 us; the launch traced here: 162 us
  waiting for transfers between devices  73 us (45%)
  Pallas kernels  28 us (17%)
  blocking collectives  27.2 us (17%)
  starting transfers between devices  25.1 us (15%)
  local copies, waits for them, and re-layouts  5.54 us (3%)
  other arithmetic  1.94 us (1%)
    ppermute x3, waiting for transfers between devices, per_device(): peers = [lax.ppermute(sent, 'label', along(n)) for n in range(1, steps)]  29.6 us
    pallas_call x8, Pallas kernels, call(): pl.pallas_call(kernel, out_shape=outs, in_specs=[small if n < scalars els...  28 us
    all_to_all x2, blocking collectives, exchange(): lax.all_to_all(array, ('dp', 'label'), split_axis=0, concat_axis=0, tiled...  27.2 us
    ppermute x1, waiting for transfers between devices, per_device(): w_near = lax.ppermute(top_weight, ('dp', 'label'), shift_z)  24.4 us
    ppermute x1, waiting for transfers between devices, per_device(): other = lax.ppermute(mine, 'label', flip_x)  9.99 us
    all_to_all x2, starting transfers between devices, exchange(): lax.all_to_all(array, ('dp', 'label'), split_axis=0, concat_axis=0, tiled...  9.97 us
    ppermute x3, starting transfers between devices, per_device(): peers = [lax.ppermute(sent, 'label', along(n)) for n in range(1, steps)]  5.63 us
    ppermute x1, waiting for transfers between devices, per_device(): w_other = lax.ppermute(w_near, 'label', flip_x)  4.91 us
  transfers between devices with their start and end apart: 15, of which 8 were waited for; matrix products, arithmetic and copies ran while one was open for 2% of the time, Pallas kernels for 14%

profile of v5, /device:TPU:0, one launch (start us, length us, event | category | flops | bytes accessed | tf_op | source)
XLA Modules:
  0.0 161.6 jit_solution(12322294048447987492)
XLA Ops:
  0.7 3.2 %shard_map.119 = (bf16[32,136,128]{2,1,0:T(8,128)(2,1)}, f32[128,128]{1,0:T(8,128)}, bf16[136,512]{1,0:T(8,128)(2,1)}) custom-call(bf16[128,512]{1,0:T(8,128)(2,1)} %q_ref, s32[4,128]{1,0:T(4,128)} %bitcast.12, s32[1,512]{1,0:T(1,128)} %bitcast.13, s32[1,128]{1,0:T(1,128)} %bitcast.14, s32[1,128]{1,0:T(1,128)} %bitcast.15), custom_call_target="tpu_custom_call" | custom-call | tf_op jit(solution)/shard_map/pallas_call | solution.py:550
  3.9 7.3 %all-to-all-start = ((bf16[32,136,128]{2,1,0:T(8,128)(2,1)}), bf16[32,136,128]{2,1,0:T(8,128)(2,1)S(1)}, u32[]{:S(2)}, u32[]{:S(2)}) async-start(bf16[32,136,128]{2,1,0:T(8,128)(2,1)} %get-tuple-element.34), calls=%async_computation | async-start | bytes 2228224 | tf_op jit(solution)/shard_map/all_to_all | solution.py:591
  11.2 3.8 %collective-permute-start = (bf16[256,512]{1,0:T(8,128)(2,1)}, bf16[256,512]{1,0:T(8,128)(2,1)S(1)}, u32[]{:S(2)}, u32[]{:S(2)}) collective-permute-start(bf16[256,512]{1,0:T(8,128)(2,1)} %weight_ref.3), channel_id=1, source_target_pairs={{0,2},{1,3},{2,4},{3,5},{4,6},{5,7},{6,0},{7,1},{8,12},{9,13},{10,... | collective-permute-start | bytes 786440 | tf_op jit(solution)/shard_map/ppermute | solution.py:633
  15.0 24.4 %collective-permute-done = bf16[256,512]{1,0:T(8,128)(2,1)S(1)} collective-permute-done((bf16[256,512]{1,0:T(8,128)(2,1)}, bf16[256,512]{1,0:T(8,128)(2,1)S(1)}, u32[]{:S(2)}, u32[]{:S(2)}) %collective-permute-start) | collective-permute-done | bytes 262176 | tf_op jit(solution)/shard_map/ppermute | solution.py:633
  39.4 1.5 collective-permute-start.4
  41.6 4.9 %collective-permute-done.4 = bf16[256,512]{1,0:T(8,128)(2,1)S(1)} collective-permute-done((bf16[256,512]{1,0:T(8,128)(2,1)S(1)}, bf16[256,512]{1,0:T(8,128)(2,1)S(1)}, u32[]{:S(2)}, u32[]{:S(2)}) %collective-permute-start.4) | collective-permute-done | bytes 262176 | tf_op jit(solution)/shard_map/ppermute | solution.py:652
  47.3 3.1 %shard_map.120 = (f32[16,64,128]{2,1,0:T(8,128)S(1)}, f32[32,1,128]{2,1,0:T(1,128)S(1)}, f32[32,128]{1,0:T(8,128)S(1)}) custom-call(s32[1]{0:T(128)} %bitcast.me_ref, bf16[32,136,128]{2,1,0:T(8,128)(2,1)S(1)} %all-to-all-done.got_ref, bf16[16,128,512]{2,1,0:T(8,128)(2,1)S(1)} %copy-done.1, bf16[16,512]{1,0:T(8,128)(2,1)S(1)} %copy-done.7), custom_call_target="tpu_custom_call" | custom-call | tf_op jit(solution)/shard_map/pallas_call | solution.py:550
  50.4 18.4 %all_to_all.20.stat_ref = f32[32,1,128]{2,1,0:T(1,128)S(1)} all-to-all(f32[32,1,128]{2,1,0:T(1,128)S(1)} %get-tuple-element.37), channel_id=1, replica_groups=mesh['dp'=4,'label'=8] {'dp','label'}, dimensions={0} | all-to-all | bytes 32768 | tf_op jit(solution)/shard_map/all_to_all | solution.py:591
  68.7 1.2 shard_map.121
  69.9 8.8 %all_to_all.21.norm_ref = f32[32,1,128]{2,1,0:T(1,128)S(1)} all-to-all(f32[32,1,128]{2,1,0:T(1,128)S(1)} %get-tuple-element.38), channel_id=1, replica_groups=mesh['dp'=4,'label'=8] {'dp','label'}, dimensions={0} | all-to-all | bytes 32768 | tf_op jit(solution)/shard_map/all_to_all | solution.py:591
  78.8 2.8 %shard_map.122 = bf16[32,128,128]{2,1,0:T(8,128)(2,1)S(1)} custom-call(f32[16,64,128]{2,1,0:T(8,128)S(1)} %get-tuple-element.35.score_ref, f32[32,128]{1,0:T(8,128)S(1)} %get-tuple-element.36.code_ref, f32[32,1,128]{2,1,0:T(1,128)S(1)} %all_to_all.21.norm_ref, bf16[16,128,512]{2,1,0:T(8,128)(2,1)S(1)} %copy-done.1, bf16[16,512]{1,0:T(8,128)(2,1)S(1)} %copy-done.7), custom_call_target="tpu_custom_call" | custom-call | tf_op jit(solution)/shard_map/pallas_call | solution.py:550
  81.6 1.0 copy-done.2
  82.6 0.8 copy-done.3
  83.4 2.6 %all-to-all-start.3 = ((bf16[32,128,128]{2,1,0:T(8,128)(2,1)}), bf16[32,128,128]{2,1,0:T(8,128)(2,1)S(1)}, u32[]{:S(2)}, u32[]{:S(2)}) async-start(bf16[32,128,128]{2,1,0:T(8,128)(2,1)} %copy-done.2), calls=%async_computation.3 | async-start | bytes 2097152 | tf_op jit(solution)/shard_map/all_to_all | solution.py:591
  86.1 1.7 %collective-permute-start.3 = (bf16[136,512]{1,0:T(8,128)(2,1)S(1)}, bf16[136,512]{1,0:T(8,128)(2,1)S(1)}, u32[]{:S(2)}, u32[]{:S(2)}) collective-permute-start(bf16[136,512]{1,0:T(8,128)(2,1)S(1)} %copy-done.15), channel_id=1, source_target_pairs={{0,2},{1,3},{2,4},{3,5},{4,6},{5,7},{6,0},{7,1},{8,10},{9,11},{10,... | collective-permute-start | bytes 417800 | tf_op jit(solution)/shard_map/ppermute | solution.py:658
  87.8 2.5 %collective-permute-start.2 = (bf16[136,512]{1,0:T(8,128)(2,1)S(1)}, bf16[136,512]{1,0:T(8,128)(2,1)S(1)}, u32[]{:S(2)}, u32[]{:S(2)}) collective-permute-start(bf16[136,512]{1,0:T(8,128)(2,1)S(1)} %copy-done.15), channel_id=1, source_target_pairs={{0,4},{1,5},{2,6},{3,7},{4,0},{5,1},{6,2},{7,3},{8,12},{9,13},{10,... | collective-permute-start | bytes 417800 | tf_op jit(solution)/shard_map/ppermute | solution.py:658
  90.3 1.4 collective-permute-start.1
  92.2 18.9 %collective-permute-done.3 = bf16[136,512]{1,0:T(8,128)(2,1)S(1)} collective-permute-done((bf16[136,512]{1,0:T(8,128)(2,1)S(1)}, bf16[136,512]{1,0:T(8,128)(2,1)S(1)}, u32[]{:S(2)}, u32[]{:S(2)}) %collective-permute-start.3) | collective-permute-done | bytes 139296 | tf_op jit(solution)/shard_map/ppermute | solution.py:658
  111.2 10.6 %collective-permute-done.2 = bf16[136,512]{1,0:T(8,128)(2,1)S(1)} collective-permute-done((bf16[136,512]{1,0:T(8,128)(2,1)S(1)}, bf16[136,512]{1,0:T(8,128)(2,1)S(1)}, u32[]{:S(2)}, u32[]{:S(2)}) %collective-permute-start.2) | collective-permute-done | bytes 139296 | tf_op jit(solution)/shard_map/ppermute | solution.py:658
  121.8 1.5 collective-permute-start.9
  123.9 10.0 %collective-permute-done.9.blocks_ref = bf16[3,136,512]{2,1,0:T(8,128)(2,1)S(1)} collective-permute-done((bf16[3,136,512]{2,1,0:T(8,128)(2,1)S(1)}, bf16[3,136,512]{2,1,0:T(8,128)(2,1)S(1)}, u32[]{:S(2)}, u32[]{:S(2)}) %collective-permute-start.9) | collective-permute-done | bytes 417824 | tf_op jit(solution)/shard_map/ppermute | solution.py:689
  133.9 0.8 copy-done.10
  135.6 5.2 %shard_map.123 = (f32[128,512]{1,0:T(8,128)}, f32[256,512]{1,0:T(8,128)}, f32[8,128]{1,0:T(8,128)}) custom-call(s32[1]{0:T(128)} %bitcast.1.where_ref, s32[1]{0:T(128)} %bitcast.me_ref, bf16[136,512]{1,0:T(8,128)(2,1)} %get-tuple-element.40.own_ref, bf16[3,136,512]{2,1,0:T(8,128)(2,1)} %copy-done.12, ...), custom_call_target="tpu_custom_call" | custom-call | tf_op jit(solution)/shard_map/pallas_call | solution.py:550
  141.5 5.1 %shard_map.125 = (f32[128,512]{1,0:T(8,128)}, f32[128,512]{1,0:T(8,128)}) custom-call(s32[1]{0:T(128)} %bitcast.1.where_ref, s32[1]{0:T(128)} %bitcast.me_ref, bf16[136,512]{1,0:T(8,128)(2,1)} %copy-done.14, bf16[3,136,512]{2,1,0:T(8,128)(2,1)} %copy-done.13, bf16[512,512]{1,0:T(8,128)(2,1)} %constant_dynamic-update-slice_fusion.near_ref, ...), custom_call_target="tpu_custom_call" | custom-call | tf_op jit(solution)/shard_map/pallas_call | solution.py:550
  146.5 1.7 %collective-permute-done.10 = f32[128,512]{1,0:T(8,128)S(1)} collective-permute-done((f32[128,512]{1,0:T(8,128)}, f32[128,512]{1,0:T(8,128)S(1)}, u32[]{:S(2)}, u32[]{:S(2)}) %collective-permute-start.10) | collective-permute-done | bytes 262176 | tf_op jit(solution)/shard_map/ppermute | solution.py:716
  148.3 1.0 add.15
  149.3 1.6 collective-permute-start.11
  150.9 6.0 %shard_map.126 = (f32[16,128,512]{2,1,0:T(8,128)}, f32[16,512]{1,0:T(8,128)}) custom-call(f32[16,64,128]{2,1,0:T(8,128)} %copy-done.3, f32[32,128]{1,0:T(8,128)} %copy-done.8, f32[32,1,128]{2,1,0:T(1,128)} %copy-done.6, bf16[32,136,128]{2,1,0:T(8,128)(2,1)} %copy-done), custom_call_target="tpu_custom_call" | custom-call | tf_op jit(solution)/shard_map/pallas_call | solution.py:550
  156.8 0.9 collective-permute-done.11
  157.8 1.5 collective-permute-done.12
  159.4 0.8 pad_maximum_fusion
  160.2 1.4 shard_map.124
  (47 shorter events, 4.2 us)
Async XLA Ops:
  0.6 46.6 %copy-start.1 = (bf16[16,128,512]{2,1,0:T(8,128)(2,1)S(1)}, bf16[16,128,512]{2,1,0:T(8,128)(2,1)}, u32[]{:S(2)}) copy-start(bf16[16,128,512]{2,1,0:T(8,128)(2,1)} %leaf_ref.1) | copy-start | bytes 6291460
  0.6 46.6 %copy-start.7 = (bf16[16,512]{1,0:T(8,128)(2,1)S(1)}, bf16[16,512]{1,0:T(8,128)(2,1)}, u32[]{:S(2)}) copy-start(bf16[16,512]{1,0:T(8,128)(2,1)} %mid_ref.3) | copy-start | bytes 49156
  3.9 43.4 %all-to-all-start = ((bf16[32,136,128]{2,1,0:T(8,128)(2,1)}), bf16[32,136,128]{2,1,0:T(8,128)(2,1)S(1)}, u32[]{:S(2)}, u32[]{:S(2)}) async-start(bf16[32,136,128]{2,1,0:T(8,128)(2,1)} %get-tuple-element.34), calls=%async_computation | async-start | bytes 2228224 | tf_op jit(solution)/shard_map/all_to_all | solution.py:591
  11.2 57.5 %copy-start.5 = (f32[128,128]{1,0:T(8,128)S(1)}, f32[128,128]{1,0:T(8,128)}, u32[]{:S(2)}) copy-start(f32[128,128]{1,0:T(8,128)} %get-tuple-element.33.info_ref) | copy-start | bytes 196612
  11.2 28.2 %collective-permute-start = (bf16[256,512]{1,0:T(8,128)(2,1)}, bf16[256,512]{1,0:T(8,128)(2,1)S(1)}, u32[]{:S(2)}, u32[]{:S(2)}) collective-permute-start(bf16[256,512]{1,0:T(8,128)(2,1)} %weight_ref.3), channel_id=1, source_target_pairs={{0,2},{1,3},{2,4},{3,5},{4,6},{5,7},{6,0},{7,1},{8,12},{9,13},{10,... | collective-permute-start | bytes 786440 | tf_op jit(solution)/shard_map/ppermute | solution.py:633
  39.4 7.1 %collective-permute-start.4 = (bf16[256,512]{1,0:T(8,128)(2,1)S(1)}, bf16[256,512]{1,0:T(8,128)(2,1)S(1)}, u32[]{:S(2)}, u32[]{:S(2)}) collective-permute-start(bf16[256,512]{1,0:T(8,128)(2,1)S(1)} %collective-permute-done), channel_id=1, source_target_pairs={{0,1},{1,0},{2,3},{3,2},{4,5},{5,4},{6,7},{7,6},{8,9},{9,8},{10,11... | collective-permute-start | bytes 786440 | tf_op jit(solution)/shard_map/ppermute | solution.py:652
  47.3 44.5 %collective-permute-start.5 = (bf16[512,512]{1,0:T(8,128)(2,1)}, bf16[512,512]{1,0:T(8,128)(2,1)}, u32[]{:S(2)}, u32[]{:S(2)}) collective-permute-start(bf16[512,512]{1,0:T(8,128)(2,1)} %constant_dynamic-update-slice_fusion.near_ref), channel_id=1, source_target_pairs={{0,16},{8,24},{16,0},{24,8},{1,17},{9,25},{17,1},{25,9},{2,18},{10... | collective-permute-start | bytes 1572872 | tf_op jit(solution)/shard_map/ppermute | solution.py:654
  47.3 34.3 %copy-start = (bf16[32,136,128]{2,1,0:T(8,128)(2,1)}, bf16[32,136,128]{2,1,0:T(8,128)(2,1)S(1)}, u32[]{:S(2)}) copy-start(bf16[32,136,128]{2,1,0:T(8,128)(2,1)S(1)} %all-to-all-done.got_ref) | copy-start | bytes 3342340
  50.4 33.0 %copy-start.8 = (f32[32,128]{1,0:T(8,128)}, f32[32,128]{1,0:T(8,128)S(1)}, u32[]{:S(2)}) copy-start(f32[32,128]{1,0:T(8,128)S(1)} %get-tuple-element.36.code_ref) | copy-start | bytes 49156
  78.8 4.6 %copy-start.6 = (f32[32,1,128]{2,1,0:T(1,128)}, f32[32,1,128]{2,1,0:T(1,128)S(1)}, u32[]{:S(2)}) copy-start(f32[32,1,128]{2,1,0:T(1,128)S(1)} %all_to_all.21.norm_ref) | copy-start | bytes 49156
  78.8 7.3 %copy-start.15 = (bf16[136,512]{1,0:T(8,128)(2,1)S(1)}, bf16[136,512]{1,0:T(8,128)(2,1)}, u32[]{:S(2)}) copy-start(bf16[136,512]{1,0:T(8,128)(2,1)} %get-tuple-element.40.own_ref) | copy-start | bytes 417796
  81.6 1.0 copy-start.2
  82.6 0.8 copy-start.3
  83.4 76.8 %all-to-all-start.3 = ((bf16[32,128,128]{2,1,0:T(8,128)(2,1)}), bf16[32,128,128]{2,1,0:T(8,128)(2,1)S(1)}, u32[]{:S(2)}, u32[]{:S(2)}) async-start(bf16[32,128,128]{2,1,0:T(8,128)(2,1)} %copy-done.2), calls=%async_computation.3 | async-start | bytes 2097152 | tf_op jit(solution)/shard_map/all_to_all | solution.py:591
  86.1 25.1 %collective-permute-start.3 = (bf16[136,512]{1,0:T(8,128)(2,1)S(1)}, bf16[136,512]{1,0:T(8,128)(2,1)S(1)}, u32[]{:S(2)}, u32[]{:S(2)}) collective-permute-start(bf16[136,512]{1,0:T(8,128)(2,1)S(1)} %copy-done.15), channel_id=1, source_target_pairs={{0,2},{1,3},{2,4},{3,5},{4,6},{5,7},{6,0},{7,1},{8,10},{9,11},{10,... | collective-permute-start | bytes 417800 | tf_op jit(solution)/shard_map/ppermute | solution.py:658
  87.8 34.0 %collective-permute-start.2 = (bf16[136,512]{1,0:T(8,128)(2,1)S(1)}, bf16[136,512]{1,0:T(8,128)(2,1)S(1)}, u32[]{:S(2)}, u32[]{:S(2)}) collective-permute-start(bf16[136,512]{1,0:T(8,128)(2,1)S(1)} %copy-done.15), channel_id=1, source_target_pairs={{0,4},{1,5},{2,6},{3,7},{4,0},{5,1},{6,2},{7,3},{8,12},{9,13},{10,... | collective-permute-start | bytes 417800 | tf_op jit(solution)/shard_map/ppermute | solution.py:658
  90.3 31.5 %collective-permute-start.1 = (bf16[136,512]{1,0:T(8,128)(2,1)S(1)}, bf16[136,512]{1,0:T(8,128)(2,1)S(1)}, u32[]{:S(2)}, u32[]{:S(2)}) collective-permute-start(bf16[136,512]{1,0:T(8,128)(2,1)S(1)} %copy-done.15), channel_id=1, source_target_pairs={{0,6},{1,7},{2,0},{3,1},{4,2},{5,3},{6,4},{7,5},{8,14},{9,15},{10,... | collective-permute-start | bytes 417800 | tf_op jit(solution)/shard_map/ppermute | solution.py:658
  91.7 42.2 %collective-permute-start.6 = (bf16[512,512]{1,0:T(8,128)(2,1)}, bf16[512,512]{1,0:T(8,128)(2,1)S(1)}, u32[]{:S(2)}, u32[]{:S(2)}) collective-permute-start(bf16[512,512]{1,0:T(8,128)(2,1)} %constant_dynamic-update-slice_fusion.near_ref), channel_id=1, source_target_pairs={{0,8},{8,0},{16,24},{24,16},{1,9},{9,1},{17,25},{25,17},{2,10},{10... | collective-permute-start | bytes 1572872 | tf_op jit(solution)/shard_map/ppermute | solution.py:655
  91.7 42.2 %collective-permute-start.7 = (bf16[512,512]{1,0:T(8,128)(2,1)}, bf16[512,512]{1,0:T(8,128)(2,1)S(1)}, u32[]{:S(2)}, u32[]{:S(2)}) collective-permute-start(bf16[512,512]{1,0:T(8,128)(2,1)} %collective-permute-done.5.y_ref), channel_id=1, source_target_pairs={{0,8},{8,0},{16,24},{24,16},{1,9},{9,1},{17,25},{25,17},{2,10},{10... | collective-permute-start | bytes 1572872 | tf_op jit(solution)/shard_map/ppermute | solution.py:679
  121.8 12.1 %copy-start.12 = (bf16[3,136,512]{2,1,0:T(8,128)(2,1)}, bf16[3,136,512]{2,1,0:T(8,128)(2,1)S(1)}, u32[]{:S(2)}) copy-start(bf16[3,136,512]{2,1,0:T(8,128)(2,1)S(1)} %pad_maximum_fusion.1.blocks_ref) | copy-start | bytes 1253380
  121.8 12.1 %collective-permute-start.9 = (bf16[3,136,512]{2,1,0:T(8,128)(2,1)S(1)}, bf16[3,136,512]{2,1,0:T(8,128)(2,1)S(1)}, u32[]{:S(2)}, u32[]{:S(2)}) collective-permute-start(bf16[3,136,512]{2,1,0:T(8,128)(2,1)S(1)} %pad_maximum_fusion.1.blocks_ref), channel_id=1, source_target_pairs={{0,1},{1,0},{2,3},{3,2},{4,5},{5,4},{6,7},{7,6},{8,9},{9,8},{10,11... | collective-permute-start | bytes 1253384 | tf_op jit(solution)/shard_map/ppermute | solution.py:689
  123.4 17.4 %collective-permute-start.8 = (bf16[136,512]{1,0:T(8,128)(2,1)S(1)}, bf16[136,512]{1,0:T(8,128)(2,1)S(1)}, u32[]{:S(2)}, u32[]{:S(2)}) collective-permute-start(bf16[136,512]{1,0:T(8,128)(2,1)S(1)} %copy-done.15), channel_id=1, source_target_pairs={{0,1},{1,0},{2,3},{3,2},{4,5},{5,4},{6,7},{7,6},{8,9},{9,8},{10,11... | collective-permute-start | bytes 417800 | tf_op jit(solution)/shard_map/ppermute | solution.py:657
  133.9 6.9 %copy-start.13 = (bf16[3,136,512]{2,1,0:T(8,128)(2,1)}, bf16[3,136,512]{2,1,0:T(8,128)(2,1)S(1)}, u32[]{:S(2)}) copy-start(bf16[3,136,512]{2,1,0:T(8,128)(2,1)S(1)} %collective-permute-done.9.blocks_ref) | copy-start | bytes 1253380
  133.9 0.8 copy-start.10
  134.8 0.8 copy-start.11
  140.8 0.7 copy-start.14
  146.5 1.7 %collective-permute-start.10 = (f32[128,512]{1,0:T(8,128)}, f32[128,512]{1,0:T(8,128)S(1)}, u32[]{:S(2)}, u32[]{:S(2)}) collective-permute-start(f32[128,512]{1,0:T(8,128)} %get-tuple-element.53), channel_id=1, source_target_pairs={{0,8},{8,0},{16,24},{24,16},{1,9},{9,1},{17,25},{25,17},{2,10},{10... | collective-permute-start | bytes 786440 | tf_op jit(solution)/shard_map/ppermute | solution.py:716
  149.3 11.0 %copy-start.4 = (f32[128,512]{1,0:T(8,128)S(1)}, f32[128,512]{1,0:T(8,128)}, u32[]{:S(2)}) copy-start(f32[128,512]{1,0:T(8,128)} %get-tuple-element.46.top_ref) | copy-start | bytes 786436
  149.3 11.0 %copy-start.9 = (f32[8,128]{1,0:T(8,128)S(1)}, f32[8,128]{1,0:T(8,128)}, u32[]{:S(2)}) copy-start(f32[8,128]{1,0:T(8,128)} %get-tuple-element.47.top_loss_ref) | copy-start | bytes 12292
  149.3 8.4 %collective-permute-start.11 = (f32[128,512]{1,0:T(8,128)S(1)}, f32[128,512]{1,0:T(8,128)S(1)}, u32[]{:S(2)}, u32[]{:S(2)}) collective-permute-start(f32[128,512]{1,0:T(8,128)S(1)} %add.15), channel_id=1, source_target_pairs={{0,16},{8,24},{16,0},{24,8},{1,17},{9,25},{17,1},{25,9},{2,18},{10... | collective-permute-start | bytes 786440 | tf_op jit(solution)/shard_map/ppermute | solution.py:717
  157.7 1.6 collective-permute-start.12
